TPU v7x, 256 devices: a whole 4x4x8 slice. The times are simulated.
256 devices in a mesh: ka: 8 (over y_hi, x), ga: 32 (over y_lo, z, core).
Axes of the slice: x: 4, y: 4 (y_hi: 2, y_lo: 2; y = y_hi * 2 + y_lo), z: 8, core: 2. Of those that a mesh axis runs over, the one named last changes fastest.
Arguments:
- orbitals: bfloat16 [16, 8, 2, 32, 1024], P('ka', None, None, 'ga'), may hold values from -6 to 6
- band_counts: int32 [16], replicated, may hold values from 1 to 8, as said below
- pair_slot: int32 [16, 16], replicated, may hold values from 0 to 15
- kernel: float32 [16, 32, 1024], P(None, None, 'ga'), may hold values from 0.2 to 8
Outputs:
- exchange_vectors: float32 [16, 8, 2, 32, 1024], P('ka', None, None, 'ga')
- exchange_matrix: float32 [16, 2, 8, 8], P('ka')
- exchange_energy: float32 [], replicated
Inputs may be any that keep to these rules, and one draw needn't show every extreme that they name: The first band_counts[k] band slots of k-point k are the occupied ones; some k-point has all 8 slots occupied.
All inputs are finite; a program needn't handle non-finite values.
Results may differ from a plain program's by a relative error of at most 0.0003.
Values may be sent and summed in bfloat16 or wider, within the bound.
No kernel may reach another device: no remote copies, remote signals or barrier semaphores. Data moves between devices by JAX's collectives and lax.ppermute only.
A program may use at most 128 MiB of HBM per device.

v0:
```python
import jax
import jax.numpy as jnp
from jax import lax
from jax.sharding import PartitionSpec as P

STEPS = 2


group_width = 2
highest = lax.Precision.HIGHEST


def passed_along(value, axis, steps):
    count = lax.axis_size(axis)
    pairs = [(source, (source + steps) % count) for source in range(count)]
    return lax.ppermute(value, axis, pairs)


def copy_for_each(shard, axis):
    peers = lax.axis_size(axis)
    return lax.all_to_all(
        jnp.broadcast_to(shard[None], (peers, *shard.shape)), axis, 0, 0, tiled=True
    )


def over_copies(shard, axis):
    return copy_for_each(shard, axis).sum(axis=0)


def tables(points):
    positions = jnp.arange(points, dtype=jnp.int32)
    product = positions[:, None] * positions[None, :] % points
    angles = product.astype(jnp.float32) * (2.0 * jnp.pi / points)
    return (jnp.cos(angles), jnp.sin(angles))


def apply_table(table, values, dimension):
    rotated = jnp.tensordot(table, values, axes=([1], [dimension]), precision=highest)
    return jnp.moveaxis(rotated, 0, dimension)


def transform(real_part, imag_part, cosine_values, sine_values, dimension, forward):
    shifted = -sine_values if forward else sine_values
    first = apply_table(cosine_values, real_part + imag_part, dimension)
    second = apply_table(shifted - cosine_values, real_part, dimension)
    third = apply_table(cosine_values + shifted, imag_part, dimension)
    return (first - third, first + second)


def select_kernel(slot_ids, kernel_flat):
    slot_total = kernel_flat.shape[0]
    onehot = (slot_ids[:, None] == jnp.arange(slot_total, dtype=jnp.int32)[None, :]).astype(
        jnp.float32
    )
    return jnp.dot(onehot, kernel_flat, precision=highest, preferred_element_type=jnp.float32)


def contract(first_field, second_field):
    return jnp.einsum("kar,kbr->kab", first_field, second_field, precision=highest)


def on_device(orbitals, band_counts, pair_slot, kernel):
    local_kpoints = orbitals.shape[0]
    band_count = orbitals.shape[1]
    planes = orbitals.shape[3]
    columns = orbitals.shape[4]
    points = kernel.shape[1]
    groups = lax.axis_size("ka")
    kpoints = local_kpoints * groups
    own_group = lax.axis_index("ka")
    cosine_values, sine_values = tables(points)
    volume = float(points * points * points)
    weight = -1.0 / kpoints
    band_index = jnp.arange(band_count, dtype=jnp.int32)
    own_counts = lax.dynamic_slice_in_dim(band_counts, own_group * local_kpoints, local_kpoints)

    def masked(block_data, counts):
        keep = (band_index[None, :] < counts[:, None]).astype(orbitals.dtype)
        return block_data * keep[:, :, None, None, None]

    def slot_table(anchor):
        own_rows = lax.dynamic_slice_in_dim(pair_slot, own_group * local_kpoints, local_kpoints, 0)
        return lax.dynamic_slice_in_dim(own_rows, anchor * local_kpoints, local_kpoints, 1)

    pair_count = local_kpoints * band_count * local_kpoints * group_width
    kernel_share = kernel.shape[2]
    own_split = jnp.transpose(orbitals.astype(jnp.float32), (2, 3, 4, 0, 1)).reshape(
        2, planes, columns, local_kpoints * band_count
    )
    totals = (
        jnp.zeros((planes, columns, local_kpoints * band_count), jnp.float32),
        jnp.zeros((planes, columns, local_kpoints * band_count), jnp.float32),
    )

    def handle(current, anchor, totals):
        counts = lax.dynamic_slice_in_dim(band_counts, anchor * local_kpoints, local_kpoints)
        incoming = jnp.transpose(masked(current, counts).astype(jnp.float32), (2, 3, 4, 0, 1))
        chosen = select_kernel(slot_table(anchor).reshape(-1), kernel.reshape(kernel.shape[0], -1))
        chosen = jnp.transpose(
            chosen.reshape(local_kpoints, local_kpoints, points, kernel_share), (2, 3, 0, 1)
        )[:, :, :, None, :, None]
        trip_count = (jnp.max(counts) + group_width - 1) // group_width
        split_shape = (points, kernel_share, local_kpoints, band_count, local_kpoints, group_width)

        def one_group(group_turn, totals):
            picked = lax.dynamic_slice_in_dim(incoming, group_turn * group_width, group_width, 4)
            picked = picked.reshape(2, planes, columns, local_kpoints * group_width)
            real_part = (
                own_split[0][..., :, None] * picked[0][..., None, :]
                + own_split[1][..., :, None] * picked[1][..., None, :]
            )
            imag_part = (
                own_split[1][..., :, None] * picked[0][..., None, :]
                - own_split[0][..., :, None] * picked[1][..., None, :]
            )
            real_part = real_part.reshape(planes, points, points, pair_count)
            imag_part = imag_part.reshape(planes, points, points, pair_count)
            real_part, imag_part = transform(
                real_part, imag_part, cosine_values, sine_values, 2, True
            )
            real_part, imag_part = transform(
                real_part, imag_part, cosine_values, sine_values, 1, True
            )
            packed = jnp.stack((real_part, imag_part)).reshape(
                2, planes, points * points, pair_count
            )
            spectra = lax.all_to_all(packed, "ga", split_axis=2, concat_axis=1, tiled=True)
            real_part, imag_part = transform(
                spectra[0], spectra[1], cosine_values, sine_values, 0, True
            )
            real_part = (real_part.reshape(split_shape) * chosen).reshape(
                points, kernel_share, pair_count
            )
            imag_part = (imag_part.reshape(split_shape) * chosen).reshape(
                points, kernel_share, pair_count
            )
            real_part, imag_part = transform(
                real_part, imag_part, cosine_values, sine_values, 0, False
            )
            returned = lax.all_to_all(
                jnp.stack((real_part, imag_part)), "ga", split_axis=1, concat_axis=2, tiled=True
            )
            real_part = returned[0].reshape(planes, points, points, pair_count)
            imag_part = returned[1].reshape(planes, points, points, pair_count)
            real_part, imag_part = transform(
                real_part, imag_part, cosine_values, sine_values, 1, False
            )
            real_part, imag_part = transform(
                real_part, imag_part, cosine_values, sine_values, 2, False
            )
            real_part = (
                real_part.reshape(
                    planes, columns, local_kpoints * band_count, local_kpoints * group_width
                )
                / volume
            )
            imag_part = (
                imag_part.reshape(
                    planes, columns, local_kpoints * band_count, local_kpoints * group_width
                )
                / volume
            )
            held_real = picked[0][..., None, :]
            held_imag = picked[1][..., None, :]
            add_real = jnp.sum(held_real * real_part - held_imag * imag_part, axis=3)
            add_imag = jnp.sum(held_real * imag_part + held_imag * real_part, axis=3)
            return (totals[0] + weight * add_real, totals[1] + weight * add_imag)

        return lax.fori_loop(0, trip_count, one_group, totals)

    block_data = orbitals
    for rotation in range(STEPS):
        anchor = (own_group - rotation) % groups
        current = block_data
        totals = handle(current, anchor, totals)
        if rotation + 1 < STEPS:
            block_data = passed_along(block_data, "ka", 1)
    stacked = jnp.stack(totals).reshape(2, planes, columns, local_kpoints, band_count)
    vectors = jnp.transpose(stacked, (3, 4, 0, 1, 2))
    flat_orbitals = orbitals.astype(jnp.float32).reshape(
        local_kpoints, band_count, 2, planes * columns
    )
    flat_vectors = vectors.reshape(local_kpoints, band_count, 2, planes * columns)
    matrix_real = (
        contract(flat_orbitals[:, :, 0], flat_vectors[:, :, 0])
        + contract(flat_orbitals[:, :, 1], flat_vectors[:, :, 1])
    ) / volume
    matrix_imag = (
        contract(flat_orbitals[:, :, 0], flat_vectors[:, :, 1])
        - contract(flat_orbitals[:, :, 1], flat_vectors[:, :, 0])
    ) / volume
    matrix = over_copies(jnp.stack((matrix_real, matrix_imag), axis=1), "ga")
    occupied = (band_index[None, :] < own_counts[:, None]).astype(jnp.float32)
    energy_part = jnp.sum(occupied * jnp.diagonal(matrix[:, 0], axis1=1, axis2=2)) / (2.0 * kpoints)
    energy = over_copies(energy_part, "ka")
    return (vectors, matrix, energy)


def solution(mesh):
    in_specs = (P("ka", None, None, "ga", None), P(), P(), P(None, None, "ga"))
    out_specs = (P("ka", None, None, "ga", None), P("ka", None, None, None), P())
    return jax.shard_map(
        on_device, mesh=mesh, in_specs=in_specs, out_specs=out_specs, check_vma=False
    )
```

profile of v0, /device:TPU:1, one launch (start us, length us, event | category | flops | bytes accessed | tf_op | source)
XLA Modules:
  0.0 806.8 jit_solution(4193160292878964922)
XLA Ops:
  10.7 375.9 %while.32 = (s32[]{:T(128)}, f32[1,1024,16]{1,2,0:T(8,128)S(1)}, f32[1,1024,16]{1,2,0:T(8,128)S(1)}, s32[]{:T(128)}, f32[2,1,1024,16]{2,3,1,0:T(8,128)S(1)}, /*i...) while((s32[]{:T(128)}, f32[1,1024,16]{1,2,0:T(8,128)S(1)}, ...), condition=%wide.region_4.5_spmd.clone.clone, body=%wide.region_1.4_spmd.clone.clone.sunk | while | flops 455792640 | bytes 40517936 | solution.py:169
  33.9 11.4 %all-to-all-start = ((f32[32,1,4096]{2,1,0:T(1,128)}), f32[32,1,4096]{2,1,0:T(1,128)S(1)}, u32[]{:S(2)}, u32[]{:S(2)}) async-start(f32[32,1,4096]{2,1,0:T(1,128)} %reshape.863), calls=%async_computation | async-start | bytes 1048576 | tf_op jit(solution)/shard_map/while/body/all_to_all | solution.py:127
  46.3 15.7 %all-to-all-done = f32[32,1,4096]{2,1,0:T(1,128)S(1)} async-done(((f32[32,1,4096]{2,1,0:T(1,128)}), f32[32,1,4096]{2,1,0:T(1,128)S(1)}, u32[]{:S(2)}, u32[]{:S(2)}) %all-to-all-start) | async-done | bytes 524320 | tf_op jit(solution)/shard_map/while/body/all_to_all | solution.py:127
  73.7 5.9 all-to-all-start.1
  79.6 16.5 %all-to-all-done.1 = f32[32,1,4096]{2,1,0:T(1,128)S(1)} async-done(((f32[32,1,4096]{2,1,0:T(1,128)}), f32[32,1,4096]{2,1,0:T(1,128)S(1)}, u32[]{:S(2)}, u32[]{:S(2)}) %all-to-all-start.1) | async-done | bytes 524320 | tf_op jit(solution)/shard_map/while/body/all_to_all | solution.py:140
  138.0 15.8 %all-to-all-done = f32[32,1,4096]{2,1,0:T(1,128)S(1)} async-done(((f32[32,1,4096]{2,1,0:T(1,128)}), f32[32,1,4096]{2,1,0:T(1,128)S(1)}, u32[]{:S(2)}, u32[]{:S(2)}) %all-to-all-start) | async-done | bytes 524320 | tf_op jit(solution)/shard_map/while/body/all_to_all | solution.py:127
  165.6 6.1 all-to-all-start.1
  171.8 16.5 %all-to-all-done.1 = f32[32,1,4096]{2,1,0:T(1,128)S(1)} async-done(((f32[32,1,4096]{2,1,0:T(1,128)}), f32[32,1,4096]{2,1,0:T(1,128)S(1)}, u32[]{:S(2)}, u32[]{:S(2)}) %all-to-all-start.1) | async-done | bytes 524320 | tf_op jit(solution)/shard_map/while/body/all_to_all | solution.py:140
  230.2 15.8 %all-to-all-done = f32[32,1,4096]{2,1,0:T(1,128)S(1)} async-done(((f32[32,1,4096]{2,1,0:T(1,128)}), f32[32,1,4096]{2,1,0:T(1,128)S(1)}, u32[]{:S(2)}, u32[]{:S(2)}) %all-to-all-start) | async-done | bytes 524320 | tf_op jit(solution)/shard_map/while/body/all_to_all | solution.py:127
  257.7 5.9 all-to-all-start.1
  263.7 16.5 %all-to-all-done.1 = f32[32,1,4096]{2,1,0:T(1,128)S(1)} async-done(((f32[32,1,4096]{2,1,0:T(1,128)}), f32[32,1,4096]{2,1,0:T(1,128)S(1)}, u32[]{:S(2)}, u32[]{:S(2)}) %all-to-all-start.1) | async-done | bytes 524320 | tf_op jit(solution)/shard_map/while/body/all_to_all | solution.py:140
  322.1 15.8 %all-to-all-done = f32[32,1,4096]{2,1,0:T(1,128)S(1)} async-done(((f32[32,1,4096]{2,1,0:T(1,128)}), f32[32,1,4096]{2,1,0:T(1,128)S(1)}, u32[]{:S(2)}, u32[]{:S(2)}) %all-to-all-start) | async-done | bytes 524320 | tf_op jit(solution)/shard_map/while/body/all_to_all | solution.py:127
  349.6 6.1 all-to-all-start.1
  355.8 16.5 %all-to-all-done.1 = f32[32,1,4096]{2,1,0:T(1,128)S(1)} async-done(((f32[32,1,4096]{2,1,0:T(1,128)}), f32[32,1,4096]{2,1,0:T(1,128)S(1)}, u32[]{:S(2)}, u32[]{:S(2)}) %all-to-all-start.1) | async-done | bytes 524320 | tf_op jit(solution)/shard_map/while/body/all_to_all | solution.py:140
  386.6 206.6 %while.33 = (s32[]{:T(128)}, f32[1,1024,16]{1,2,0:T(8,128)S(1)}, f32[1,1024,16]{1,2,0:T(8,128)S(1)}, s32[]{:T(128)}, f32[2,1,1024,16]{2,3,1,0:T(8,128)S(1)}, /*i...) while((s32[]{:T(128)}, f32[1,1024,16]{1,2,0:T(8,128)S(1)}, ...), condition=%wide.region_9.10_spmd.clone.clone, body=%wide.region_6.9_spmd.clone.clone.sunk | while | flops 455792640 | bytes 40517936 | solution.py:169
  409.6 13.2 %copy.480 = f32[2,1,1024,64]{3,1,0,2:T(1,128)S(1)} copy(f32[2,1,1024,64]{3,2,1,0:T(8,128)S(1)} %pad_maximum_fusion.12) | data formatting | bytes 1048576 | tf_op jit(solution)/shard_map/while/body/stack | solution.py:124
  436.1 15.8 %all-to-all-done.2 = f32[32,1,4096]{2,1,0:T(1,128)S(1)} async-done(((f32[32,1,4096]{2,1,0:T(1,128)}), f32[32,1,4096]{2,1,0:T(1,128)S(1)}, u32[]{:S(2)}, u32[]{:S(2)}) %all-to-all-start.2) | async-done | bytes 524320 | tf_op jit(solution)/shard_map/while/body/all_to_all | solution.py:127
  463.6 6.1 all-to-all-start.3
  469.7 16.5 %all-to-all-done.3 = f32[32,1,4096]{2,1,0:T(1,128)S(1)} async-done(((f32[32,1,4096]{2,1,0:T(1,128)}), f32[32,1,4096]{2,1,0:T(1,128)S(1)}, u32[]{:S(2)}, u32[]{:S(2)}) %all-to-all-start.3) | async-done | bytes 524320 | tf_op jit(solution)/shard_map/while/body/all_to_all | solution.py:140
  527.9 15.8 %all-to-all-done.2 = f32[32,1,4096]{2,1,0:T(1,128)S(1)} async-done(((f32[32,1,4096]{2,1,0:T(1,128)}), f32[32,1,4096]{2,1,0:T(1,128)S(1)}, u32[]{:S(2)}, u32[]{:S(2)}) %all-to-all-start.2) | async-done | bytes 524320 | tf_op jit(solution)/shard_map/while/body/all_to_all | solution.py:127
  555.3 5.9 all-to-all-start.3
  561.3 16.5 %all-to-all-done.3 = f32[32,1,4096]{2,1,0:T(1,128)S(1)} async-done(((f32[32,1,4096]{2,1,0:T(1,128)}), f32[32,1,4096]{2,1,0:T(1,128)S(1)}, u32[]{:S(2)}, u32[]{:S(2)}) %all-to-all-start.3) | async-done | bytes 524320 | tf_op jit(solution)/shard_map/while/body/all_to_all | solution.py:140
  602.3 7.2 all-to-all-done.4
  614.3 191.7 %all_to_all.67 = f32[8,1,1]{2,1,0:T(1,128)S(1)} all-to-all(f32[8,1,1]{2,1,0:T(1,128)S(1)} %broadcast_in_dim.13), channel_id=1, replica_groups=mesh['ka'=8,'ga'=32] {'ka'}, dimensions={0} | all-to-all | bytes 64 | tf_op jit(solution)/shard_map/all_to_all | solution.py:21
  (393 shorter events, 332.5 us)
Async XLA Ops:
  0.6 2.2 copy-start.2
  0.7 0.7 copy-start.4
  2.8 4.3 copy-start.1
  2.9 7.7 collective-permute-start
  33.9 28.0 %all-to-all-start = ((f32[32,1,4096]{2,1,0:T(1,128)}), f32[32,1,4096]{2,1,0:T(1,128)S(1)}, u32[]{:S(2)}, u32[]{:S(2)}) async-start(f32[32,1,4096]{2,1,0:T(1,128)} %reshape.863), calls=%async_computation | async-start | bytes 1048576 | tf_op jit(solution)/shard_map/while/body/all_to_all | solution.py:127
  73.7 22.5 %all-to-all-start.1 = ((f32[32,1,4096]{2,1,0:T(1,128)}), f32[32,1,4096]{2,1,0:T(1,128)S(1)}, u32[]{:S(2)}, u32[]{:S(2)}) async-start(f32[32,1,4096]{2,1,0:T(1,128)} %reshape.865), calls=%async_computation.1 | async-start | bytes 1048576 | tf_op jit(solution)/shard_map/while/body/all_to_all | solution.py:140
  131.5 22.4 %all-to-all-start = ((f32[32,1,4096]{2,1,0:T(1,128)}), f32[32,1,4096]{2,1,0:T(1,128)S(1)}, u32[]{:S(2)}, u32[]{:S(2)}) async-start(f32[32,1,4096]{2,1,0:T(1,128)} %reshape.863), calls=%async_computation | async-start | bytes 1048576 | tf_op jit(solution)/shard_map/while/body/all_to_all | solution.py:127
  165.6 22.7 %all-to-all-start.1 = ((f32[32,1,4096]{2,1,0:T(1,128)}), f32[32,1,4096]{2,1,0:T(1,128)S(1)}, u32[]{:S(2)}, u32[]{:S(2)}) async-start(f32[32,1,4096]{2,1,0:T(1,128)} %reshape.865), calls=%async_computation.1 | async-start | bytes 1048576 | tf_op jit(solution)/shard_map/while/body/all_to_all | solution.py:140
  223.6 22.4 %all-to-all-start = ((f32[32,1,4096]{2,1,0:T(1,128)}), f32[32,1,4096]{2,1,0:T(1,128)S(1)}, u32[]{:S(2)}, u32[]{:S(2)}) async-start(f32[32,1,4096]{2,1,0:T(1,128)} %reshape.863), calls=%async_computation | async-start | bytes 1048576 | tf_op jit(solution)/shard_map/while/body/all_to_all | solution.py:127
  257.7 22.5 %all-to-all-start.1 = ((f32[32,1,4096]{2,1,0:T(1,128)}), f32[32,1,4096]{2,1,0:T(1,128)S(1)}, u32[]{:S(2)}, u32[]{:S(2)}) async-start(f32[32,1,4096]{2,1,0:T(1,128)} %reshape.865), calls=%async_computation.1 | async-start | bytes 1048576 | tf_op jit(solution)/shard_map/while/body/all_to_all | solution.py:140
  315.5 22.4 %all-to-all-start = ((f32[32,1,4096]{2,1,0:T(1,128)}), f32[32,1,4096]{2,1,0:T(1,128)S(1)}, u32[]{:S(2)}, u32[]{:S(2)}) async-start(f32[32,1,4096]{2,1,0:T(1,128)} %reshape.863), calls=%async_computation | async-start | bytes 1048576 | tf_op jit(solution)/shard_map/while/body/all_to_all | solution.py:127
  349.6 22.7 %all-to-all-start.1 = ((f32[32,1,4096]{2,1,0:T(1,128)}), f32[32,1,4096]{2,1,0:T(1,128)S(1)}, u32[]{:S(2)}, u32[]{:S(2)}) async-start(f32[32,1,4096]{2,1,0:T(1,128)} %reshape.865), calls=%async_computation.1 | async-start | bytes 1048576 | tf_op jit(solution)/shard_map/while/body/all_to_all | solution.py:140
  429.6 22.4 %all-to-all-start.2 = ((f32[32,1,4096]{2,1,0:T(1,128)}), f32[32,1,4096]{2,1,0:T(1,128)S(1)}, u32[]{:S(2)}, u32[]{:S(2)}) async-start(f32[32,1,4096]{2,1,0:T(1,128)} %reshape.869), calls=%async_computation.2 | async-start | bytes 1048576 | tf_op jit(solution)/shard_map/while/body/all_to_all | solution.py:127
  463.6 22.7 %all-to-all-start.3 = ((f32[32,1,4096]{2,1,0:T(1,128)}), f32[32,1,4096]{2,1,0:T(1,128)S(1)}, u32[]{:S(2)}, u32[]{:S(2)}) async-start(f32[32,1,4096]{2,1,0:T(1,128)} %reshape.871), calls=%async_computation.3 | async-start | bytes 1048576 | tf_op jit(solution)/shard_map/while/body/all_to_all | solution.py:140
  521.3 22.4 %all-to-all-start.2 = ((f32[32,1,4096]{2,1,0:T(1,128)}), f32[32,1,4096]{2,1,0:T(1,128)S(1)}, u32[]{:S(2)}, u32[]{:S(2)}) async-start(f32[32,1,4096]{2,1,0:T(1,128)} %reshape.869), calls=%async_computation.2 | async-start | bytes 1048576 | tf_op jit(solution)/shard_map/while/body/all_to_all | solution.py:127
  555.3 22.5 %all-to-all-start.3 = ((f32[32,1,4096]{2,1,0:T(1,128)}), f32[32,1,4096]{2,1,0:T(1,128)S(1)}, u32[]{:S(2)}, u32[]{:S(2)}) async-start(f32[32,1,4096]{2,1,0:T(1,128)} %reshape.871), calls=%async_computation.3 | async-start | bytes 1048576 | tf_op jit(solution)/shard_map/while/body/all_to_all | solution.py:140
  593.2 0.8 copy-start
  595.9 13.6 %all-to-all-start.4 = ((f32[32,1,256]{2,1,0:T(1,128)}), f32[32,1,256]{2,1,0:T(1,128)S(1)}, u32[]{:S(2)}, u32[]{:S(2)}) async-start(f32[32,1,256]{2,1,0:T(1,128)} %reshape.849), calls=%async_computation.4 | async-start | bytes 65536 | tf_op jit(solution)/shard_map/all_to_all | solution.py:21
  611.2 0.6 copy-start.3
  612.3 0.7 copy-start.5
where the time goes:
time: 811 us; the launch traced here: 807 us
  waiting for transfers between devices  203 us (25%)
  blocking collectives  192 us (24%)
  matrix products  141 us (17%)
  local copies, waits for them, and re-layouts  107 us (13%)
  starting transfers between devices  83.4 us (10%)
  other arithmetic  60.3 us (7%)
  loops' own time  17.6 us (2%)
    all_to_all x1, blocking collectives, copy_for_each(): lax.all_to_all(jnp.broadcast_to(shard[None], (peers, *shard.shape)), axis...  192 us
    dot_general x108, matrix products, apply_table(): jnp.tensordot(table, values, axes=([1], [dimension]), precision=highest)  139 us
    all_to_all x6, waiting for transfers between devices, one_group(): lax.all_to_all(jnp.stack((real_part, imag_part)), 'ga', split_axis=1, con...  99.2 us
    all_to_all x6, waiting for transfers between devices, one_group(): lax.all_to_all(packed, 'ga', split_axis=2, concat_axis=1, tiled=True)  94.7 us
    all_to_all x6, starting transfers between devices, one_group(): lax.all_to_all(packed, 'ga', split_axis=2, concat_axis=1, tiled=True)  39.6 us
    all_to_all x6, starting transfers between devices, one_group(): lax.all_to_all(jnp.stack((real_part, imag_part)), 'ga', split_axis=1, con...  36.1 us
    while x30, local copies, waits for them, and re-layouts  33.8 us
    while x6, other arithmetic  26.1 us
  transfers between devices with their start and end apart: 14, of which 14 were waited for; matrix products, arithmetic and copies ran while one was open for 1% of the time, Pallas kernels for 0%

commit v1 on v0

v1 whole, which is shorter than its diff:
```python
import numpy as np
import jax
import jax.numpy as jnp
from jax import lax
from jax.experimental import pallas as pl
from jax.experimental.pallas import tpu as pltpu
from jax.sharding import PartitionSpec as P

highest = lax.Precision.HIGHEST
f32 = jnp.float32
bf16 = jnp.bfloat16


def embed(matrix):
    return np.block([[matrix.real, -matrix.imag], [matrix.imag, matrix.real]])


def split(matrix):
    high = matrix.astype(np.float32).astype(bf16)
    low = (matrix - high.astype(np.float64)).astype(np.float32).astype(bf16)
    return high, low


def constants():
    rows = np.arange(128)
    x_at, yh_at = rows // 8, rows % 8
    jj_at, glo_at, gxh_at = rows // 64, rows // 8 % 8, rows % 8
    forward, inverse = [], []
    for parity in range(2):
        gx_at = 4 * gxh_at + 2 * jj_at + parity
        phase = gx_at[:, None] * x_at[None, :] / 32.0 + glo_at[:, None] * yh_at[None, :] / 8.0
        real = embed(np.exp(-2j * np.pi * phase))
        for held, matrix in ((forward, real), (inverse, real.T)):
            high, low = split(matrix)
            held.append(np.concatenate((high, low, high), axis=1))
    lanes = np.arange(128)
    first, last = lanes // 32, lanes % 32
    phase = first[:, None] * first[None, :] / 4.0 + last[:, None] * last[None, :] / 32.0
    real = embed(np.exp(-2j * np.pi * phase)).T
    right = []
    for matrix in (real, real.T):
        high, low = split(matrix)
        right.append(np.concatenate((high, low, high), axis=0))
    turn = 2.0 * np.pi * (glo_at[:, None] * first[None, :]) / 32.0
    twiddle = np.stack((np.cos(turn), np.sin(turn))).astype(np.float32)
    return np.stack(forward + inverse), np.stack(right), twiddle


def two_terms(value):
    high = value.astype(bf16)
    low = (value - high.astype(f32)).astype(bf16)
    return high, low


def exchange_kernel(
    scale, first_call, trips, received, partners, left, right, twiddle, held, total,
    own, screen,
):
    for a in range(2):
        own[a] = received[:, 4 + a].astype(f32)
    raw = received[:, 6].astype(f32)
    raw = (raw[:, :8] + raw[:, 8:]) * scale
    raw = raw.reshape(4, 64, 128)
    lane_group = lax.broadcasted_iota(jnp.int32, (64, 128), 1) // 32
    for j in range(4):
        placed = jnp.zeros((64, 128), f32)
        for i in range(4):
            shift = (i - j) % 4 * 32
            moved = pltpu.roll(raw[i], shift, 1) if shift else raw[i]
            placed = jnp.where(lane_group == i, moved, placed)
        screen[j % 2, (j // 2) * 64 : (j // 2) * 64 + 64] = placed
    if first_call:
        total[...] = jnp.zeros_like(total)
    else:
        total[...] = held[...]

    def one_partner(b, carry):
        other = partners[:, b].astype(f32)
        other_real, other_imag = other[:, :8], other[:, 8:]
        sums, gaps = [[], []], [[], []]
        for a in range(2):
            own_real, own_imag = own[a, :, :8], own[a, :, 8:]
            density = (
                own_real * other_real + own_imag * other_imag,
                own_imag * other_real - own_real * other_imag,
            )
            for part in range(2):
                low, high = density[part][:16], density[part][16:]
                sums[part].append((low + high).reshape(128, 128))
                gaps[part].append((low - high).reshape(128, 128))
        back = []
        for parity, parts in enumerate((sums, gaps)):
            stacked = jnp.concatenate(
                [jnp.concatenate(parts[part], axis=1) for part in range(2)], axis=0
            )
            high, low = two_terms(stacked)
            turned = jnp.dot(
                left[parity],
                jnp.concatenate((high, high, low), axis=0),
                preferred_element_type=f32,
            )
            cosine, sine = twiddle[0], twiddle[1]
            lines = []
            for a in range(2):
                real = turned[:128, a * 128 : a * 128 + 128]
                imag = turned[128:, a * 128 : a * 128 + 128]
                lines.append(
                    jnp.concatenate((real * cosine + imag * sine, imag * cosine - real * sine), axis=1)
                )
            high, low = two_terms(jnp.concatenate(lines, axis=0))
            spectra = jnp.dot(
                jnp.concatenate((high, high, low), axis=1), right[0], preferred_element_type=f32
            )
            factor = screen[parity]
            factor = jnp.concatenate((factor, factor), axis=1)
            factor = jnp.concatenate((factor, factor), axis=0)
            high, low = two_terms(spectra * factor)
            lines = jnp.dot(
                jnp.concatenate((high, high, low), axis=1), right[1], preferred_element_type=f32
            )
            reals, imags = [], []
            for a in range(2):
                real = lines[a * 128 : a * 128 + 128, :128]
                imag = lines[a * 128 : a * 128 + 128, 128:]
                reals.append(real * cosine - imag * sine)
                imags.append(imag * cosine + real * sine)
            stacked = jnp.concatenate(
                (jnp.concatenate(reals, axis=1), jnp.concatenate(imags, axis=1)), axis=0
            )
            high, low = two_terms(stacked)
            back.append(
                jnp.dot(
                    left[2 + parity],
                    jnp.concatenate((high, high, low), axis=0),
                    preferred_element_type=f32,
                )
            )
        even, odd = back
        for side in range(2):
            field = even + odd if side == 0 else even - odd
            rows = slice(side * 16, side * 16 + 16)
            b_real, b_imag = other_real[rows], other_imag[rows]
            for a in range(2):
                real = field[:128, a * 128 : a * 128 + 128].reshape(16, 8, 128)
                imag = field[128:, a * 128 : a * 128 + 128].reshape(16, 8, 128)
                total[rows, 2 * a] += b_real * real - b_imag * imag
                total[rows, 2 * a + 1] += b_real * imag + b_imag * real
        return carry

    lax.fori_loop(0, trips[0], one_partner, 0)


def exchange(scale, trips, received, partners, left, right, twiddle, held):
    first_call = held is None
    vmem = pl.BlockSpec(memory_space=pltpu.VMEM)
    operands = [trips, received, partners, left, right, twiddle]
    specs = [pl.BlockSpec(memory_space=pltpu.SMEM)] + [vmem] * 5

    if first_call:

        def body(trips, received, partners, left, right, twiddle, *rest):
            exchange_kernel(scale, True, trips, received, partners, left, right, twiddle, None, *rest)

    else:
        operands.append(held)
        specs.append(vmem)

        def body(*refs):
            exchange_kernel(scale, False, *refs)

    return pl.pallas_call(
        body,
        out_shape=jax.ShapeDtypeStruct((32, 4, 8, 128), f32),
        in_specs=specs,
        out_specs=vmem,
        scratch_shapes=[pltpu.VMEM((2, 32, 16, 128), f32), pltpu.VMEM((2, 128, 128), f32)],
        cost_estimate=pl.CostEstimate(
            flops=4 * 12 * 2 * 512 * 256 * 256, bytes_accessed=4 << 20, transcendentals=0
        ),
        name="exchange_first" if first_call else "exchange_second",
    )(*operands)


def contract(first_field, second_field):
    return jnp.einsum("kar,kbr->kab", first_field, second_field, precision=highest)


def over_copies(shard, axis):
    peers = lax.axis_size(axis)
    return lax.all_to_all(
        jnp.broadcast_to(shard[None], (peers, *shard.shape)), axis, 0, 0, tiled=True
    ).sum(axis=0)


def on_device(orbitals, band_counts, pair_slot, kernel):
    left, right, twiddle = (jnp.asarray(table) for table in constants())
    groups = lax.axis_size("ka")
    own_group = lax.axis_index("ka")
    member = lax.axis_index("ga")
    core = member % 2
    chip = member // 2
    partner_group = (own_group - 1) % groups
    volume = 32768.0

    pairs = [(source, (source + 1) % groups) for source in range(groups)]
    before = lax.ppermute(orbitals, "ka", pairs)
    window = jnp.concatenate(
        (own_group * 2 + jnp.arange(2), partner_group * 2 + jnp.arange(2))
    ).astype(jnp.int32)

    both = jnp.stack((orbitals, before)).reshape(4, 4, 2, 16, 128)
    partners = jnp.swapaxes(both, 1, 2)[:, None]
    partners = jnp.broadcast_to(partners, (4, 4, 2, 4, 16, 128))
    owns = orbitals.reshape(1, 4, 2, 2, 16, 128)
    owns = jnp.broadcast_to(owns, (4, 4, 2, 2, 16, 128))
    slots = pair_slot[own_group * 2 + jnp.arange(2)][:, window].T.reshape(8)
    chosen = kernel.reshape(16, 8, 128)[slots]
    chosen_high = lax.reduce_precision(chosen, 8, 7)
    chosen_low = chosen - chosen_high
    chosen = jnp.concatenate((chosen_high.astype(bf16), chosen_low.astype(bf16)), axis=1).reshape(4, 2, 1, 1, 1, 16, 128)
    chosen = jnp.broadcast_to(chosen, (4, 2, 2, 2, 1, 16, 128)).reshape(4, 4, 2, 1, 16, 128)
    packed = jnp.concatenate((partners, owns, chosen), axis=3).reshape(32, 7, 16, 128)
    received = lax.all_to_all(packed, "ga", 0, 0, tiled=True)
    swapped = lax.ppermute(received[:, :4], "ga", [(i, i ^ 1) for i in range(32)])

    count = band_counts[window[chip // 4]]
    own_trips = (count - core + 1) // 2
    swapped_trips = (count - (1 - core) + 1) // 2
    scale = -1.0 / (16.0 * volume)
    total = exchange(scale, own_trips.reshape(1), received, received, left, right, twiddle, None)
    total = exchange(scale, swapped_trips.reshape(1), received, swapped, left, right, twiddle, total)

    returned = lax.all_to_all(total, "ga", 0, 0, tiled=True)
    vectors = returned.reshape(4, 2, 8, 2, 1024).sum(axis=0)
    flat_orbitals = orbitals.astype(f32).reshape(2, 8, 2, 1024)
    matrix_real = (
        contract(flat_orbitals[:, :, 0], vectors[:, :, 0])
        + contract(flat_orbitals[:, :, 1], vectors[:, :, 1])
    ) / volume
    matrix_imag = (
        contract(flat_orbitals[:, :, 0], vectors[:, :, 1])
        - contract(flat_orbitals[:, :, 1], vectors[:, :, 0])
    ) / volume
    matrix = over_copies(jnp.stack((matrix_real, matrix_imag), axis=1), "ga")
    own_counts = lax.dynamic_slice_in_dim(band_counts, own_group * 2, 2)
    occupied = (jnp.arange(8)[None, :] < own_counts[:, None]).astype(f32)
    energy_part = jnp.sum(occupied * jnp.diagonal(matrix[:, 0], axis1=1, axis2=2)) / 32.0
    energy = over_copies(energy_part, "ka")
    return (vectors.reshape(2, 8, 2, 1, 1024), matrix, energy)


def solution(mesh):
    in_specs = (P("ka", None, None, "ga", None), P(), P(), P(None, None, "ga"))
    out_specs = (P("ka", None, None, "ga", None), P("ka", None, None, None), P())
    return jax.shard_map(
        on_device, mesh=mesh, in_specs=in_specs, out_specs=out_specs, check_vma=False
    )
```

time: 811 us -> 129 us (0.16)
  blocking collectives: 192 us -> 10.2 us
  waiting for transfers between devices: 203 us -> 49.1 us
  matrix products: 141 us -> 0.73 us
  local copies, waits for them, and re-layouts: 107 us -> 10 us
  starting transfers between devices: 83.4 us -> 25.3 us
  other arithmetic: 60.3 us -> 4.56 us
  Pallas kernels: 0 us -> 23.7 us
  loops' own time: 17.6 us -> 0 us
    all_to_all x1, blocking collectives: 192 us -> 10.2 us  [over_copies(): lax.all_to_all(jnp.broadcast_to(shard[None], (peers, *shard.shape)), axis...]
    all_to_all x13 -> x3, waiting for transfers between devices: 201 us -> 47.4 us  [the longest x1 23.7 us: on_device(): received = lax.all_to_all(packed, 'ga', 0, 0, tiled=True)]
    dot_general x110 -> x0, matrix products: 140 us -> none  [the longest x108 139 us: apply_table(): jnp.tensordot(table, values, axes=([1], [dimension]), precision=highest)]
    all_to_all x13 -> x3, starting transfers between devices: 81.3 us -> 20.7 us  [the longest x1 11.6 us: on_device(): received = lax.all_to_all(packed, 'ga', 0, 0, tiled=True)]
    while x30 -> x0, local copies, waits for them, and re-layouts: 33.8 us -> none
    while x6 -> x0, other arithmetic: 26.1 us -> none
    another operation x14 -> x0, local copies, waits for them, and re-layouts: 24.1 us -> none  [the longest x12 24.1 us: one_group(): jnp.stack((real_part, imag_part))]
    pallas_call x0 -> x2, Pallas kernels: none -> 23.7 us  [exchange(): pl.pallas_call(body, out_shape=jax.ShapeDtypeStruct((32, 4, 8, 128), f32)...]
  transfers between devices with their start and end apart: 14 -> 5, of which waited for: 14 -> 4; matrix products, arithmetic and copies ran while one was open for 1% -> 5% of each run, Pallas kernels for 0% -> 9%
where the time goes in v1:
time: 129 us
  waiting for transfers between devices  49.1 us (38%)
  starting transfers between devices  25.3 us (20%)
  Pallas kernels  23.7 us (18%)
  blocking collectives  10.2 us (8%)
  local copies, waits for them, and re-layouts  10 us (8%)
  between operations  4.91 us (4%)
  other arithmetic  4.56 us (4%)
    pallas_call x2, Pallas kernels, exchange(): pl.pallas_call(body, out_shape=jax.ShapeDtypeStruct((32, 4, 8, 128), f32)...  23.7 us
    all_to_all x1, waiting for transfers between devices, on_device(): received = lax.all_to_all(packed, 'ga', 0, 0, tiled=True)  23.7 us
    all_to_all x1, waiting for transfers between devices, on_device(): returned = lax.all_to_all(total, 'ga', 0, 0, tiled=True)  16.5 us
    all_to_all x1, starting transfers between devices, on_device(): received = lax.all_to_all(packed, 'ga', 0, 0, tiled=True)  11.6 us
    all_to_all x1, blocking collectives, over_copies(): lax.all_to_all(jnp.broadcast_to(shard[None], (peers, *shard.shape)), axis...  10.2 us
    all_to_all x1, waiting for transfers between devices, over_copies(): lax.all_to_all(jnp.broadcast_to(shard[None], (peers, *shard.shape)), axis...  7.23 us
    all_to_all x1, starting transfers between devices, over_copies(): lax.all_to_all(jnp.broadcast_to(shard[None], (peers, *shard.shape)), axis...  5.52 us
    all_to_all x1, starting transfers between devices, on_device(): returned = lax.all_to_all(total, 'ga', 0, 0, tiled=True)  3.68 us
  transfers between devices with their start and end apart: 5, of which 4 were waited for; matrix products, arithmetic and copies ran while one was open for 5% of the time, Pallas kernels for 9%

profile of v1, /device:TPU:1, one launch (start us, length us, event | category | flops | bytes accessed | tf_op | source)
XLA Modules:
  0.0 128.6 jit_solution(7238943718068893016)
XLA Ops:
  0.6 2.1 %collective-permute-start = (bf16[2,8,2,1,1024]{4,2,3,1,0:T(2,128)(2,1)}, bf16[2,8,2,1,1024]{4,2,3,1,0:T(2,128)(2,1)S(1)}, u32[]{:S(2)}, u32[]{:S(2)}) collective-permute-start(bf16[2,8,2,1,1024]{4,2,3,1,0:T(2,128)(2,1)} %param.7), channel_id=1, source_target_pairs={{0,32},{32,64},{64,96},{96,128},{128,160},{160,192},{192,224},{224... | collective-permute-start | bytes 196616 | tf_op jit(solution)/shard_map/ppermute | solution.py:206
  2.8 0.9 broadcast_in_dim.25
  3.7 1.1 reshape.180
  6.8 1.7 %collective-permute-done = bf16[2,8,2,1,1024]{4,2,3,1,0:T(2,128)(2,1)S(1)} collective-permute-done((bf16[2,8,2,1,1024]{4,2,3,1,0:T(2,128)(2,1)}, bf16[2,8,2,1,1024]{4,2,3,1,0:T(2,128)(2,1)S(1)}, u32[]{:S(2)}, u32[]{:S(2)}) %collective-permute-start) | collective-permute-done | bytes 65568 | tf_op jit(solution)/shard_map/ppermute | solution.py:206
  8.5 1.0 pad_maximum_fusion.1
  9.9 1.0 pad_maximum_fusion
  10.9 11.6 %all-to-all-start = ((bf16[32,7,16,128]{3,2,1,0:T(8,128)(2,1)}), bf16[32,7,16,128]{3,2,1,0:T(8,128)(2,1)S(1)}, u32[]{:S(2)}, u32[]{:S(2)}) async-start(bf16[32,7,16,128]{3,2,1,0:T(8,128)(2,1)} %pad_maximum_fusion), calls=%async_computation | async-start | bytes 1835008 | tf_op jit(solution)/shard_map/all_to_all | solution.py:223
  22.5 23.7 %all-to-all-done.received.partners.refs_1_ = bf16[32,7,16,128]{3,2,1,0:T(8,128)(2,1)S(1)} async-done(((bf16[32,7,16,128]{3,2,1,0:T(8,128)(2,1)}), bf16[32,7,16,128]{3,2,1,0:T(8,128)(2,1)S(1)}, u32[]{:S(2)}, u32[]{:S(2)}) %all-to-all-start) | async-done | bytes 917536 | tf_op jit(solution)/shard_map/all_to_all | solution.py:223
  46.3 2.5 %collective-permute-start.1 = (bf16[32,4,16,128]{3,2,1,0:T(8,128)(2,1)S(1)}, bf16[32,4,16,128]{3,2,1,0:T(8,128)(2,1)S(1)}, u32[]{:S(2)}, u32[]{:S(2)}) collective-permute-start(bf16[32,4,16,128]{3,2,1,0:T(8,128)(2,1)S(1)} %slice.36), channel_id=1, source_target_pairs={{0,1},{1,0},{2,3},{3,2},{4,5},{5,4},{6,7},{7,6},{8,9},{9,8},{10,11... | collective-permute-start | bytes 1572872 | tf_op jit(solution)/shard_map/ppermute | solution.py:224
  48.8 0.6 dynamic_slice.9
  51.4 0.6 dynamic_slice.10
  53.3 11.8 %exchange_first.1.refs_6_ = f32[32,4,8,128]{3,2,1,0:T(8,128)} custom-call(s32[1]{0:T(128)} %bitcast.17.trips, bf16[32,7,16,128]{3,2,1,0:T(8,128)(2,1)} %copy-done.1, bf16[32,7,16,128]{3,2,1,0:T(8,128)(2,1)} %copy-done.1, bf16[4,256,768]{2,1,0:T(8,128)(2,1)} %constant.100.clone.left.refs_3_, bf16[2,768,256]{2,1,0:T(8,128)(2,1)} %constant.101.clone.right.refs_4_, ...), custom_call_target="tpu_custom_call" | custom-call | flops 3221225472 | bytes 4194304 | tf_op jit(solution)/shard_map/exchange_first/pallas_call | solution.py:171
  65.2 0.8 copy-done.4
  66.0 11.9 %exchange_second.1 = f32[32,4,8,128]{3,2,1,0:T(8,128)} custom-call(s32[1]{0:T(128)} %bitcast.2.refs_0_, bf16[32,7,16,128]{3,2,1,0:T(8,128)(2,1)} %copy-done.1, bf16[32,4,16,128]{3,2,1,0:T(8,128)(2,1)} %copy-done.4, bf16[4,256,768]{2,1,0:T(8,128)(2,1)} %constant.100.clone.left.refs_3_, bf16[2,768,256]{2,1,0:T(8,128)(2,1)} %constant.101.clone.right.refs_4_, ...), custom_call_target="tpu_custom_call" | custom-call | flops 3221225472 | bytes 4194304 | tf_op jit(solution)/shard_map/exchange_second/pallas_call | solution.py:171
  77.9 3.7 %all-to-all-start.1 = ((f32[32,4,8,128]{3,2,1,0:T(8,128)}), f32[32,4,8,128]{3,2,1,0:T(8,128)S(1)}, u32[]{:S(2)}, u32[]{:S(2)}) async-start(f32[32,4,8,128]{3,2,1,0:T(8,128)} %exchange_second.1), calls=%async_computation.1 | async-start | bytes 1048576 | tf_op jit(solution)/shard_map/all_to_all | solution.py:233
  81.7 16.5 %all-to-all-done.1 = f32[32,4,8,128]{3,2,1,0:T(8,128)S(1)} async-done(((f32[32,4,8,128]{3,2,1,0:T(8,128)}), f32[32,4,8,128]{3,2,1,0:T(8,128)S(1)}, u32[]{:S(2)}, u32[]{:S(2)}) %all-to-all-start.1) | async-done | bytes 524320 | tf_op jit(solution)/shard_map/all_to_all | solution.py:233
  99.8 0.9 reshape.216
  100.6 5.5 %all-to-all-start.2 = ((f32[32,1,256]{2,1,0:T(1,128)}), f32[32,1,256]{2,1,0:T(1,128)S(1)}, u32[]{:S(2)}, u32[]{:S(2)}) async-start(f32[32,1,256]{2,1,0:T(1,128)} %reshape.216), calls=%async_computation.2 | async-start | bytes 65536 | tf_op jit(solution)/shard_map/all_to_all | solution.py:190
  106.2 0.8 copy.60
  107.0 7.2 %all-to-all-done.2 = f32[32,1,256]{2,1,0:T(1,128)S(1)} async-done(((f32[32,1,256]{2,1,0:T(1,128)}), f32[32,1,256]{2,1,0:T(1,128)S(1)}, u32[]{:S(2)}, u32[]{:S(2)}) %all-to-all-start.2) | async-done | bytes 32800 | tf_op jit(solution)/shard_map/all_to_all | solution.py:190
  114.7 0.7 reduce.1
  116.5 0.6 fusion.7
  117.8 10.2 %all_to_all.21 = f32[8,1,1]{2,1,0:T(1,128)S(1)} all-to-all(f32[8,1,1]{2,1,0:T(1,128)S(1)} %broadcast_in_dim.56), channel_id=1, replica_groups=mesh['ka'=8,'ga'=32] {'ka'}, dimensions={0} | all-to-all | bytes 64 | tf_op jit(solution)/shard_map/all_to_all | solution.py:190
  128.0 0.6 reduce_sum.39
  (57 shorter events, 5.7 us)
Async XLA Ops:
  0.6 4.2 %copy-start = (s32[16,16]{1,0:T(8,128)S(1)}, s32[16,16]{1,0:T(8,128)}, u32[]{:S(2)}) copy-start(s32[16,16]{1,0:T(8,128)} %param.9) | copy-start | bytes 3076
  0.6 7.9 %collective-permute-start = (bf16[2,8,2,1,1024]{4,2,3,1,0:T(2,128)(2,1)}, bf16[2,8,2,1,1024]{4,2,3,1,0:T(2,128)(2,1)S(1)}, u32[]{:S(2)}, u32[]{:S(2)}) collective-permute-start(bf16[2,8,2,1,1024]{4,2,3,1,0:T(2,128)(2,1)} %param.7), channel_id=1, source_target_pairs={{0,32},{32,64},{64,96},{96,128},{128,160},{160,192},{192,224},{224... | collective-permute-start | bytes 196616 | tf_op jit(solution)/shard_map/ppermute | solution.py:206
  10.9 40.4 %copy-start.5 = (s32[16]{0:T(128)S(1)}, s32[16]{0:T(128)}, u32[]{:S(2)}) copy-start(s32[16]{0:T(128)} %param.8) | copy-start | bytes 196
  10.9 35.3 %all-to-all-start = ((bf16[32,7,16,128]{3,2,1,0:T(8,128)(2,1)}), bf16[32,7,16,128]{3,2,1,0:T(8,128)(2,1)S(1)}, u32[]{:S(2)}, u32[]{:S(2)}) async-start(bf16[32,7,16,128]{3,2,1,0:T(8,128)(2,1)} %pad_maximum_fusion), calls=%async_computation | async-start | bytes 1835008 | tf_op jit(solution)/shard_map/all_to_all | solution.py:223
  46.2 7.1 %copy-start.1 = (bf16[32,7,16,128]{3,2,1,0:T(8,128)(2,1)}, bf16[32,7,16,128]{3,2,1,0:T(8,128)(2,1)S(1)}, u32[]{:S(2)}) copy-start(bf16[32,7,16,128]{3,2,1,0:T(8,128)(2,1)S(1)} %all-to-all-done.received.partners.refs_1_) | copy-start | bytes 2752516
  46.3 18.9 %collective-permute-start.1 = (bf16[32,4,16,128]{3,2,1,0:T(8,128)(2,1)S(1)}, bf16[32,4,16,128]{3,2,1,0:T(8,128)(2,1)S(1)}, u32[]{:S(2)}, u32[]{:S(2)}) collective-permute-start(bf16[32,4,16,128]{3,2,1,0:T(8,128)(2,1)S(1)} %slice.36), channel_id=1, source_target_pairs={{0,1},{1,0},{2,3},{3,2},{4,5},{5,4},{6,7},{7,6},{8,9},{9,8},{10,11... | collective-permute-start | bytes 1572872 | tf_op jit(solution)/shard_map/ppermute | solution.py:224
  65.2 0.8 copy-start.4
  66.0 15.6 %copy-start.2 = (bf16[2,8,2,1,1024]{4,2,3,1,0:T(2,128)(2,1)S(1)}, bf16[2,8,2,1,1024]{4,2,3,1,0:T(2,128)(2,1)}, u32[]{:S(2)}) copy-start(bf16[2,8,2,1,1024]{4,2,3,1,0:T(2,128)(2,1)} %param.7) | copy-start | bytes 196612
  77.9 20.3 %all-to-all-start.1 = ((f32[32,4,8,128]{3,2,1,0:T(8,128)}), f32[32,4,8,128]{3,2,1,0:T(8,128)S(1)}, u32[]{:S(2)}, u32[]{:S(2)}) async-start(f32[32,4,8,128]{3,2,1,0:T(8,128)} %exchange_second.1), calls=%async_computation.1 | async-start | bytes 1048576 | tf_op jit(solution)/shard_map/all_to_all | solution.py:233
  100.6 13.6 %all-to-all-start.2 = ((f32[32,1,256]{2,1,0:T(1,128)}), f32[32,1,256]{2,1,0:T(1,128)S(1)}, u32[]{:S(2)}, u32[]{:S(2)}) async-start(f32[32,1,256]{2,1,0:T(1,128)} %reshape.216), calls=%async_computation.2 | async-start | bytes 65536 | tf_op jit(solution)/shard_map/all_to_all | solution.py:190
  115.8 12.8 %copy-start.3 = (f32[2,2,8,8]{3,2,1,0:T(8,128)}, f32[2,2,8,8]{3,2,1,0:T(8,128)S(1)}, u32[]{:S(2)}) copy-start(f32[2,2,8,8]{3,2,1,0:T(8,128)S(1)} %reduce_sum.37) | copy-start | bytes 3076

commit v2 on v1

v2 whole, which is shorter than its diff:
```python
import numpy as np
import jax
import jax.numpy as jnp
from jax import lax
from jax.experimental import pallas as pl
from jax.experimental.pallas import tpu as pltpu
from jax.sharding import PartitionSpec as P

highest = lax.Precision.HIGHEST
f32 = jnp.float32
bf16 = jnp.bfloat16


def embed(matrix):
    return np.block([[matrix.real, -matrix.imag], [matrix.imag, matrix.real]])


def split(matrix):
    high = matrix.astype(np.float32).astype(bf16)
    low = (matrix - high.astype(np.float64)).astype(np.float32).astype(bf16)
    return high, low


def constants():
    rows = np.arange(128)
    x_at, yh_at = rows // 8, rows % 8
    jj_at, glo_at, gxh_at = rows // 64, rows // 8 % 8, rows % 8
    forward, inverse = [], []
    for parity in range(2):
        gx_at = 4 * gxh_at + 2 * jj_at + parity
        phase = gx_at[:, None] * x_at[None, :] / 32.0 + glo_at[:, None] * yh_at[None, :] / 8.0
        real = embed(np.exp(-2j * np.pi * phase))
        for held, matrix in ((forward, real), (inverse, real.T)):
            high, low = split(matrix)
            held.append(np.concatenate((high, low), axis=1))
    lanes = np.arange(128)
    first, last = lanes // 32, lanes % 32
    phase = first[:, None] * first[None, :] / 4.0 + last[:, None] * last[None, :] / 32.0
    real = embed(np.exp(-2j * np.pi * phase)).T
    right = []
    for matrix in (real, real.T):
        high, low = split(matrix)
        right.append(np.concatenate((high, low), axis=0))
    turn = 2.0 * np.pi * (glo_at[:, None] * first[None, :]) / 32.0
    twiddle = np.stack((np.cos(turn), np.sin(turn))).astype(np.float32)
    return np.stack(forward + inverse), np.stack(right), twiddle


def two_terms(value):
    high = value.astype(bf16)
    low = (value - high.astype(f32)).astype(bf16)
    return high, low


MIB = 1 << 20


def place():
    group = lax.axis_index("ka")
    member = lax.axis_index("ga")
    return group, member, member // 2, member % 2


def pack_kernel(pair_slot, orbitals, before, kernel, packed):
    group = lax.axis_index("ka")
    partner_group = lax.rem(group + 7, 8)
    for k2 in range(4):
        source = orbitals if k2 < 2 else before
        second = (group if k2 < 2 else partner_group) * 2 + k2 % 2
        for k in range(2):
            slot = pair_slot[group * 2 + k, second]
            block = kernel[slot]
            high = block.astype(bf16)
            low = (block - high.astype(f32)).astype(bf16)
            unit = jnp.concatenate((high, low), axis=0)
            for chip in range(2):
                for core in range(2):
                    packed[k2 * 8 + k * 4 + chip * 2 + core, 6] = unit
        for b in range(8):
            unit = source[k2 % 2 * 8 + b]
            for aset in range(4):
                packed[k2 * 8 + aset * 2 + b % 2, b // 2] = unit
        for a in range(16):
            packed[k2 * 8 + a // 2, 4 + a % 2] = orbitals[a]


def pack(pair_slot, orbitals, before, kernel):
    vmem = pl.BlockSpec(memory_space=pltpu.VMEM)
    return pl.pallas_call(
        pack_kernel,
        out_shape=jax.ShapeDtypeStruct((32, 7, 16, 128), bf16),
        in_specs=[pl.BlockSpec(memory_space=pltpu.SMEM), vmem, vmem, vmem],
        out_specs=vmem,
        compiler_params=pltpu.CompilerParams(vmem_limit_bytes=4 * MIB),
        name="pack",
    )(pair_slot, orbitals, before, kernel)


def screen_of(received, scale, screen):
    raw = received[:, 6].astype(f32)
    raw = (raw[:, :8] + raw[:, 8:]) * scale
    raw = raw.reshape(4, 64, 128)
    lane_group = lax.broadcasted_iota(jnp.int32, (64, 128), 1) // 32
    for j in range(4):
        placed = jnp.zeros((64, 128), f32)
        for i in range(4):
            shift = (i - j) % 4 * 32
            moved = pltpu.roll(raw[i], shift, 1) if shift else raw[i]
            placed = jnp.where(lane_group == i, moved, placed)
        screen[j % 2, (j // 2) * 64 : (j // 2) * 64 + 64] = placed


def thrice(table, axis):
    size = table.shape[axis] // 2
    return jnp.concatenate((table, lax.slice_in_dim(table, 0, size, axis=axis)), axis=axis)


def through(parts, parity, left, right, twiddle, screen):
    stacked = jnp.concatenate([jnp.concatenate(parts[part], axis=1) for part in range(2)], axis=0)
    high, low = two_terms(stacked)
    turned = jnp.dot(
        thrice(left[parity], 1), jnp.concatenate((high, high, low), axis=0), preferred_element_type=f32
    )
    cosine, sine = twiddle[0], twiddle[1]
    lines = []
    for a in range(2):
        real = turned[:128, a * 128 : a * 128 + 128]
        imag = turned[128:, a * 128 : a * 128 + 128]
        lines.append(
            jnp.concatenate((real * cosine + imag * sine, imag * cosine - real * sine), axis=1)
        )
    high, low = two_terms(jnp.concatenate(lines, axis=0))
    spectra = jnp.dot(
        jnp.concatenate((high, high, low), axis=1), thrice(right[0], 0), preferred_element_type=f32
    )
    factor = screen[parity]
    factor = jnp.concatenate((factor, factor), axis=1)
    factor = jnp.concatenate((factor, factor), axis=0)
    high, low = two_terms(spectra * factor)
    lines = jnp.dot(
        jnp.concatenate((high, high, low), axis=1), thrice(right[1], 0), preferred_element_type=f32
    )
    reals, imags = [], []
    for a in range(2):
        real = lines[a * 128 : a * 128 + 128, :128]
        imag = lines[a * 128 : a * 128 + 128, 128:]
        reals.append(real * cosine - imag * sine)
        imags.append(imag * cosine + real * sine)
    stacked = jnp.concatenate(
        (jnp.concatenate(reals, axis=1), jnp.concatenate(imags, axis=1)), axis=0
    )
    high, low = two_terms(stacked)
    return jnp.dot(
        thrice(left[2 + parity], 1), jnp.concatenate((high, high, low), axis=0), preferred_element_type=f32
    )


def exchange_kernel(
    scale, second_call, counts, received, partners, left, right, twiddle, held, total, energy,
    own, screen,
):
    group, member, chip, core = place()
    k2 = chip // 4
    k2_at = lax.rem(group + 8 - k2 // 2, 8) * 2 + k2 % 2
    parity_of_b = 1 - core if second_call else core
    trips = (counts[k2_at] - parity_of_b + 1) // 2
    for a in range(2):
        own[a] = received[:, 4 + a].astype(f32)
    screen_of(received, scale, screen)
    if second_call:
        total[...] = held[...]
    else:
        total[...] = jnp.zeros_like(total)

    def turn(step, carry):
        others, backs = [], []
        for half in range(UNROLL):
            b = step * UNROLL + half
            other = partners[:, b].astype(f32)
            if half:
                other = other * jnp.where(b < trips, 1.0, 0.0).astype(f32)
            other_real, other_imag = other[:, :8], other[:, 8:]
            sums, gaps = [[], []], [[], []]
            for a in range(2):
                own_real, own_imag = own[a, :, :8], own[a, :, 8:]
                density = (
                    own_real * other_real + own_imag * other_imag,
                    own_imag * other_real - own_real * other_imag,
                )
                for part in range(2):
                    low, high = density[part][:16], density[part][16:]
                    sums[part].append((low + high).reshape(128, 128))
                    gaps[part].append((low - high).reshape(128, 128))
            others.append((other_real, other_imag))
            backs.append(
                [
                    through(parts, parity, left, right, twiddle, screen)
                    for parity, parts in enumerate((sums, gaps))
                ]
            )
        for side in range(2):
            rows = slice(side * 16, side * 16 + 16)
            for a in range(2):
                add_real, add_imag = 0.0, 0.0
                for (even, odd), (other_real, other_imag) in zip(backs, others):
                    field = even + odd if side == 0 else even - odd
                    b_real, b_imag = other_real[rows], other_imag[rows]
                    real = field[:128, a * 128 : a * 128 + 128].reshape(16, 8, 128)
                    imag = field[128:, a * 128 : a * 128 + 128].reshape(16, 8, 128)
                    add_real += b_real * real - b_imag * imag
                    add_imag += b_real * imag + b_imag * real
                total[rows, 2 * a] += add_real
                total[rows, 2 * a + 1] += add_imag
        return carry

    lax.fori_loop(0, (trips + UNROLL - 1) // UNROLL, turn, 0)

    if second_call:
        energy_sum = jnp.zeros((8, 128), f32)
        for a in range(2):
            flat = lax.rem(chip, 4) * 4 + core * 2 + a
            occupied = jnp.where(lax.rem(flat, 8) < counts[group * 2 + flat // 8], 1.0, 0.0)
            both = own[a, :, :8] * total[:, 2 * a] + own[a, :, 8:] * total[:, 2 * a + 1]
            energy_sum += jnp.sum(both, axis=0) * occupied.astype(f32)
        energy[...] = jnp.full((8, 128), jnp.sum(energy_sum) * (1.0 / (32.0 * 32768.0)), f32)


UNROLL = 2


def exchange(scale, counts, received, partners, left, right, twiddle, held):
    second_call = held is not None
    vmem = pl.BlockSpec(memory_space=pltpu.VMEM)
    operands = [counts, received, partners, left, right, twiddle]
    specs = [pl.BlockSpec(memory_space=pltpu.SMEM)] + [vmem] * 5
    field = jax.ShapeDtypeStruct((32, 4, 8, 128), f32)
    aliases = {}
    if second_call:
        operands.append(held)
        specs.append(vmem)
        aliases = {6: 0}
        out_shape, out_specs = (field, jax.ShapeDtypeStruct((8, 128), f32)), (vmem, vmem)

        def body(*refs):
            exchange_kernel(scale, True, *refs)

    else:
        out_shape, out_specs = field, vmem

        def body(counts, received, partners, left, right, twiddle, total, own, screen):
            exchange_kernel(
                scale, False, counts, received, partners, left, right, twiddle, None, total, None,
                own, screen,
            )

    return pl.pallas_call(
        body,
        out_shape=out_shape,
        in_specs=specs,
        out_specs=out_specs,
        scratch_shapes=[pltpu.VMEM((2, 32, 16, 128), f32), pltpu.VMEM((2, 128, 128), f32)],
        input_output_aliases=aliases,
        compiler_params=pltpu.CompilerParams(vmem_limit_bytes=24 * MIB),
        cost_estimate=pl.CostEstimate(
            flops=4 * 12 * 2 * 512 * 256 * 256, bytes_accessed=4 << 20, transcendentals=0
        ),
        name="exchange_second" if second_call else "exchange_first",
    )(*operands)


def finish_kernel(returned, orbitals, energies, vectors, message):
    fields = returned[0] + returned[1] + returned[2] + returned[3]
    vectors[...] = fields
    fields = fields.reshape(16, 2, 8, 128)
    sums = []
    for k in range(2):
        own = orbitals[k * 8 : k * 8 + 8].astype(f32)
        own_real, own_imag = own[:, None, :8], own[:, None, 8:]
        real = fields[None, k * 8 : k * 8 + 8, 0]
        imag = fields[None, k * 8 : k * 8 + 8, 1]
        for product in (own_real * real + own_imag * imag, own_real * imag - own_imag * real):
            sums.append(jnp.sum(product, axis=2).reshape(64, 128))
    sums = jnp.concatenate(sums, axis=0)
    flat = lax.dot_general(
        jnp.full((8, 128), 1.0 / 32768.0, f32), sums, (((1,), (1,)), ((), ())),
        precision=highest, preferred_element_type=f32,
    )
    total = energies[:1]
    rows = jnp.concatenate((flat[:1, :128], flat[:1, 128:], total, total), axis=0)
    message[...] = jnp.broadcast_to(rows[None], (32, 4, 128))


def finish(returned, orbitals, energies):
    vmem = pl.BlockSpec(memory_space=pltpu.VMEM)
    return pl.pallas_call(
        finish_kernel,
        out_shape=(
            jax.ShapeDtypeStruct((32, 8, 128), f32),
            jax.ShapeDtypeStruct((32, 4, 128), f32),
        ),
        in_specs=[vmem] * 3,
        out_specs=(vmem, vmem),
        compiler_params=pltpu.CompilerParams(vmem_limit_bytes=8 * MIB),
        name="finish",
    )(returned, orbitals, energies)


def on_device(orbitals, band_counts, pair_slot, kernel):
    left, right, twiddle = (jnp.asarray(table) for table in constants())
    groups = lax.axis_size("ka")
    scale = -1.0 / (16.0 * 32768.0)

    orbitals = orbitals.reshape(16, 16, 128)
    before = lax.ppermute(orbitals, "ka", [(i, (i + 1) % groups) for i in range(groups)])
    packed = pack(pair_slot, orbitals, before, kernel.reshape(16, 8, 128))
    received = lax.all_to_all(packed, "ga", 0, 0, tiled=True)
    swapped = lax.ppermute(received[:, :4], "ga", [(i, i ^ 1) for i in range(32)])
    total = exchange(scale, band_counts, received, received, left, right, twiddle, None)
    total, energy = exchange(scale, band_counts, received, swapped, left, right, twiddle, total)

    returned = lax.all_to_all(total, "ga", 0, 0, tiled=True)
    for step in (1, 2, 4):
        energy = energy + lax.ppermute(energy, "ka", [(i, i ^ step) for i in range(groups)])
    vectors, message = finish(returned.reshape(4, 32, 8, 128), orbitals, energy)
    sums = lax.all_to_all(message, "ga", 0, 0, tiled=True).sum(axis=0)
    return (
        vectors.reshape(2, 8, 2, 1, 1024),
        sums[:2].reshape(2, 2, 8, 8),
        sums[2, 0],
    )


def solution(mesh):
    in_specs = (P("ka", None, None, "ga", None), P(), P(), P(None, None, "ga"))
    out_specs = (P("ka", None, None, "ga", None), P("ka", None, None, None), P())
    return jax.shard_map(
        on_device, mesh=mesh, in_specs=in_specs, out_specs=out_specs, check_vma=False
    )
```

time: 129 us -> 103 us (0.80)
  blocking collectives: 10.2 us -> 53.3 us
  waiting for transfers between devices: 49.1 us -> 9.36 us
  Pallas kernels: 23.7 us -> 12.9 us
  local copies, waits for them, and re-layouts: 10 us -> 3.24 us
  other arithmetic: 4.56 us -> 0.05 us
  between operations: 4.91 us -> 0.7 us
  starting transfers between devices: 25.3 us -> 22.6 us
    all_to_all x1 -> x2, blocking collectives: 10.2 us -> 53.3 us  [the longest x1 35.1 us: on_device(): received = lax.all_to_all(packed, 'ga', 0, 0, tiled=True)]
    all_to_all x2 -> x0, waiting for transfers between devices: 30.9 us -> none  [the longest x1 23.7 us: on_device(): received = lax.all_to_all(packed, 'ga', 0, 0, tiled=True)]
    all_to_all x2 -> x0, starting transfers between devices: 17.1 us -> none  [the longest x1 11.6 us: on_device(): received = lax.all_to_all(packed, 'ga', 0, 0, tiled=True)]
    all_to_all x1, waiting for transfers between devices: 16.5 us -> 0.01 us  [on_device(): returned = lax.all_to_all(total, 'ga', 0, 0, tiled=True)]
    ppermute x1 -> x4, starting transfers between devices: 2.11 us -> 15.6 us  [the longest x3 13.5 us: on_device(): lax.ppermute(energy, 'ka', [(i, i ^ step) for i in range(groups)])]
    pallas_call x2 -> x4, Pallas kernels: 23.7 us -> 12.9 us  [the longest x2 11.3 us: exchange(): pl.pallas_call(body, out_shape=out_shape, in_specs=specs, out_specs=out_s...]
    ppermute x1 -> x4, waiting for transfers between devices: 1.73 us -> 9.36 us  [the longest x3 4.87 us: on_device(): lax.ppermute(energy, 'ka', [(i, i ^ step) for i in range(groups)])]
    unnamed x16 -> x10, local copies, waits for them, and re-layouts: 2.84 us -> 0.02 us
  transfers between devices with their start and end apart: 5 -> 6, of which waited for: 4 -> 4; matrix products, arithmetic and copies ran while one was open for 5% -> 1% of each run, Pallas kernels for 9% -> 5%
where the time goes in v2:
time: 103 us; the launch traced here: 102 us
  blocking collectives  53.3 us (52%)
  starting transfers between devices  22.6 us (22%)
  Pallas kernels  12.9 us (13%)
  waiting for transfers between devices  9.36 us (9%)
  local copies, waits for them, and re-layouts  3.24 us (3%)
    all_to_all x1, blocking collectives, on_device(): received = lax.all_to_all(packed, 'ga', 0, 0, tiled=True)  35.1 us
    all_to_all x1, blocking collectives, on_device(): sums = lax.all_to_all(message, 'ga', 0, 0, tiled=True).sum(axis=0)  18.3 us
    ppermute x3, starting transfers between devices, on_device(): lax.ppermute(energy, 'ka', [(i, i ^ step) for i in range(groups)])  13.5 us
    pallas_call x2, Pallas kernels, exchange(): pl.pallas_call(body, out_shape=out_shape, in_specs=specs, out_specs=out_s...  11.3 us
    ppermute x3, waiting for transfers between devices, on_device(): lax.ppermute(energy, 'ka', [(i, i ^ step) for i in range(groups)])  4.87 us
    ppermute x1, waiting for transfers between devices, on_device(): lax.ppermute(orbitals, 'ka', [(i, (i + 1) % groups) for i in range(groups)])  4.49 us
    all_to_all x1, starting transfers between devices, on_device(): returned = lax.all_to_all(total, 'ga', 0, 0, tiled=True)  4.45 us
    ppermute x1, starting transfers between devices, on_device(): lax.ppermute(received[:, :4], 'ga', [(i, i ^ 1) for i in range(32)])  2.47 us
  transfers between devices with their start and end apart: 6, of which 4 were waited for; matrix products, arithmetic and copies ran while one was open for 1% of the time, Pallas kernels for 5%

profile of v2, /device:TPU:1, one launch (start us, length us, event | category | flops | bytes accessed | tf_op | source)
XLA Modules:
  0.0 102.1 jit_solution(4901816213658328103)
XLA Ops:
  0.6 0.9 reshape.21.orbitals
  1.5 0.0 copy-start
  1.5 2.1 %collective-permute-start = (bf16[16,16,128]{2,1,0:T(8,128)(2,1)S(1)}, bf16[16,16,128]{2,1,0:T(8,128)(2,1)S(1)}, u32[]{:S(2)}, u32[]{:S(2)}) collective-permute-start(bf16[16,16,128]{2,1,0:T(8,128)(2,1)S(1)} %reshape.21.orbitals), channel_id=1, source_target_pairs={{0,32},{32,64},{64,96},{96,128},{128,160},{160,192},{192,224},{224... | collective-permute-start | bytes 196616 | tf_op jit(solution)/shard_map/ppermute | solution.py:314
  3.6 1.1 %reshape.22.kernel = f32[16,8,128]{2,1,0:T(8,128)S(1)} reshape(f32[16,32,32]{2,1,0:T(8,128)} %param.10) | data formatting | bytes 131072 | tf_op jit(solution)/shard_map/reshape | solution.py:315
  4.7 4.5 %collective-permute-done.before = bf16[16,16,128]{2,1,0:T(8,128)(2,1)S(1)} collective-permute-done((bf16[16,16,128]{2,1,0:T(8,128)(2,1)S(1)}, bf16[16,16,128]{2,1,0:T(8,128)(2,1)S(1)}, u32[]{:S(2)}, u32[]{:S(2)}) %collective-permute-start) | collective-permute-done | bytes 65568 | tf_op jit(solution)/shard_map/ppermute | solution.py:314
  9.2 0.8 pack.1
  10.0 0.0 copy-start.2
  10.0 35.1 %all_to_all.15.received.partners.refs_1_ = bf16[32,7,16,128]{3,2,1,0:T(8,128)(2,1)S(1)} all-to-all(bf16[32,7,16,128]{3,2,1,0:T(8,128)(2,1)S(1)} %pack.1), channel_id=1, replica_groups=mesh['ka'=8,'ga'=32] {'ga'}, dimensions={0} | all-to-all | bytes 1835008 | tf_op jit(solution)/shard_map/all_to_all | solution.py:316
  45.1 0.1 slice.12
  45.1 2.5 %collective-permute-start.1 = (bf16[32,4,16,128]{3,2,1,0:T(8,128)(2,1)S(1)}, bf16[32,4,16,128]{3,2,1,0:T(8,128)(2,1)S(1)}, u32[]{:S(2)}, u32[]{:S(2)}) collective-permute-start(bf16[32,4,16,128]{3,2,1,0:T(8,128)(2,1)S(1)} %slice.12), channel_id=1, source_target_pairs={{0,1},{1,0},{2,3},{3,2},{4,5},{5,4},{6,7},{7,6},{8,9},{9,8},{10,11... | collective-permute-start | bytes 1572872 | tf_op jit(solution)/shard_map/ppermute | solution.py:317
  47.6 5.4 %exchange_first.1.refs_6_ = f32[32,4,8,128]{3,2,1,0:T(8,128)} custom-call(s32[16]{0:T(128)S(1)} %copy-done.1, bf16[32,7,16,128]{3,2,1,0:T(8,128)(2,1)S(1)} %all_to_all.15.received.partners.refs_1_, bf16[32,7,16,128]{3,2,1,0:T(8,128)(2,1)S(1)} %all_to_all.15.received.partners.refs_1_, bf16[4,256,512]{2,1,0:T(8,128)(2,1)S(1)} %copy-done.2, ...), custom_call_target="tpu_custom_call" | custom-call | flops 3221225472 | bytes 4194304 | tf_op jit(solution)/shard_map/exchange_first/pallas_call | solution.py:256
  53.0 0.0 collective-permute-done.1.refs_2_
  53.0 5.9 %exchange_second.1 = (f32[32,4,8,128]{3,2,1,0:T(8,128)}, f32[8,128]{1,0:T(8,128)S(1)}) custom-call(s32[16]{0:T(128)S(1)} %copy-done.1, bf16[32,7,16,128]{3,2,1,0:T(8,128)(2,1)S(1)} %all_to_all.15.received.partners.refs_1_, bf16[32,4,16,128]{3,2,1,0:T(8,128)(2,1)S(1)} %collective-permute-done.1.refs_2_, ...), custom_call_target="tpu_custom_call", output_to_operand_aliasing={{0}: (6, {})} | custom-call | flops 3221225472 | bytes 4194304 | tf_op jit(solution)/shard_map/exchange_second/pallas_call | solution.py:256
  58.9 4.4 %all-to-all-start.1 = ((f32[32,4,8,128]{3,2,1,0:T(8,128)}), f32[32,4,8,128]{3,2,1,0:T(8,128)S(1)}, u32[]{:S(2)}, u32[]{:S(2)}) async-start(f32[32,4,8,128]{3,2,1,0:T(8,128)} %get-tuple-element.7), calls=%async_computation.1 | async-start | bytes 1048576 | tf_op jit(solution)/shard_map/all_to_all | solution.py:321
  63.4 0.1 collective-permute-start.2
  63.5 2.7 %collective-permute-done.2 = f32[8,128]{1,0:T(8,128)S(1)} collective-permute-done((f32[8,128]{1,0:T(8,128)S(1)}, f32[8,128]{1,0:T(8,128)S(1)}, u32[]{:S(2)}, u32[]{:S(2)}) %collective-permute-start.2) | collective-permute-done | bytes 4128 | tf_op jit(solution)/shard_map/ppermute | solution.py:323
  66.2 5.9 %collective-permute-start.3 = (f32[8,128]{1,0:T(8,128)S(1)}, f32[8,128]{1,0:T(8,128)S(1)}, u32[]{:S(2)}, u32[]{:S(2)}) collective-permute-start(f32[8,128]{1,0:T(8,128)S(1)} %add.9), channel_id=1, source_target_pairs={{0,64},{32,96},{64,0},{96,32},{128,192},{160,224},{192,128},{224,1... | collective-permute-start | bytes 12296 | tf_op jit(solution)/shard_map/ppermute | solution.py:323
  72.1 1.1 %collective-permute-done.3 = f32[8,128]{1,0:T(8,128)S(1)} collective-permute-done((f32[8,128]{1,0:T(8,128)S(1)}, f32[8,128]{1,0:T(8,128)S(1)}, u32[]{:S(2)}, u32[]{:S(2)}) %collective-permute-start.3) | collective-permute-done | bytes 4128 | tf_op jit(solution)/shard_map/ppermute | solution.py:323
  73.3 7.5 %collective-permute-start.4 = (f32[8,128]{1,0:T(8,128)S(1)}, f32[8,128]{1,0:T(8,128)S(1)}, u32[]{:S(2)}, u32[]{:S(2)}) collective-permute-start(f32[8,128]{1,0:T(8,128)S(1)} %add.10), channel_id=1, source_target_pairs={{0,128},{32,160},{64,192},{96,224},{128,0},{160,32},{192,64},{224,... | collective-permute-start | bytes 12296 | tf_op jit(solution)/shard_map/ppermute | solution.py:323
  80.8 1.0 collective-permute-done.4
  81.8 0.8 finish.1
  82.6 18.3 %all_to_all.16 = f32[32,4,128]{2,1,0:T(4,128)S(1)} all-to-all(f32[32,4,128]{2,1,0:T(4,128)S(1)} %get-tuple-element.10), channel_id=1, replica_groups=mesh['ka'=8,'ga'=32] {'ga'}, dimensions={0} | all-to-all | bytes 131072 | tf_op jit(solution)/shard_map/all_to_all | solution.py:325
  100.9 0.5 slice.11
  101.4 0.7 reshape.25
  (14 shorter events, 0.1 us)
Async XLA Ops:
  1.5 7.7 %copy-start = (s32[16,16]{1,0:T(8,128)S(1)}, s32[16,16]{1,0:T(8,128)}, u32[]{:S(2)}) copy-start(s32[16,16]{1,0:T(8,128)} %pair_slot.1) | copy-start | bytes 3076
  1.5 7.7 %collective-permute-start = (bf16[16,16,128]{2,1,0:T(8,128)(2,1)S(1)}, bf16[16,16,128]{2,1,0:T(8,128)(2,1)S(1)}, u32[]{:S(2)}, u32[]{:S(2)}) collective-permute-start(bf16[16,16,128]{2,1,0:T(8,128)(2,1)S(1)} %reshape.21.orbitals), channel_id=1, source_target_pairs={{0,32},{32,64},{64,96},{96,128},{128,160},{160,192},{192,224},{224... | collective-permute-start | bytes 196616 | tf_op jit(solution)/shard_map/ppermute | solution.py:314
  10.0 37.6 %copy-start.2 = (bf16[4,256,512]{2,1,0:T(8,128)(2,1)S(1)}, bf16[4,256,512]{2,1,0:T(8,128)(2,1)}, u32[]{:S(2)}) copy-start(bf16[4,256,512]{2,1,0:T(8,128)(2,1)} %constant.8.clone.left.refs_3_) | copy-start | bytes 3145732
  45.1 2.5 %copy-start.1 = (s32[16]{0:T(128)S(1)}, s32[16]{0:T(128)}, u32[]{:S(2)}) copy-start(s32[16]{0:T(128)} %refs_0_.1) | copy-start | bytes 196
  45.1 2.5 %copy-start.3 = (bf16[2,512,256]{2,1,0:T(8,128)(2,1)S(1)}, bf16[2,512,256]{2,1,0:T(8,128)(2,1)}, u32[]{:S(2)}) copy-start(bf16[2,512,256]{2,1,0:T(8,128)(2,1)} %constant.9.clone.right.refs_4_) | copy-start | bytes 1572868
  45.1 2.5 %copy-start.4 = (f32[2,128,128]{2,1,0:T(8,128)S(1)}, f32[2,128,128]{2,1,0:T(8,128)}, u32[]{:S(2)}) copy-start(f32[2,128,128]{2,1,0:T(8,128)} %constant.10.clone.twiddle.refs_5_) | copy-start | bytes 393220
  45.1 7.8 %collective-permute-start.1 = (bf16[32,4,16,128]{3,2,1,0:T(8,128)(2,1)S(1)}, bf16[32,4,16,128]{3,2,1,0:T(8,128)(2,1)S(1)}, u32[]{:S(2)}, u32[]{:S(2)}) collective-permute-start(bf16[32,4,16,128]{3,2,1,0:T(8,128)(2,1)S(1)} %slice.12), channel_id=1, source_target_pairs={{0,1},{1,0},{2,3},{3,2},{4,5},{5,4},{6,7},{7,6},{8,9},{9,8},{10,11... | collective-permute-start | bytes 1572872 | tf_op jit(solution)/shard_map/ppermute | solution.py:317
  58.9 22.9 %all-to-all-start.1 = ((f32[32,4,8,128]{3,2,1,0:T(8,128)}), f32[32,4,8,128]{3,2,1,0:T(8,128)S(1)}, u32[]{:S(2)}, u32[]{:S(2)}) async-start(f32[32,4,8,128]{3,2,1,0:T(8,128)} %get-tuple-element.7), calls=%async_computation.1 | async-start | bytes 1048576 | tf_op jit(solution)/shard_map/all_to_all | solution.py:321
  63.4 2.8 %collective-permute-start.2 = (f32[8,128]{1,0:T(8,128)S(1)}, f32[8,128]{1,0:T(8,128)S(1)}, u32[]{:S(2)}, u32[]{:S(2)}) collective-permute-start(f32[8,128]{1,0:T(8,128)S(1)} %get-tuple-element.8), channel_id=1, source_target_pairs={{0,32},{32,0},{64,96},{96,64},{128,160},{160,128},{192,224},{224,1... | collective-permute-start | bytes 12296 | tf_op jit(solution)/shard_map/ppermute | solution.py:323
  66.2 7.1 %collective-permute-start.3 = (f32[8,128]{1,0:T(8,128)S(1)}, f32[8,128]{1,0:T(8,128)S(1)}, u32[]{:S(2)}, u32[]{:S(2)}) collective-permute-start(f32[8,128]{1,0:T(8,128)S(1)} %add.9), channel_id=1, source_target_pairs={{0,64},{32,96},{64,0},{96,32},{128,192},{160,224},{192,128},{224,1... | collective-permute-start | bytes 12296 | tf_op jit(solution)/shard_map/ppermute | solution.py:323
  73.3 8.5 %collective-permute-start.4 = (f32[8,128]{1,0:T(8,128)S(1)}, f32[8,128]{1,0:T(8,128)S(1)}, u32[]{:S(2)}, u32[]{:S(2)}) collective-permute-start(f32[8,128]{1,0:T(8,128)S(1)} %add.10), channel_id=1, source_target_pairs={{0,128},{32,160},{64,192},{96,224},{128,0},{160,32},{192,64},{224,... | collective-permute-start | bytes 12296 | tf_op jit(solution)/shard_map/ppermute | solution.py:323

commit v3 on v2

v3 whole, which is shorter than its diff:
```python
import functools

import numpy as np
import jax
import jax.numpy as jnp
from jax import lax
from jax.experimental import pallas as pl
from jax.experimental.pallas import tpu as pltpu
from jax.sharding import PartitionSpec as P

highest = lax.Precision.HIGHEST
f32 = jnp.float32
bf16 = jnp.bfloat16


def embed(matrix):
    return np.block([[matrix.real, -matrix.imag], [matrix.imag, matrix.real]])


def split(matrix):
    high = matrix.astype(np.float32).astype(bf16)
    low = (matrix - high.astype(np.float64)).astype(np.float32).astype(bf16)
    return high, low


def constants():
    rows = np.arange(128)
    x_at, yh_at = rows // 8, rows % 8
    jj_at, glo_at, gxh_at = rows // 64, rows // 8 % 8, rows % 8
    forward, inverse = [], []
    for parity in range(2):
        gx_at = 4 * gxh_at + 2 * jj_at + parity
        phase = gx_at[:, None] * x_at[None, :] / 32.0 + glo_at[:, None] * yh_at[None, :] / 8.0
        real = embed(np.exp(-2j * np.pi * phase))
        for held, matrix in ((forward, real), (inverse, real.T)):
            high, low = split(matrix)
            held.append(np.concatenate((high, low), axis=1))
    lanes = np.arange(128)
    first, last = lanes // 32, lanes % 32
    phase = first[:, None] * first[None, :] / 4.0 + last[:, None] * last[None, :] / 32.0
    real = embed(np.exp(-2j * np.pi * phase)).T
    right = []
    for matrix in (real, real.T):
        high, low = split(matrix)
        right.append(np.concatenate((high, low), axis=0))
    turn = 2.0 * np.pi * (glo_at[:, None] * first[None, :]) / 32.0
    twiddle = np.stack((np.cos(turn), np.sin(turn))).astype(np.float32)
    return np.stack(forward + inverse), np.stack(right), twiddle


def two_terms(value):
    high = value.astype(bf16)
    low = (value - high.astype(f32)).astype(bf16)
    return high, low


MIB = 1 << 20


def place():
    member = lax.axis_index("ga")
    return lax.axis_index("ka"), member // 16, member // 4 % 4, member // 2 % 2, member % 2


def pack_kernel(pair_slot, orbitals, before, kernel, packed):
    group = lax.axis_index("ka")
    partner_group = lax.rem(group + 7, 8)
    for k2 in range(4):
        source = orbitals if k2 < 2 else before
        second = (group if k2 < 2 else partner_group) * 2 + k2 % 2
        for k in range(2):
            slot = pair_slot[group * 2 + k, second]
            block = kernel[slot]
            high = block.astype(bf16)
            low = (block - high.astype(f32)).astype(bf16)
            unit = jnp.concatenate((high, low), axis=0)
            for quarter in range(4):
                to = quarter // 2 * 16 + k2 * 4 + k * 2 + quarter % 2
                for j in range(2):
                    packed[to, j] = source[k2 % 2 * 8 + quarter * 2 + j]
                    packed[to, 2 + j] = orbitals[k * 8 + quarter * 2 + j]
                packed[to, 4] = unit


def pack(pair_slot, orbitals, before, kernel):
    vmem = pl.BlockSpec(memory_space=pltpu.VMEM)
    return pl.pallas_call(
        pack_kernel,
        out_shape=jax.ShapeDtypeStruct((32, 5, 16, 128), bf16),
        in_specs=[pl.BlockSpec(memory_space=pltpu.SMEM), vmem, vmem, vmem],
        out_specs=vmem,
        compiler_params=pltpu.CompilerParams(vmem_limit_bytes=4 * MIB),
        name="pack",
    )(pair_slot, orbitals, before, kernel)


def screen_of(received, scale, screen):
    raw = received[:, 4].astype(f32)
    raw = (raw[:, :8] + raw[:, 8:]) * scale
    raw = raw.reshape(4, 64, 128)
    lane_group = lax.broadcasted_iota(jnp.int32, (64, 128), 1) // 32
    for j in range(4):
        placed = jnp.zeros((64, 128), f32)
        for i in range(4):
            shift = (i - j) % 4 * 32
            moved = pltpu.roll(raw[i], shift, 1) if shift else raw[i]
            placed = jnp.where(lane_group == i, moved, placed)
        screen[j % 2, (j // 2) * 64 : (j // 2) * 64 + 64] = placed


def thrice(table, axis):
    size = table.shape[axis] // 2
    return jnp.concatenate((table, lax.slice_in_dim(table, 0, size, axis=axis)), axis=axis)


def enter(parts, table):
    stacked = jnp.concatenate([jnp.concatenate(parts[part], axis=1) for part in range(2)], axis=0)
    high, low = two_terms(stacked)
    return jnp.dot(
        thrice(table, 1), jnp.concatenate((high, high, low), axis=0), preferred_element_type=f32
    )


def across(turned, table, cosine, sine):
    lines = []
    for a in range(2):
        real = turned[:128, a * 128 : a * 128 + 128]
        imag = turned[128:, a * 128 : a * 128 + 128]
        lines.append(
            jnp.concatenate((real * cosine + imag * sine, imag * cosine - real * sine), axis=1)
        )
    high, low = two_terms(jnp.concatenate(lines, axis=0))
    return jnp.dot(
        jnp.concatenate((high, high, low), axis=1), thrice(table, 0), preferred_element_type=f32
    )


def screened(spectra, factor, table):
    factor = jnp.concatenate((factor, factor), axis=1)
    factor = jnp.concatenate((factor, factor), axis=0)
    high, low = two_terms(spectra * factor)
    return jnp.dot(
        jnp.concatenate((high, high, low), axis=1), thrice(table, 0), preferred_element_type=f32
    )


def leave(lines, table, cosine, sine):
    reals, imags = [], []
    for a in range(2):
        real = lines[a * 128 : a * 128 + 128, :128]
        imag = lines[a * 128 : a * 128 + 128, 128:]
        reals.append(real * cosine - imag * sine)
        imags.append(imag * cosine + real * sine)
    stacked = jnp.concatenate(
        (jnp.concatenate(reals, axis=1), jnp.concatenate(imags, axis=1)), axis=0
    )
    high, low = two_terms(stacked)
    return jnp.dot(
        thrice(table, 1), jnp.concatenate((high, high, low), axis=0), preferred_element_type=f32
    )


def exchange_kernel(scale, call, counts, received, partners, left, right, twiddle, *rest):
    if call == 0:
        total, screen = rest
        screen_of(received, scale, screen)
        held = None
    elif call < 3:
        screen, held, total = rest
    else:
        screen, held, total, energy = rest
    group, y_at, k2, k, core = place()
    k2_at = lax.rem(group + 8 - k2 // 2, 8) * 2 + k2 % 2
    quarter = (1 - y_at if call >= 2 else y_at) * 2 + (1 - core if call % 2 else core)
    occupied_here = counts[k2_at] - 2 * quarter

    @pl.when(occupied_here > 0)
    def _():
        second_kept = jnp.where(occupied_here > 1, 1.0, 0.0).astype(f32)
        others, chains = [], []
        for half in range(2):
            other = partners[:, half].astype(f32)
            if half:
                other = other * second_kept
            other_real, other_imag = other[:, :8], other[:, 8:]
            sums, gaps = [[], []], [[], []]
            for a in range(2):
                own = received[:, 2 + a].astype(f32)
                own_real, own_imag = own[:, :8], own[:, 8:]
                density = (
                    own_real * other_real + own_imag * other_imag,
                    own_imag * other_real - own_real * other_imag,
                )
                for part in range(2):
                    low, high = density[part][:16], density[part][16:]
                    sums[part].append((low + high).reshape(128, 128))
                    gaps[part].append((low - high).reshape(128, 128))
            others.append((other_real, other_imag))
            chains += [(0, sums), (1, gaps)]
        cosine, sine = twiddle[0], twiddle[1]
        values = [enter(parts, left[parity]) for parity, parts in chains]
        values = [across(value, right[0], cosine, sine) for value in values]
        values = [
            screened(value, screen[parity], right[1])
            for value, (parity, parts) in zip(values, chains)
        ]
        values = [
            leave(value, left[2 + parity], cosine, sine)
            for value, (parity, parts) in zip(values, chains)
        ]
        backs = [values[2 * half : 2 * half + 2] for half in range(2)]
        for side in range(2):
            rows = slice(side * 16, side * 16 + 16)
            for a in range(2):
                add_real, add_imag = 0.0, 0.0
                if held is not None:
                    add_real, add_imag = held[rows, 2 * a], held[rows, 2 * a + 1]
                for (even, odd), (other_real, other_imag) in zip(backs, others):
                    field = even + odd if side == 0 else even - odd
                    b_real, b_imag = other_real[rows], other_imag[rows]
                    real = field[:128, a * 128 : a * 128 + 128].reshape(16, 8, 128)
                    imag = field[128:, a * 128 : a * 128 + 128].reshape(16, 8, 128)
                    add_real += b_real * real - b_imag * imag
                    add_imag += b_real * imag + b_imag * real
                total[rows, 2 * a] = add_real
                total[rows, 2 * a + 1] = add_imag

    @pl.when(occupied_here <= 0)
    def _():
        total[...] = jnp.zeros_like(total) if held is None else held[...]

    if call == 3:
        energy_sum = jnp.zeros((8, 128), f32)
        for a in range(2):
            band = y_at * 4 + core * 2 + a
            occupied = jnp.where(band < counts[group * 2 + k], 1.0, 0.0).astype(f32)
            own = received[:, 2 + a].astype(f32)
            both = own[:, :8] * total[:, 2 * a] + own[:, 8:] * total[:, 2 * a + 1]
            energy_sum += jnp.sum(both, axis=0) * occupied
        energy[...] = jnp.full((8, 128), jnp.sum(energy_sum) * (1.0 / (32.0 * 32768.0)), f32)


def exchange(scale, call, counts, received, partners, left, right, twiddle, *carried):
    vmem = pl.BlockSpec(memory_space=pltpu.VMEM)
    operands = (counts, received, partners, left, right, twiddle, *carried)
    shapes = [jax.ShapeDtypeStruct((32, 4, 8, 128), f32)]
    if call == 0:
        shapes.append(jax.ShapeDtypeStruct((2, 128, 128), f32))
    if call == 3:
        shapes.append(jax.ShapeDtypeStruct((8, 128), f32))
    return pl.pallas_call(
        functools.partial(exchange_kernel, scale, call),
        out_shape=tuple(shapes),
        in_specs=[pl.BlockSpec(memory_space=pltpu.SMEM)] + [vmem] * (len(operands) - 1),
        out_specs=(vmem,) * len(shapes),
        compiler_params=pltpu.CompilerParams(vmem_limit_bytes=24 * MIB),
        cost_estimate=pl.CostEstimate(
            flops=2 * 12 * 2 * 512 * 256 * 256, bytes_accessed=4 << 20, transcendentals=0
        ),
        name=("exchange_0", "exchange_1", "exchange_2", "exchange_3")[call],
    )(*operands)


def finish_kernel(returned, orbitals, energies, vectors, message):
    fields = []
    for k in range(2):
        for y_at in range(2):
            fields.append(sum(returned[y_at, k2, k] for k2 in range(4)))
    fields = jnp.concatenate(fields, axis=0)
    vectors[...] = fields
    fields = fields.reshape(16, 2, 8, 128)
    sums = []
    for k in range(2):
        own = orbitals[k * 8 : k * 8 + 8].astype(f32)
        own_real, own_imag = own[:, None, :8], own[:, None, 8:]
        real = fields[None, k * 8 : k * 8 + 8, 0]
        imag = fields[None, k * 8 : k * 8 + 8, 1]
        for product in (own_real * real + own_imag * imag, own_real * imag - own_imag * real):
            sums.append(jnp.sum(product, axis=2).reshape(64, 128))
    sums = jnp.concatenate(sums, axis=0)
    flat = lax.dot_general(
        jnp.full((8, 128), 1.0 / 32768.0, f32), sums, (((1,), (1,)), ((), ())),
        precision=highest, preferred_element_type=f32,
    )
    total = energies[:1]
    rows = jnp.concatenate((flat[:1, :128], flat[:1, 128:], total, total), axis=0)
    message[...] = jnp.broadcast_to(rows[None], (32, 4, 128))


def finish(returned, orbitals, energies):
    vmem = pl.BlockSpec(memory_space=pltpu.VMEM)
    return pl.pallas_call(
        finish_kernel,
        out_shape=(
            jax.ShapeDtypeStruct((32, 8, 128), f32),
            jax.ShapeDtypeStruct((32, 4, 128), f32),
        ),
        in_specs=[vmem] * 3,
        out_specs=(vmem, vmem),
        compiler_params=pltpu.CompilerParams(vmem_limit_bytes=8 * MIB),
        name="finish",
    )(returned, orbitals, energies)


def close_kernel(messages, matrix, energy):
    total = jnp.sum(messages[...], axis=0)
    lane = lax.broadcasted_iota(jnp.int32, (32, 128), 1)
    row = lax.broadcasted_iota(jnp.int32, (32, 128), 0)
    spread = jnp.concatenate(
        [jnp.broadcast_to(total[k : k + 1], (16, 128)) for k in range(2)], axis=0
    )
    spread = jnp.where(lane // 8 == row % 16, spread, 0.0)
    gather = jnp.where(
        lax.broadcasted_iota(jnp.int32, (128, 128), 0) % 8
        == lax.broadcasted_iota(jnp.int32, (128, 128), 1),
        1.0,
        0.0,
    )
    spread = jnp.dot(spread, gather, precision=highest, preferred_element_type=f32)
    for k in range(2):
        for part in range(2):
            first = k * 16 + part * 8
            matrix[k, part] = spread[first : first + 8, :8]
    energy[...] = total[2:3, :1]


def close(messages):
    vmem = pl.BlockSpec(memory_space=pltpu.VMEM)
    return pl.pallas_call(
        close_kernel,
        out_shape=(jax.ShapeDtypeStruct((2, 2, 8, 8), f32), jax.ShapeDtypeStruct((1, 1), f32)),
        in_specs=[vmem],
        out_specs=(vmem, vmem),
        compiler_params=pltpu.CompilerParams(vmem_limit_bytes=4 * MIB),
        name="close",
    )(messages)


def on_device(orbitals, band_counts, pair_slot, kernel):
    left, right, twiddle = (jnp.asarray(table) for table in constants())
    groups = lax.axis_size("ka")
    scale = -1.0 / (16.0 * 32768.0)

    orbitals = orbitals.reshape(16, 16, 128)
    before = lax.ppermute(orbitals, "ka", [(i, (i + 1) % groups) for i in range(groups)])
    packed = pack(pair_slot, orbitals, before, kernel.reshape(16, 8, 128))
    received = lax.all_to_all(packed, "ga", 0, 0, tiled=True)

    def shown(value, bit):
        return lax.ppermute(value, "ga", [(i, i ^ bit) for i in range(32)])

    mine = received[:, :2]
    next_y = shown(mine, 16)
    next_core = shown(mine, 1)
    tables = (left, right, twiddle)
    total, screen = exchange(scale, 0, band_counts, received, received, *tables)
    (total,) = exchange(scale, 1, band_counts, received, next_core, *tables, screen, total)
    next_y, total = lax.optimization_barrier((next_y, total))
    next_both = shown(next_y, 1)
    (total,) = exchange(scale, 2, band_counts, received, next_y, *tables, screen, total)
    total, energy = exchange(scale, 3, band_counts, received, next_both, *tables, screen, total)

    returned = lax.all_to_all(total, "ga", 0, 0, tiled=True)
    for bit in (1, 2, 4):
        energy = energy + lax.ppermute(energy, "ka", [(i, i ^ bit) for i in range(groups)])
    vectors, message = finish(returned.reshape(2, 4, 2, 8, 8, 128), orbitals, energy)
    matrix, energy = close(lax.all_to_all(message, "ga", 0, 0, tiled=True))
    return (vectors.reshape(2, 8, 2, 1, 1024), matrix, energy[0, 0])


def solution(mesh):
    in_specs = (P("ka", None, None, "ga", None), P(), P(), P(None, None, "ga"))
    out_specs = (P("ka", None, None, "ga", None), P("ka", None, None, None), P())
    return jax.shard_map(
        on_device, mesh=mesh, in_specs=in_specs, out_specs=out_specs, check_vma=False
    )
```

time: 103 us -> 92.6 us (0.90)
  waiting for transfers between devices: 9.36 us -> 20.5 us
  blocking collectives: 53.3 us -> 43.8 us
  starting transfers between devices: 22.6 us -> 15.2 us
  Pallas kernels: 12.9 us -> 9.98 us
  local copies, waits for them, and re-layouts: 3.24 us -> 1.99 us
    ppermute x4 -> x6, starting transfers between devices: 16 us -> 6.36 us  [the longest x3 3.64 us: shown(): return lax.ppermute(value, 'ga', [(i, i ^ bit) for i in range(32)])]
    ppermute x4 -> x6, waiting for transfers between devices: 4.88 us -> 10.8 us  [the longest x3 8.63 us: on_device(): lax.ppermute(energy, 'ka', [(i, i ^ bit) for i in range(groups)])]
    all_to_all x1, waiting for transfers between devices: 0.01 us -> 5.21 us  [on_device(): returned = lax.all_to_all(total, 'ga', 0, 0, tiled=True)]
    all_to_all x1, blocking collectives: 35.1 us -> 30.3 us  [on_device(): received = lax.all_to_all(packed, 'ga', 0, 0, tiled=True)]
    all_to_all x1, blocking collectives: 18.3 us -> 13.5 us  [on_device(): matrix, energy = close(lax.all_to_all(message, 'ga', 0, 0, tiled=True))]
    pallas_call x3 -> x6, Pallas kernels: 12 us -> 9.15 us  [the longest x4 7.6 us: exchange(): pl.pallas_call(functools.partial(exchange_kernel, scale, call), out_shape...]
    all_to_all x1, starting transfers between devices: 4.45 us -> 6.75 us  [on_device(): returned = lax.all_to_all(total, 'ga', 0, 0, tiled=True)]
  transfers between devices with their start and end apart: 6 -> 8, of which waited for: 4 -> 7; matrix products, arithmetic and copies ran while one was open for 1% -> 1% of each run, Pallas kernels for 5% -> 7%
where the time goes in v3:
time: 92.6 us; the launch traced here: 92.2 us
  blocking collectives  43.8 us (47%)
  waiting for transfers between devices  20.5 us (22%)
  starting transfers between devices  15.2 us (16%)
  Pallas kernels  9.98 us (11%)
  local copies, waits for them, and re-layouts  1.99 us (2%)
    all_to_all x1, blocking collectives, on_device(): received = lax.all_to_all(packed, 'ga', 0, 0, tiled=True)  30.3 us
    all_to_all x1, blocking collectives, on_device(): matrix, energy = close(lax.all_to_all(message, 'ga', 0, 0, tiled=True))  13.5 us
    ppermute x3, waiting for transfers between devices, on_device(): lax.ppermute(energy, 'ka', [(i, i ^ bit) for i in range(groups)])  8.63 us
    pallas_call x4, Pallas kernels, exchange(): pl.pallas_call(functools.partial(exchange_kernel, scale, call), out_shape...  7.6 us
    all_to_all x1, starting transfers between devices, on_device(): returned = lax.all_to_all(total, 'ga', 0, 0, tiled=True)  6.75 us
    all_to_all x1, waiting for transfers between devices, on_device(): returned = lax.all_to_all(total, 'ga', 0, 0, tiled=True)  5.21 us
    ppermute x1, waiting for transfers between devices, on_device(): lax.ppermute(orbitals, 'ka', [(i, (i + 1) % groups) for i in range(groups)])  4.49 us
    ppermute x3, starting transfers between devices, shown(): return lax.ppermute(value, 'ga', [(i, i ^ bit) for i in range(32)])  3.64 us
  transfers between devices with their start and end apart: 8, of which 7 were waited for; matrix products, arithmetic and copies ran while one was open for 1% of the time, Pallas kernels for 7%

profile of v3, /device:TPU:1, one launch (start us, length us, event | category | flops | bytes accessed | tf_op | source)
XLA Modules:
  0.0 92.2 jit_solution(638974187598920679)
XLA Ops:
  0.6 0.9 reshape.18.orbitals
  1.5 2.1 %collective-permute-start = (bf16[16,16,128]{2,1,0:T(8,128)(2,1)S(1)}, bf16[16,16,128]{2,1,0:T(8,128)(2,1)S(1)}, u32[]{:S(2)}, u32[]{:S(2)}) collective-permute-start(bf16[16,16,128]{2,1,0:T(8,128)(2,1)S(1)} %reshape.18.orbitals), channel_id=1, source_target_pairs={{0,32},{32,64},{64,96},{96,128},{128,160},{160,192},{192,224},{224... | collective-permute-start | bytes 196616 | tf_op jit(solution)/shard_map/ppermute | solution.py:345
  3.6 1.1 %reshape.19.kernel = f32[16,8,128]{2,1,0:T(8,128)S(1)} reshape(f32[16,32,32]{2,1,0:T(8,128)} %param.10) | data formatting | bytes 131072 | tf_op jit(solution)/shard_map/reshape | solution.py:346
  4.7 4.5 %collective-permute-done.before = bf16[16,16,128]{2,1,0:T(8,128)(2,1)S(1)} collective-permute-done((bf16[16,16,128]{2,1,0:T(8,128)(2,1)S(1)}, bf16[16,16,128]{2,1,0:T(8,128)(2,1)S(1)}, u32[]{:S(2)}, u32[]{:S(2)}) %collective-permute-start) | collective-permute-done | bytes 65568 | tf_op jit(solution)/shard_map/ppermute | solution.py:345
  9.2 0.7 pack.1
  10.0 30.3 %all_to_all.15.received.partners = bf16[32,5,16,128]{3,2,1,0:T(8,128)(2,1)S(1)} all-to-all(bf16[32,5,16,128]{3,2,1,0:T(8,128)(2,1)S(1)} %pack.1), channel_id=1, replica_groups=mesh['ka'=8,'ga'=32] {'ga'}, dimensions={0} | all-to-all | bytes 1310720 | tf_op jit(solution)/shard_map/all_to_all | solution.py:347
  40.3 2.1 %collective-permute-start.2 = (bf16[32,2,16,128]{3,2,1,0:T(8,128)(2,1)S(1)}, bf16[32,2,16,128]{3,2,1,0:T(8,128)(2,1)S(1)}, u32[]{:S(2)}, u32[]{:S(2)}) collective-permute-start(bf16[32,2,16,128]{3,2,1,0:T(8,128)(2,1)S(1)} %slice.4), channel_id=1, source_target_pairs={{0,1},{1,0},{2,3},{3,2},{4,5},{5,4},{6,7},{7,6},{8,9},{9,8},{10,11... | collective-permute-start | bytes 786440 | tf_op jit(solution)/shard_map/ppermute | solution.py:350
  42.4 0.6 collective-permute-start.1
  43.0 2.9 %exchange_0.1 = (f32[32,4,8,128]{3,2,1,0:T(8,128)S(1)}, f32[2,128,128]{2,1,0:T(8,128)S(1)}) custom-call(s32[16]{0:T(128)S(1)} %copy-done.1, bf16[32,5,16,128]{3,2,1,0:T(8,128)(2,1)S(1)} %all_to_all.15.received.partners, bf16[32,5,16,128]{3,2,1,0:T(8,128)(2,1)S(1)} %all_to_all.15.received.partners, bf16[4,256,512]{2,1,0:T(8,128)(2,1)S(1)} %copy-done.2, ...), custom_call_target="tpu_custom_call" | custom-call | flops 1610612736 | bytes 4194304 | tf_op jit(solution)/shard_map/exchange_0/pallas_call | solution.py:251
  45.9 2.7 %exchange_1.1.rest_1_ = f32[32,4,8,128]{3,2,1,0:T(8,128)S(1)} custom-call(s32[16]{0:T(128)S(1)} %copy-done.1, bf16[32,5,16,128]{3,2,1,0:T(8,128)(2,1)S(1)} %all_to_all.15.received.partners, bf16[32,2,16,128]{3,2,1,0:T(8,128)(2,1)S(1)} %collective-permute-done.2.partners, bf16[4,256,512]{2,1,0:T(8,128)(2,1)S(1)} %copy-done.2, ...), custom_call_target="tpu_custom_call" | custom-call | flops 1610612736 | bytes 4194304 | tf_op jit(solution)/shard_map/exchange_1/pallas_call | solution.py:251
  48.6 1.6 %collective-permute-done.1.partners = bf16[32,2,16,128]{3,2,1,0:T(8,128)(2,1)S(1)} collective-permute-done((bf16[32,2,16,128]{3,2,1,0:T(8,128)(2,1)S(1)}, bf16[32,2,16,128]{3,2,1,0:T(8,128)(2,1)S(1)}, u32[]{:S(2)}, u32[]{:S(2)}) %collective-permute-start.1) | collective-permute-done | bytes 262176 | tf_op jit(solution)/shard_map/ppermute | solution.py:350
  50.2 1.0 %collective-permute-start.3 = (bf16[32,2,16,128]{3,2,1,0:T(8,128)(2,1)S(1)}, bf16[32,2,16,128]{3,2,1,0:T(8,128)(2,1)S(1)}, u32[]{:S(2)}, u32[]{:S(2)}) collective-permute-start(bf16[32,2,16,128]{3,2,1,0:T(8,128)(2,1)S(1)} %collective-permute-done.1.partners), channel_id=1, source_target_pairs={{0,1},{1,0},{2,3},{3,2},{4,5},{5,4},{6,7},{7,6},{8,9},{9,8},{10,11... | collective-permute-start | bytes 786440 | tf_op jit(solution)/shard_map/ppermute | solution.py:350
  51.1 0.6 exchange_2.1.rest_1_
  51.8 0.5 collective-permute-done.3.partners
  52.3 1.4 %exchange_3.1 = (f32[32,4,8,128]{3,2,1,0:T(8,128)}, f32[8,128]{1,0:T(8,128)S(1)}) custom-call(s32[16]{0:T(128)S(1)} %copy-done.1, bf16[32,5,16,128]{3,2,1,0:T(8,128)(2,1)S(1)} %all_to_all.15.received.partners, bf16[32,2,16,128]{3,2,1,0:T(8,128)(2,1)S(1)} %collective-permute-done.3.partners, bf16[4,256,512]{2,1,0:T(8,128)(2,1)S(1)} %copy-done.2, ...), custom_call_target="tpu_custom_call" | custom-call | flops 1610612736 | bytes 4194304 | tf_op jit(solution)/shard_map/exchange_3/pallas_call | solution.py:251
  53.7 6.7 %all-to-all-start.1 = ((f32[32,4,8,128]{3,2,1,0:T(8,128)}), f32[32,4,8,128]{3,2,1,0:T(8,128)S(1)}, u32[]{:S(2)}, u32[]{:S(2)}) async-start(f32[32,4,8,128]{3,2,1,0:T(8,128)} %get-tuple-element.17), calls=%async_computation.1 | async-start | bytes 1048576 | tf_op jit(solution)/shard_map/all_to_all | solution.py:363
  60.6 2.7 %collective-permute-done.4 = f32[8,128]{1,0:T(8,128)S(1)} collective-permute-done((f32[8,128]{1,0:T(8,128)S(1)}, f32[8,128]{1,0:T(8,128)S(1)}, u32[]{:S(2)}, u32[]{:S(2)}) %collective-permute-start.4) | collective-permute-done | bytes 4128 | tf_op jit(solution)/shard_map/ppermute | solution.py:365
  63.3 4.3 %collective-permute-done.5 = f32[8,128]{1,0:T(8,128)S(1)} collective-permute-done((f32[8,128]{1,0:T(8,128)S(1)}, f32[8,128]{1,0:T(8,128)S(1)}, u32[]{:S(2)}, u32[]{:S(2)}) %collective-permute-start.5) | collective-permute-done | bytes 4128 | tf_op jit(solution)/shard_map/ppermute | solution.py:365
  67.6 2.6 %collective-permute-start.6 = (f32[8,128]{1,0:T(8,128)S(1)}, f32[8,128]{1,0:T(8,128)S(1)}, u32[]{:S(2)}, u32[]{:S(2)}) collective-permute-start(f32[8,128]{1,0:T(8,128)S(1)} %add.10), channel_id=1, source_target_pairs={{0,128},{32,160},{64,192},{96,224},{128,0},{160,32},{192,64},{224,... | collective-permute-start | bytes 12296 | tf_op jit(solution)/shard_map/ppermute | solution.py:365
  70.2 1.6 %collective-permute-done.6 = f32[8,128]{1,0:T(8,128)S(1)} collective-permute-done((f32[8,128]{1,0:T(8,128)S(1)}, f32[8,128]{1,0:T(8,128)S(1)}, u32[]{:S(2)}, u32[]{:S(2)}) %collective-permute-start.6) | collective-permute-done | bytes 4128 | tf_op jit(solution)/shard_map/ppermute | solution.py:365
  71.9 5.2 %all-to-all-done.1 = f32[32,4,8,128]{3,2,1,0:T(8,128)S(1)} async-done(((f32[32,4,8,128]{3,2,1,0:T(8,128)}), f32[32,4,8,128]{3,2,1,0:T(8,128)S(1)}, u32[]{:S(2)}, u32[]{:S(2)}) %all-to-all-start.1) | async-done | bytes 524320 | tf_op jit(solution)/shard_map/all_to_all | solution.py:363
  77.1 0.8 finish.1
  77.9 13.5 %all_to_all.16.messages = f32[32,4,128]{2,1,0:T(4,128)S(1)} all-to-all(f32[32,4,128]{2,1,0:T(4,128)S(1)} %get-tuple-element.20), channel_id=1, replica_groups=mesh['ka'=8,'ga'=32] {'ga'}, dimensions={0} | all-to-all | bytes 131072 | tf_op jit(solution)/shard_map/all_to_all | solution.py:367
  91.4 0.8 close.1
  (17 shorter events, 0.2 us)
Async XLA Ops:
  1.5 7.7 %copy-start = (s32[16,16]{1,0:T(8,128)S(1)}, s32[16,16]{1,0:T(8,128)}, u32[]{:S(2)}) copy-start(s32[16,16]{1,0:T(8,128)} %pair_slot.1) | copy-start | bytes 3076
  1.5 7.7 %collective-permute-start = (bf16[16,16,128]{2,1,0:T(8,128)(2,1)S(1)}, bf16[16,16,128]{2,1,0:T(8,128)(2,1)S(1)}, u32[]{:S(2)}, u32[]{:S(2)}) collective-permute-start(bf16[16,16,128]{2,1,0:T(8,128)(2,1)S(1)} %reshape.18.orbitals), channel_id=1, source_target_pairs={{0,32},{32,64},{64,96},{96,128},{128,160},{160,192},{192,224},{224... | collective-permute-start | bytes 196616 | tf_op jit(solution)/shard_map/ppermute | solution.py:345
  9.9 33.0 %copy-start.2 = (bf16[4,256,512]{2,1,0:T(8,128)(2,1)S(1)}, bf16[4,256,512]{2,1,0:T(8,128)(2,1)}, u32[]{:S(2)}) copy-start(bf16[4,256,512]{2,1,0:T(8,128)(2,1)} %constant.6.clone.left) | copy-start | bytes 3145732
  10.0 33.0 %copy-start.3 = (bf16[2,512,256]{2,1,0:T(8,128)(2,1)S(1)}, bf16[2,512,256]{2,1,0:T(8,128)(2,1)}, u32[]{:S(2)}) copy-start(bf16[2,512,256]{2,1,0:T(8,128)(2,1)} %constant.7.clone.right) | copy-start | bytes 1572868
  40.3 2.7 %copy-start.1 = (s32[16]{0:T(128)S(1)}, s32[16]{0:T(128)}, u32[]{:S(2)}) copy-start(s32[16]{0:T(128)} %counts.7) | copy-start | bytes 196
  40.3 2.7 %copy-start.4 = (f32[2,128,128]{2,1,0:T(8,128)S(1)}, f32[2,128,128]{2,1,0:T(8,128)}, u32[]{:S(2)}) copy-start(f32[2,128,128]{2,1,0:T(8,128)} %constant.8.clone.twiddle) | copy-start | bytes 393220
  40.3 5.6 %collective-permute-start.2 = (bf16[32,2,16,128]{3,2,1,0:T(8,128)(2,1)S(1)}, bf16[32,2,16,128]{3,2,1,0:T(8,128)(2,1)S(1)}, u32[]{:S(2)}, u32[]{:S(2)}) collective-permute-start(bf16[32,2,16,128]{3,2,1,0:T(8,128)(2,1)S(1)} %slice.4), channel_id=1, source_target_pairs={{0,1},{1,0},{2,3},{3,2},{4,5},{5,4},{6,7},{7,6},{8,9},{9,8},{10,11... | collective-permute-start | bytes 786440 | tf_op jit(solution)/shard_map/ppermute | solution.py:350
  42.4 7.8 %collective-permute-start.1 = (bf16[32,2,16,128]{3,2,1,0:T(8,128)(2,1)S(1)}, bf16[32,2,16,128]{3,2,1,0:T(8,128)(2,1)S(1)}, u32[]{:S(2)}, u32[]{:S(2)}) collective-permute-start(bf16[32,2,16,128]{3,2,1,0:T(8,128)(2,1)S(1)} %slice.4), channel_id=1, source_target_pairs={{0,16},{1,17},{2,18},{3,19},{4,20},{5,21},{6,22},{7,23},{8,24},{9,... | collective-permute-start | bytes 786440 | tf_op jit(solution)/shard_map/ppermute | solution.py:350
  50.2 2.1 %collective-permute-start.3 = (bf16[32,2,16,128]{3,2,1,0:T(8,128)(2,1)S(1)}, bf16[32,2,16,128]{3,2,1,0:T(8,128)(2,1)S(1)}, u32[]{:S(2)}, u32[]{:S(2)}) collective-permute-start(bf16[32,2,16,128]{3,2,1,0:T(8,128)(2,1)S(1)} %collective-permute-done.1.partners), channel_id=1, source_target_pairs={{0,1},{1,0},{2,3},{3,2},{4,5},{5,4},{6,7},{7,6},{8,9},{9,8},{10,11... | collective-permute-start | bytes 786440 | tf_op jit(solution)/shard_map/ppermute | solution.py:350
  53.7 23.3 %all-to-all-start.1 = ((f32[32,4,8,128]{3,2,1,0:T(8,128)}), f32[32,4,8,128]{3,2,1,0:T(8,128)S(1)}, u32[]{:S(2)}, u32[]{:S(2)}) async-start(f32[32,4,8,128]{3,2,1,0:T(8,128)} %get-tuple-element.17), calls=%async_computation.1 | async-start | bytes 1048576 | tf_op jit(solution)/shard_map/all_to_all | solution.py:363
  60.5 2.8 %collective-permute-start.4 = (f32[8,128]{1,0:T(8,128)S(1)}, f32[8,128]{1,0:T(8,128)S(1)}, u32[]{:S(2)}, u32[]{:S(2)}) collective-permute-start(f32[8,128]{1,0:T(8,128)S(1)} %get-tuple-element.18), channel_id=1, source_target_pairs={{0,32},{32,0},{64,96},{96,64},{128,160},{160,128},{192,224},{224,1... | collective-permute-start | bytes 12296 | tf_op jit(solution)/shard_map/ppermute | solution.py:365
  63.3 4.3 %collective-permute-start.5 = (f32[8,128]{1,0:T(8,128)S(1)}, f32[8,128]{1,0:T(8,128)S(1)}, u32[]{:S(2)}, u32[]{:S(2)}) collective-permute-start(f32[8,128]{1,0:T(8,128)S(1)} %add.9), channel_id=1, source_target_pairs={{0,64},{32,96},{64,0},{96,32},{128,192},{160,224},{192,128},{224,1... | collective-permute-start | bytes 12296 | tf_op jit(solution)/shard_map/ppermute | solution.py:365
  67.6 4.3 %collective-permute-start.6 = (f32[8,128]{1,0:T(8,128)S(1)}, f32[8,128]{1,0:T(8,128)S(1)}, u32[]{:S(2)}, u32[]{:S(2)}) collective-permute-start(f32[8,128]{1,0:T(8,128)S(1)} %add.10), channel_id=1, source_target_pairs={{0,128},{32,160},{64,192},{96,224},{128,0},{160,32},{192,64},{224,... | collective-permute-start | bytes 12296 | tf_op jit(solution)/shard_map/ppermute | solution.py:365

commit v4 on v3

v4 whole, which is shorter than its diff:
```python
import functools

import numpy as np
import jax
import jax.numpy as jnp
from jax import lax
from jax.experimental import pallas as pl
from jax.experimental.pallas import tpu as pltpu
from jax.sharding import PartitionSpec as P

highest = lax.Precision.HIGHEST
f32 = jnp.float32
bf16 = jnp.bfloat16


def embed(matrix):
    return np.block([[matrix.real, -matrix.imag], [matrix.imag, matrix.real]])


def split(matrix):
    high = matrix.astype(np.float32).astype(bf16)
    low = (matrix - high.astype(np.float64)).astype(np.float32).astype(bf16)
    return high, low


def constants():
    rows = np.arange(128)
    x_at, yh_at = rows // 8, rows % 8
    jj_at, glo_at, gxh_at = rows // 64, rows // 8 % 8, rows % 8
    forward, inverse = [], []
    for parity in range(2):
        gx_at = 4 * gxh_at + 2 * jj_at + parity
        phase = gx_at[:, None] * x_at[None, :] / 32.0 + glo_at[:, None] * yh_at[None, :] / 8.0
        real = embed(np.exp(-2j * np.pi * phase))
        for held, matrix in ((forward, real), (inverse, real.T)):
            high, low = split(matrix)
            held.append(np.concatenate((high, low), axis=1))
    lanes = np.arange(128)
    first, last = lanes // 32, lanes % 32
    phase = first[:, None] * first[None, :] / 4.0 + last[:, None] * last[None, :] / 32.0
    real = embed(np.exp(-2j * np.pi * phase)).T
    right = []
    for matrix in (real, real.T):
        high, low = split(matrix)
        right.append(np.concatenate((high, low), axis=0))
    turn = 2.0 * np.pi * (glo_at[:, None] * first[None, :]) / 32.0
    twiddle = np.stack((np.cos(turn), np.sin(turn))).astype(np.float32)
    return np.stack(forward + inverse), np.stack(right), twiddle


def two_terms(value):
    high = value.astype(bf16)
    low = (value - high.astype(f32)).astype(bf16)
    return high, low


MIB = 1 << 20


def place():
    member = lax.axis_index("ga")
    return lax.axis_index("ka"), member // 16, member // 4 % 4, member // 2 % 2, member % 2


def y_band(y_at, core):
    return 4 * y_at + core


def z_band(y_at, k, core):
    return 2 + 4 * ((y_at + k) % 2) + core


def choose_kernel(pair_slot, kernel, chosen):
    group = lax.axis_index("ka")
    partner_group = lax.rem(group + 7, 8)
    for k2 in range(4):
        second = (group if k2 < 2 else partner_group) * 2 + k2 % 2
        for k in range(2):
            block = kernel[pair_slot[group * 2 + k, second]]
            high, low = two_terms(block)
            for core in range(2):
                rows = slice(core * 4, core * 4 + 4)
                chosen[k2 * 2 + k, core] = jnp.concatenate((high[rows], low[rows]), axis=0)


def choose(pair_slot, kernel):
    vmem = pl.BlockSpec(memory_space=pltpu.VMEM)
    return pl.pallas_call(
        choose_kernel,
        out_shape=jax.ShapeDtypeStruct((8, 2, 8, 128), bf16),
        in_specs=[pl.BlockSpec(memory_space=pltpu.SMEM), vmem],
        out_specs=vmem,
        compiler_params=pltpu.CompilerParams(vmem_limit_bytes=4 * MIB),
        name="choose",
    )(pair_slot, kernel)


KERNEL_ROWS = slice(0, 8)
BAND_ROWS = (slice(8, 24), slice(24, 40))
OWN_ROWS = (slice(40, 56), slice(56, 72))


def pack_kernel(orbitals, before, chosen, packed):
    for k2 in range(4):
        source = orbitals if k2 < 2 else before
        for k in range(2):
            for quarter in range(4):
                y_at, core = quarter // 2, quarter % 2
                to = y_at * 16 + k2 * 4 + k * 2 + core
                packed[to, KERNEL_ROWS] = chosen[k2 * 2 + k, core]
                packed[to, BAND_ROWS[0]] = source[k2 % 2 * 8 + y_band(y_at, core)]
                packed[to, BAND_ROWS[1]] = source[k2 % 2 * 8 + z_band(y_at, k, core)]
                for j in range(2):
                    packed[to, OWN_ROWS[j]] = orbitals[k * 8 + quarter * 2 + j]


def pack(orbitals, before, chosen):
    vmem = pl.BlockSpec(memory_space=pltpu.VMEM)
    return pl.pallas_call(
        pack_kernel,
        out_shape=jax.ShapeDtypeStruct((32, 72, 128), bf16),
        in_specs=[vmem, vmem, vmem],
        out_specs=vmem,
        compiler_params=pltpu.CompilerParams(vmem_limit_bytes=4 * MIB),
        name="pack",
    )(orbitals, before, chosen)


def screen_of(received, other, core, scale, screen):
    halves = []
    for half in (received, other):
        half = half[:, KERNEL_ROWS].astype(f32)
        halves.append(((half + pltpu.roll(half, 4, 1)) * scale).reshape(256, 128))
    row = lax.broadcasted_iota(jnp.int32, (256, 128), 0) % 8
    raw = jnp.where(row // 4 == core, halves[0], halves[1]).reshape(4, 64, 128)
    lane_group = lax.broadcasted_iota(jnp.int32, (64, 128), 1) // 32
    for j in range(4):
        placed = jnp.zeros((64, 128), f32)
        for i in range(4):
            shift = (i - j) % 4 * 32
            moved = pltpu.roll(raw[i], shift, 1) if shift else raw[i]
            placed = jnp.where(lane_group == i, moved, placed)
        screen[j % 2, (j // 2) * 64 : (j // 2) * 64 + 64] = placed


def thrice(table, axis):
    size = table.shape[axis] // 2
    return jnp.concatenate((table, lax.slice_in_dim(table, 0, size, axis=axis)), axis=axis)


def enter(parts, table):
    stacked = jnp.concatenate([jnp.concatenate(parts[part], axis=1) for part in range(2)], axis=0)
    high, low = two_terms(stacked)
    return jnp.dot(
        thrice(table, 1), jnp.concatenate((high, high, low), axis=0), preferred_element_type=f32
    )


def across(turned, table, cosine, sine):
    lines = []
    for a in range(2):
        real = turned[:128, a * 128 : a * 128 + 128]
        imag = turned[128:, a * 128 : a * 128 + 128]
        lines.append(
            jnp.concatenate((real * cosine + imag * sine, imag * cosine - real * sine), axis=1)
        )
    high, low = two_terms(jnp.concatenate(lines, axis=0))
    return jnp.dot(
        jnp.concatenate((high, high, low), axis=1), thrice(table, 0), preferred_element_type=f32
    )


def screened(spectra, factor, table):
    factor = jnp.concatenate((factor, factor), axis=1)
    factor = jnp.concatenate((factor, factor), axis=0)
    high, low = two_terms(spectra * factor)
    return jnp.dot(
        jnp.concatenate((high, high, low), axis=1), thrice(table, 0), preferred_element_type=f32
    )


def leave(lines, table, cosine, sine):
    reals, imags = [], []
    for a in range(2):
        real = lines[a * 128 : a * 128 + 128, :128]
        imag = lines[a * 128 : a * 128 + 128, 128:]
        reals.append(real * cosine - imag * sine)
        imags.append(imag * cosine + real * sine)
    stacked = jnp.concatenate(
        (jnp.concatenate(reals, axis=1), jnp.concatenate(imags, axis=1)), axis=0
    )
    high, low = two_terms(stacked)
    return jnp.dot(
        thrice(table, 1), jnp.concatenate((high, high, low), axis=0), preferred_element_type=f32
    )


def exchange_kernel(scale, call, counts, received, *refs):
    left, right, twiddle, *rest = refs[SOURCES[call] :]
    group, y_at, k2, k, core = place()
    if call < 2:
        source = refs[0] if call else received
        partners = [lambda rows, at=at: source[rows, at] for at in BAND_ROWS]
    else:
        partners = [lambda rows, ref=ref: ref[rows] for ref in refs[:2]]
    if call == 0:
        total, screen = rest
        screen_of(received, refs[0], core, scale, screen)
        held = None
    else:
        screen, held, total = rest
    k2_at = lax.rem(group + 8 - k2 // 2, 8) * 2 + k2 % 2
    core_from = 1 - core if call % 2 else core
    bands = (
        y_band(1 - y_at if call >= 2 else y_at, core_from),
        z_band(y_at, 1 - k if call >= 2 else k, core_from),
    )
    lane = lax.broadcasted_iota(jnp.int32, (1, 16), 1)

    def count_of(kpoint):
        return jnp.sum(jnp.where(lane == kpoint, counts[...].astype(f32), 0.0), axis=1, keepdims=True)

    count = count_of(k2_at)
    kept = [
        jnp.where(count > band.astype(f32), 1.0, 0.0).reshape(1, 1, 1) for band in bands
    ]
    others, chains = [], []
    for half in range(2):
        other = partners[half](slice(0, 32)).astype(f32)
        other_real, other_imag = other[:, :8], other[:, 8:]
        sums, gaps = [[], []], [[], []]
        for a in range(2):
            own = received[:, OWN_ROWS[a]].astype(f32)
            own_real, own_imag = own[:, :8], own[:, 8:]
            density = (
                own_real * other_real + own_imag * other_imag,
                own_imag * other_real - own_real * other_imag,
            )
            for part in range(2):
                low, high = density[part][:16], density[part][16:]
                sums[part].append((low + high).reshape(128, 128))
                gaps[part].append((low - high).reshape(128, 128))
        others.append((half, kept[half]))
        chains += [(0, sums), (1, gaps)]
    cosine, sine = twiddle[0], twiddle[1]
    values = [enter(parts, left[parity]) for parity, parts in chains]
    values = [across(value, right[0], cosine, sine) for value in values]
    values = [
        screened(value, screen[parity], right[1])
        for value, (parity, parts) in zip(values, chains)
    ]
    values = [
        leave(value, left[2 + parity], cosine, sine)
        for value, (parity, parts) in zip(values, chains)
    ]
    backs = [values[2 * half : 2 * half + 2] for half in range(2)]
    for side in range(2):
        rows = slice(side * 16, side * 16 + 16)
        for a in range(2):
            add_real, add_imag = 0.0, 0.0
            if held is not None:
                add_real, add_imag = held[rows, 2 * a], held[rows, 2 * a + 1]
            for (even, odd), (half, factor) in zip(backs, others):
                field = even + odd if side == 0 else even - odd
                other = partners[half](rows).astype(f32) * factor
                b_real, b_imag = other[:, :8], other[:, 8:]
                real = field[:128, a * 128 : a * 128 + 128].reshape(16, 8, 128)
                imag = field[128:, a * 128 : a * 128 + 128].reshape(16, 8, 128)
                add_real += b_real * real - b_imag * imag
                add_imag += b_real * imag + b_imag * real
            total[rows, 2 * a] = add_real
            total[rows, 2 * a + 1] = add_imag


def energy_kernel(counts, received, total, energy):
    group, y_at, k2, k, core = place()
    lane = lax.broadcasted_iota(jnp.int32, (1, 16), 1)
    count = jnp.sum(
        jnp.where(lane == group * 2 + k, counts[...].astype(f32), 0.0), axis=1, keepdims=True
    )
    energy_sum = jnp.zeros((8, 128), f32)
    for a in range(2):
        band = y_at * 4 + core * 2 + a
        occupied = jnp.where(count > band.astype(f32), 1.0, 0.0)
        own = received[:, OWN_ROWS[a]].astype(f32)
        both = own[:, :8] * total[:, 2 * a] + own[:, 8:] * total[:, 2 * a + 1]
        energy_sum += jnp.sum(both, axis=0) * occupied
    energy[...] = jnp.full((8, 128), jnp.sum(energy_sum) * (1.0 / (32.0 * 32768.0)), f32)


def energy_part(counts, received, total):
    vmem = pl.BlockSpec(memory_space=pltpu.VMEM)
    return pl.pallas_call(
        energy_kernel,
        out_shape=jax.ShapeDtypeStruct((8, 128), f32),
        in_specs=[vmem] * 3,
        out_specs=vmem,
        compiler_params=pltpu.CompilerParams(vmem_limit_bytes=4 * MIB),
        name="energy_part",
    )(counts, received, total)


SOURCES = (1, 1, 2, 2)


def exchange(scale, call, counts, received, partners, tables, *carried):
    vmem = pl.BlockSpec(memory_space=pltpu.VMEM)
    operands = (counts, received, *partners, *tables, *carried)
    shapes = [jax.ShapeDtypeStruct((32, 4, 8, 128), f32)]
    if call == 0:
        shapes.append(jax.ShapeDtypeStruct((2, 128, 128), f32))
    return pl.pallas_call(
        functools.partial(exchange_kernel, scale, call),
        out_shape=tuple(shapes),
        in_specs=[vmem] * len(operands),
        out_specs=(vmem,) * len(shapes),
        compiler_params=pltpu.CompilerParams(vmem_limit_bytes=24 * MIB),
        cost_estimate=pl.CostEstimate(
            flops=2 * 12 * 2 * 512 * 256 * 256, bytes_accessed=4 << 20, transcendentals=0
        ),
        name=("exchange_0", "exchange_1", "exchange_2", "exchange_3")[call],
    )(*operands)


def finish_kernel(returned, orbitals, energies, vectors, message):
    fields = []
    for k in range(2):
        for y_at in range(2):
            fields.append(sum(returned[y_at, k2, k] for k2 in range(4)))
    fields = jnp.concatenate(fields, axis=0)
    vectors[...] = fields
    lane = lax.broadcasted_iota(jnp.int32, (8, 128), 1)
    rows = []
    for k in range(2):
        left = jnp.concatenate(
            [orbitals[k * 8 : k * 8 + 8, row] for row in range(16)], axis=1
        ).astype(f32)
        own = fields[k * 16 : k * 16 + 16].reshape(8, 2, 8, 128)
        real = [own[:, 0, row] for row in range(8)]
        imag = [own[:, 1, row] for row in range(8)]
        right = jnp.concatenate(
            (
                jnp.concatenate(real + imag, axis=1),
                jnp.concatenate(imag + [-value for value in real], axis=1),
            ),
            axis=0,
        )
        left = left.astype(bf16)
        product = jnp.zeros((8, 16), f32)
        for _ in range(3):
            term = right.astype(bf16)
            right = right - term.astype(f32)
            product += lax.dot_general(
                left, term, (((1,), (1,)), ((), ())), preferred_element_type=f32
            )
        spread = jnp.concatenate([product * (1.0 / 32768.0)] * 8, axis=1)
        row_at = lax.broadcasted_iota(jnp.int32, (8, 128), 0)
        spread = jnp.where(lane // 16 == row_at, spread, 0.0)
        rows.append(jnp.sum(spread, axis=0, keepdims=True))
    total = energies[:1]
    rows = jnp.concatenate((*rows, total, total), axis=0)
    message[...] = jnp.broadcast_to(rows[None], (32, 4, 128))


def finish(returned, orbitals, energies):
    vmem = pl.BlockSpec(memory_space=pltpu.VMEM)
    return pl.pallas_call(
        finish_kernel,
        out_shape=(
            jax.ShapeDtypeStruct((32, 8, 128), f32),
            jax.ShapeDtypeStruct((32, 4, 128), f32),
        ),
        in_specs=[vmem] * 3,
        out_specs=(vmem, vmem),
        compiler_params=pltpu.CompilerParams(vmem_limit_bytes=8 * MIB),
        name="finish",
    )(returned, orbitals, energies)


def close_kernel(messages, matrix, energy):
    total = jnp.sum(messages[...], axis=0)
    lane = lax.broadcasted_iota(jnp.int32, (32, 128), 1)
    row = lax.broadcasted_iota(jnp.int32, (32, 128), 0)
    spread = jnp.concatenate(
        [jnp.broadcast_to(total[k : k + 1], (16, 128)) for k in range(2)], axis=0
    )
    spread = jnp.where(lane // 8 == row % 8 * 2 + row // 8 % 2, spread, 0.0)
    gather = jnp.where(
        lax.broadcasted_iota(jnp.int32, (128, 128), 0) % 8
        == lax.broadcasted_iota(jnp.int32, (128, 128), 1),
        1.0,
        0.0,
    )
    spread = jnp.dot(spread, gather, precision=highest, preferred_element_type=f32)
    for k in range(2):
        for part in range(2):
            first = k * 16 + part * 8
            matrix[k, part] = spread[first : first + 8, :8]
    energy[...] = total[2:3, :1]


def close(messages):
    vmem = pl.BlockSpec(memory_space=pltpu.VMEM)
    return pl.pallas_call(
        close_kernel,
        out_shape=(jax.ShapeDtypeStruct((2, 2, 8, 8), f32), jax.ShapeDtypeStruct((1, 1), f32)),
        in_specs=[vmem],
        out_specs=(vmem, vmem),
        compiler_params=pltpu.CompilerParams(vmem_limit_bytes=4 * MIB),
        name="close",
    )(messages)


def on_device(orbitals, band_counts, pair_slot, kernel):
    left, right, twiddle = (jnp.asarray(table) for table in constants())
    groups = lax.axis_size("ka")
    scale = -1.0 / (16.0 * 32768.0)

    before = lax.ppermute(orbitals, "ka", [(i, (i + 1) % groups) for i in range(groups)])
    chosen = choose(pair_slot, kernel.reshape(16, 8, 128))
    counts = band_counts.reshape(1, 16)
    orbitals = orbitals.reshape(16, 16, 128)
    packed = pack(orbitals, before.reshape(16, 16, 128), chosen)
    received = lax.all_to_all(packed, "ga", 0, 0, tiled=True)

    def shown(value, bit):
        return lax.ppermute(value, "ga", [(i, i ^ bit) for i in range(32)])

    tables = (left, right, twiddle)
    next_core = shown(received[:, :40], 1)
    next_y, next_z = shown(received[:, BAND_ROWS[0]], 16), shown(received[:, BAND_ROWS[1]], 2)
    total, screen = exchange(scale, 0, counts, received, (next_core,), tables)
    (total,) = exchange(scale, 1, counts, received, (next_core,), tables, screen, total)
    next_y, next_z, total = lax.optimization_barrier((next_y, next_z, total))
    far = (shown(next_y, 1), shown(next_z, 1))
    (total,) = exchange(scale, 2, counts, received, (next_y, next_z), tables, screen, total)
    (total,) = exchange(scale, 3, counts, received, far, tables, screen, total)

    returned = lax.all_to_all(total, "ga", 0, 0, tiled=True)
    energy = energy_part(counts, received, total)
    shown_energy = lambda value, bit: lax.ppermute(value, "ka", [(i, i ^ bit) for i in range(groups)])
    near = [shown_energy(energy, bit) for bit in (1, 2, 3)]
    energy = (energy + near[0]) + (near[1] + near[2])
    energy = energy + shown_energy(energy, 4)
    vectors, message = finish(returned.reshape(2, 4, 2, 8, 8, 128), orbitals, energy)
    matrix, energy = close(lax.all_to_all(message, "ga", 0, 0, tiled=True))
    return (vectors.reshape(2, 8, 2, 1, 1024), matrix, energy[0, 0])


def solution(mesh):
    in_specs = (P("ka", None, None, "ga", None), P(), P(), P(None, None, "ga"))
    out_specs = (P("ka", None, None, "ga", None), P("ka", None, None, None), P())
    return jax.shard_map(
        on_device, mesh=mesh, in_specs=in_specs, out_specs=out_specs, check_vma=False
    )
```

time: 92.6 us -> 87.2 us (0.942)
  waiting for transfers between devices: 20.5 us -> 11.9 us
  Pallas kernels: 9.98 us -> 13.2 us
  blocking collectives: 43.8 us -> 41.9 us
  starting transfers between devices: 15.2 us -> 16.9 us
    ppermute x3 -> x4, waiting for transfers between devices: 8.63 us -> 2.95 us  [on_device(): lax.ppermute(value, 'ka', [(i, i ^ bit) for i in range(groups)])]
    ppermute x3 -> x4, starting transfers between devices: 2.72 us -> 6.56 us  [on_device(): lax.ppermute(value, 'ka', [(i, i ^ bit) for i in range(groups)])]
    all_to_all x1, starting transfers between devices: 6.75 us -> 3.77 us  [on_device(): returned = lax.all_to_all(total, 'ga', 0, 0, tiled=True)]
    ppermute x3 -> x5, waiting for transfers between devices: 2.13 us -> 0.01 us  [shown(): return lax.ppermute(value, 'ga', [(i, i ^ bit) for i in range(32)])]
    pallas_call x4, Pallas kernels: 7.6 us -> 9.63 us  [exchange(): pl.pallas_call(functools.partial(exchange_kernel, scale, call), out_shape...]
    ppermute x1, waiting for transfers between devices: 4.49 us -> 3.03 us  [on_device(): lax.ppermute(orbitals, 'ka', [(i, (i + 1) % groups) for i in range(groups)])]
    pallas_call x1 -> x3, Pallas kernels: 0.75 us -> 2.07 us  [the longest x1 1.28 us: energy_part(): pl.pallas_call(energy_kernel, out_shape=jax.ShapeDtypeStruct((8, 128), f3...]
    all_to_all x1, blocking collectives: 30.3 us -> 29.1 us  [on_device(): received = lax.all_to_all(packed, 'ga', 0, 0, tiled=True)]
  transfers between devices with their start and end apart: 8 -> 11, of which waited for: 7 -> 5; matrix products, arithmetic and copies ran while one was open for 1% -> 2% of each run, Pallas kernels for 7% -> 10%
where the time goes in v4:
time: 87.2 us; the launch traced here: 86.9 us
  blocking collectives  41.9 us (48%)
  starting transfers between devices  16.9 us (19%)
  Pallas kernels  13.2 us (15%)
  waiting for transfers between devices  11.9 us (14%)
  local copies, waits for them, and re-layouts  2.11 us (2%)
    all_to_all x1, blocking collectives, on_device(): received = lax.all_to_all(packed, 'ga', 0, 0, tiled=True)  29.1 us
    all_to_all x1, blocking collectives, on_device(): matrix, energy = close(lax.all_to_all(message, 'ga', 0, 0, tiled=True))  12.8 us
    pallas_call x4, Pallas kernels, exchange(): pl.pallas_call(functools.partial(exchange_kernel, scale, call), out_shape...  9.63 us
    ppermute x4, starting transfers between devices, on_device(): lax.ppermute(value, 'ka', [(i, i ^ bit) for i in range(groups)])  6.56 us
    all_to_all x1, waiting for transfers between devices, on_device(): returned = lax.all_to_all(total, 'ga', 0, 0, tiled=True)  5.89 us
    ppermute x5, starting transfers between devices, shown(): return lax.ppermute(value, 'ga', [(i, i ^ bit) for i in range(32)])  4.48 us
    all_to_all x1, starting transfers between devices, on_device(): returned = lax.all_to_all(total, 'ga', 0, 0, tiled=True)  3.77 us
    ppermute x1, waiting for transfers between devices, on_device(): lax.ppermute(orbitals, 'ka', [(i, (i + 1) % groups) for i in range(groups)])  3.03 us
  transfers between devices with their start and end apart: 11, of which 5 were waited for; matrix products, arithmetic and copies ran while one was open for 2% of the time, Pallas kernels for 10%

profile of v4, /device:TPU:1, one launch (start us, length us, event | category | flops | bytes accessed | tf_op | source)
XLA Modules:
  0.0 86.9 jit_solution(6689469351050726139)
XLA Ops:
  0.6 2.1 %collective-permute-start = (bf16[2,8,2,1,1024]{4,2,3,1,0:T(2,128)(2,1)}, bf16[2,8,2,1,1024]{4,2,3,1,0:T(2,128)(2,1)S(1)}, u32[]{:S(2)}, u32[]{:S(2)}) collective-permute-start(bf16[2,8,2,1,1024]{4,2,3,1,0:T(2,128)(2,1)} %param.7), channel_id=1, source_target_pairs={{0,32},{32,64},{64,96},{96,128},{128,160},{160,192},{192,224},{224... | collective-permute-start | bytes 196616 | tf_op jit(solution)/shard_map/ppermute | solution.py:419
  2.7 0.9 %reshape.25.orbitals = bf16[16,16,128]{2,1,0:T(8,128)(2,1)S(1)} reshape(bf16[2,8,2,1,1024]{4,2,3,1,0:T(2,128)(2,1)} %param.7) | data formatting | bytes 131072 | tf_op jit(solution)/shard_map/reshape | solution.py:422
  3.7 1.1 %reshape.27.kernel = f32[16,8,128]{2,1,0:T(8,128)S(1)} reshape(f32[16,32,32]{2,1,0:T(8,128)} %param.10) | data formatting | bytes 131072 | tf_op jit(solution)/shard_map/reshape | solution.py:420
  4.8 0.7 choose.1.chosen
  5.5 3.0 %collective-permute-done = bf16[2,8,2,1,1024]{4,2,3,1,0:T(2,128)(2,1)S(1)} collective-permute-done((bf16[2,8,2,1,1024]{4,2,3,1,0:T(2,128)(2,1)}, bf16[2,8,2,1,1024]{4,2,3,1,0:T(2,128)(2,1)S(1)}, u32[]{:S(2)}, u32[]{:S(2)}) %collective-permute-start) | collective-permute-done | bytes 65568 | tf_op jit(solution)/shard_map/ppermute | solution.py:419
  8.6 29.1 %all_to_all.15.received = bf16[32,72,128]{2,1,0:T(8,128)(2,1)S(1)} all-to-all(bf16[32,72,128]{2,1,0:T(8,128)(2,1)S(1)} %pack.1), channel_id=1, replica_groups=mesh['ka'=8,'ga'=32] {'ga'}, dimensions={0} | all-to-all | bytes 1179648 | tf_op jit(solution)/shard_map/all_to_all | solution.py:424
  37.8 2.1 %collective-permute-start.3 = (bf16[32,40,128]{2,1,0:T(8,128)(2,1)S(1)}, bf16[32,40,128]{2,1,0:T(8,128)(2,1)S(1)}, u32[]{:S(2)}, u32[]{:S(2)}) collective-permute-start(bf16[32,40,128]{2,1,0:T(8,128)(2,1)S(1)} %slice.14), channel_id=1, source_target_pairs={{0,1},{1,0},{2,3},{3,2},{4,5},{5,4},{6,7},{7,6},{8,9},{9,8},{10,11... | collective-permute-start | bytes 983048 | tf_op jit(solution)/shard_map/ppermute | solution.py:427
  40.5 0.9 %collective-permute-start.2 = (bf16[32,16,128]{2,1,0:T(8,128)(2,1)S(1)}, bf16[32,16,128]{2,1,0:T(8,128)(2,1)S(1)}, u32[]{:S(2)}, u32[]{:S(2)}) collective-permute-start(bf16[32,16,128]{2,1,0:T(8,128)(2,1)S(1)} %get-tuple-element.24), channel_id=1, source_target_pairs={{0,2},{1,3},{2,0},{3,1},{4,6},{5,7},{6,4},{7,5},{8,10},{9,11},{10,... | collective-permute-start | bytes 393224 | tf_op jit(solution)/shard_map/ppermute | solution.py:427
  41.4 2.2 %exchange_0.1 = (f32[32,4,8,128]{3,2,1,0:T(8,128)S(1)}, f32[2,128,128]{2,1,0:T(8,128)S(1)}) custom-call(s32[1,16]{1,0:T(1,128)S(1)} %bitcast.9, bf16[32,72,128]{2,1,0:T(8,128)(2,1)S(1)} %all_to_all.15.received, bf16[32,40,128]{2,1,0:T(8,128)(2,1)S(1)} %collective-permute-done.3.refs_0_, bf16[4,256,512]{2,1,0:T(8,128)(2,1)S(1)} %copy-done.2, ...), custom_call_target="tpu_custom_call" | custom-call | flops 1610612736 | bytes 4194304 | tf_op jit(solution)/shard_map/exchange_0/pallas_call | solution.py:312
  43.6 2.2 %exchange_1.1.refs_6_ = f32[32,4,8,128]{3,2,1,0:T(8,128)S(1)} custom-call(s32[1,16]{1,0:T(1,128)S(1)} %bitcast.10, bf16[32,72,128]{2,1,0:T(8,128)(2,1)S(1)} %all_to_all.15.received, bf16[32,40,128]{2,1,0:T(8,128)(2,1)S(1)} %collective-permute-done.3.refs_0_, bf16[4,256,512]{2,1,0:T(8,128)(2,1)S(1)} %copy-done.2, bf16[2,512,256]{2,1,0:T(8,128)(2,1)S(1)} %copy-done.3, ...), custom_call_target="tpu_custom_call" | custom-call | flops 1610612736 | bytes 4194304 | tf_op jit(solution)/shard_map/exchange_1/pallas_call | solution.py:312
  45.9 0.7 collective-permute-start.4
  46.8 2.2 %exchange_2.1.refs_6_ = f32[32,4,8,128]{3,2,1,0:T(8,128)S(1)} custom-call(s32[1,16]{1,0:T(1,128)S(1)} %bitcast.11, bf16[32,72,128]{2,1,0:T(8,128)(2,1)S(1)} %all_to_all.15.received, bf16[32,16,128]{2,1,0:T(8,128)(2,1)S(1)} %collective-permute-done.1.refs_0_, bf16[32,16,128]{2,1,0:T(8,128)(2,1)S(1)} %collective-permute-done.2.refs_1_, ...), custom_call_target="tpu_custom_call" | custom-call | flops 1610612736 | bytes 4194304 | tf_op jit(solution)/shard_map/exchange_2/pallas_call | solution.py:312
  49.0 3.0 %exchange_3.1.total = f32[32,4,8,128]{3,2,1,0:T(8,128)} custom-call(s32[1,16]{1,0:T(1,128)S(1)} %bitcast.12, bf16[32,72,128]{2,1,0:T(8,128)(2,1)S(1)} %all_to_all.15.received, bf16[32,16,128]{2,1,0:T(8,128)(2,1)S(1)} %collective-permute-done.4.refs_0_, bf16[32,16,128]{2,1,0:T(8,128)(2,1)S(1)} %collective-permute-done.5.refs_1_, ...), custom_call_target="tpu_custom_call" | custom-call | flops 1610612736 | bytes 4194304 | tf_op jit(solution)/shard_map/exchange_3/pallas_call | solution.py:312
  52.0 3.8 %all-to-all-start.1 = ((f32[32,4,8,128]{3,2,1,0:T(8,128)}), f32[32,4,8,128]{3,2,1,0:T(8,128)S(1)}, u32[]{:S(2)}, u32[]{:S(2)}) async-start(f32[32,4,8,128]{3,2,1,0:T(8,128)} %exchange_3.1.total), calls=%async_computation.1 | async-start | bytes 1048576 | tf_op jit(solution)/shard_map/all_to_all | solution.py:439
  55.8 1.3 %energy_part.1 = f32[8,128]{1,0:T(8,128)S(1)} custom-call(s32[1,16]{1,0:T(1,128)S(1)} %bitcast.13, bf16[32,72,128]{2,1,0:T(8,128)(2,1)S(1)} %all_to_all.15.received, f32[32,4,8,128]{3,2,1,0:T(8,128)} %exchange_3.1.total), custom_call_target="tpu_custom_call" | custom-call | tf_op jit(solution)/shard_map/energy_part/pallas_call | solution.py:293
  57.2 0.5 collective-permute-start.7
  57.7 3.3 %collective-permute-start.8 = (f32[8,128]{1,0:T(8,128)S(1)}, f32[8,128]{1,0:T(8,128)S(1)}, u32[]{:S(2)}, u32[]{:S(2)}) collective-permute-start(f32[8,128]{1,0:T(8,128)S(1)} %energy_part.1), channel_id=1, source_target_pairs={{0,96},{32,64},{64,32},{96,0},{128,224},{160,192},{192,160},{224,1... | collective-permute-start | bytes 12296 | tf_op jit(solution)/shard_map/ppermute | solution.py:441
  61.3 1.0 %collective-permute-done.8 = f32[8,128]{1,0:T(8,128)S(1)} collective-permute-done((f32[8,128]{1,0:T(8,128)S(1)}, f32[8,128]{1,0:T(8,128)S(1)}, u32[]{:S(2)}, u32[]{:S(2)}) %collective-permute-start.8) | collective-permute-done | bytes 4128 | tf_op jit(solution)/shard_map/ppermute | solution.py:441
  62.3 2.6 %collective-permute-start.9 = (f32[8,128]{1,0:T(8,128)S(1)}, f32[8,128]{1,0:T(8,128)S(1)}, u32[]{:S(2)}, u32[]{:S(2)}) collective-permute-start(f32[8,128]{1,0:T(8,128)S(1)} %add_add_fusion), channel_id=1, source_target_pairs={{0,128},{32,160},{64,192},{96,224},{128,0},{160,32},{192,64},{224,... | collective-permute-start | bytes 12296 | tf_op jit(solution)/shard_map/ppermute | solution.py:441
  65.0 1.6 %collective-permute-done.9 = f32[8,128]{1,0:T(8,128)S(1)} collective-permute-done((f32[8,128]{1,0:T(8,128)S(1)}, f32[8,128]{1,0:T(8,128)S(1)}, u32[]{:S(2)}, u32[]{:S(2)}) %collective-permute-start.9) | collective-permute-done | bytes 4128 | tf_op jit(solution)/shard_map/ppermute | solution.py:441
  66.6 5.9 %all-to-all-done.1 = f32[32,4,8,128]{3,2,1,0:T(8,128)S(1)} async-done(((f32[32,4,8,128]{3,2,1,0:T(8,128)}), f32[32,4,8,128]{3,2,1,0:T(8,128)S(1)}, u32[]{:S(2)}, u32[]{:S(2)}) %all-to-all-start.1) | async-done | bytes 524320 | tf_op jit(solution)/shard_map/all_to_all | solution.py:439
  72.5 0.7 finish.1
  73.2 12.8 %all_to_all.16.messages = f32[32,4,128]{2,1,0:T(4,128)S(1)} all-to-all(f32[32,4,128]{2,1,0:T(4,128)S(1)} %get-tuple-element.18), channel_id=1, replica_groups=mesh['ka'=8,'ga'=32] {'ga'}, dimensions={0} | all-to-all | bytes 131072 | tf_op jit(solution)/shard_map/all_to_all | solution.py:446
  86.0 0.8 close.1
  (26 shorter events, 1.4 us)
Async XLA Ops:
  0.6 7.9 %collective-permute-start = (bf16[2,8,2,1,1024]{4,2,3,1,0:T(2,128)(2,1)}, bf16[2,8,2,1,1024]{4,2,3,1,0:T(2,128)(2,1)S(1)}, u32[]{:S(2)}, u32[]{:S(2)}) collective-permute-start(bf16[2,8,2,1,1024]{4,2,3,1,0:T(2,128)(2,1)} %param.7), channel_id=1, source_target_pairs={{0,32},{32,64},{64,96},{96,128},{128,160},{160,192},{192,224},{224... | collective-permute-start | bytes 196616 | tf_op jit(solution)/shard_map/ppermute | solution.py:419
  3.7 1.1 %copy-start = (s32[16,16]{1,0:T(8,128)S(1)}, s32[16,16]{1,0:T(8,128)}, u32[]{:S(2)}) copy-start(s32[16,16]{1,0:T(8,128)} %pair_slot.1) | copy-start | bytes 3076
  8.6 32.7 %copy-start.2 = (bf16[4,256,512]{2,1,0:T(8,128)(2,1)S(1)}, bf16[4,256,512]{2,1,0:T(8,128)(2,1)}, u32[]{:S(2)}) copy-start(bf16[4,256,512]{2,1,0:T(8,128)(2,1)} %constant.6.clone.refs_1_.refs_2_) | copy-start | bytes 3145732
  37.7 3.6 %copy-start.3 = (bf16[2,512,256]{2,1,0:T(8,128)(2,1)S(1)}, bf16[2,512,256]{2,1,0:T(8,128)(2,1)}, u32[]{:S(2)}) copy-start(bf16[2,512,256]{2,1,0:T(8,128)(2,1)} %constant.7.clone.refs_2_.refs_3_) | copy-start | bytes 1572868
  37.8 3.6 %copy-start.4 = (f32[2,128,128]{2,1,0:T(8,128)S(1)}, f32[2,128,128]{2,1,0:T(8,128)}, u32[]{:S(2)}) copy-start(f32[2,128,128]{2,1,0:T(8,128)} %constant.8.clone.refs_3_.refs_4_) | copy-start | bytes 393220
  37.8 3.6 %collective-permute-start.3 = (bf16[32,40,128]{2,1,0:T(8,128)(2,1)S(1)}, bf16[32,40,128]{2,1,0:T(8,128)(2,1)S(1)}, u32[]{:S(2)}, u32[]{:S(2)}) collective-permute-start(bf16[32,40,128]{2,1,0:T(8,128)(2,1)S(1)} %slice.14), channel_id=1, source_target_pairs={{0,1},{1,0},{2,3},{3,2},{4,5},{5,4},{6,7},{7,6},{8,9},{9,8},{10,11... | collective-permute-start | bytes 983048 | tf_op jit(solution)/shard_map/ppermute | solution.py:427
  40.0 5.9 %collective-permute-start.1 = (bf16[32,16,128]{2,1,0:T(8,128)(2,1)S(1)}, bf16[32,16,128]{2,1,0:T(8,128)(2,1)S(1)}, u32[]{:S(2)}, u32[]{:S(2)}) collective-permute-start(bf16[32,16,128]{2,1,0:T(8,128)(2,1)S(1)} %get-tuple-element.25), channel_id=1, source_target_pairs={{0,16},{1,17},{2,18},{3,19},{4,20},{5,21},{6,22},{7,23},{8,24},{9,... | collective-permute-start | bytes 393224 | tf_op jit(solution)/shard_map/ppermute | solution.py:427
  40.5 0.9 %copy-start.1 = (s32[16]{0:T(128)S(1)}, s32[16]{0:T(128)}, u32[]{:S(2)}) copy-start(s32[16]{0:T(128)} %param.8) | copy-start | bytes 196
  40.5 5.4 %collective-permute-start.2 = (bf16[32,16,128]{2,1,0:T(8,128)(2,1)S(1)}, bf16[32,16,128]{2,1,0:T(8,128)(2,1)S(1)}, u32[]{:S(2)}, u32[]{:S(2)}) collective-permute-start(bf16[32,16,128]{2,1,0:T(8,128)(2,1)S(1)} %get-tuple-element.24), channel_id=1, source_target_pairs={{0,2},{1,3},{2,0},{3,1},{4,6},{5,7},{6,4},{7,5},{8,10},{9,11},{10,... | collective-permute-start | bytes 393224 | tf_op jit(solution)/shard_map/ppermute | solution.py:427
  45.9 3.1 %collective-permute-start.4 = (bf16[32,16,128]{2,1,0:T(8,128)(2,1)S(1)}, bf16[32,16,128]{2,1,0:T(8,128)(2,1)S(1)}, u32[]{:S(2)}, u32[]{:S(2)}) collective-permute-start(bf16[32,16,128]{2,1,0:T(8,128)(2,1)S(1)} %collective-permute-done.1.refs_0_), channel_id=1, source_target_pairs={{0,1},{1,0},{2,3},{3,2},{4,5},{5,4},{6,7},{7,6},{8,9},{9,8},{10,11... | collective-permute-start | bytes 393224 | tf_op jit(solution)/shard_map/ppermute | solution.py:427
  46.5 2.5 %collective-permute-start.5 = (bf16[32,16,128]{2,1,0:T(8,128)(2,1)S(1)}, bf16[32,16,128]{2,1,0:T(8,128)(2,1)S(1)}, u32[]{:S(2)}, u32[]{:S(2)}) collective-permute-start(bf16[32,16,128]{2,1,0:T(8,128)(2,1)S(1)} %collective-permute-done.2.refs_1_), channel_id=1, source_target_pairs={{0,1},{1,0},{2,3},{3,2},{4,5},{5,4},{6,7},{7,6},{8,9},{9,8},{10,11... | collective-permute-start | bytes 393224 | tf_op jit(solution)/shard_map/ppermute | solution.py:427
  52.0 20.5 %all-to-all-start.1 = ((f32[32,4,8,128]{3,2,1,0:T(8,128)}), f32[32,4,8,128]{3,2,1,0:T(8,128)S(1)}, u32[]{:S(2)}, u32[]{:S(2)}) async-start(f32[32,4,8,128]{3,2,1,0:T(8,128)} %exchange_3.1.total), calls=%async_computation.1 | async-start | bytes 1048576 | tf_op jit(solution)/shard_map/all_to_all | solution.py:439
  57.1 3.9 %collective-permute-start.6 = (f32[8,128]{1,0:T(8,128)S(1)}, f32[8,128]{1,0:T(8,128)S(1)}, u32[]{:S(2)}, u32[]{:S(2)}) collective-permute-start(f32[8,128]{1,0:T(8,128)S(1)} %energy_part.1), channel_id=1, source_target_pairs={{0,32},{32,0},{64,96},{96,64},{128,160},{160,128},{192,224},{224,1... | collective-permute-start | bytes 12296 | tf_op jit(solution)/shard_map/ppermute | solution.py:441
  57.2 4.1 %collective-permute-start.7 = (f32[8,128]{1,0:T(8,128)S(1)}, f32[8,128]{1,0:T(8,128)S(1)}, u32[]{:S(2)}, u32[]{:S(2)}) collective-permute-start(f32[8,128]{1,0:T(8,128)S(1)} %energy_part.1), channel_id=1, source_target_pairs={{0,64},{32,96},{64,0},{96,32},{128,192},{160,224},{192,128},{224,1... | collective-permute-start | bytes 12296 | tf_op jit(solution)/shard_map/ppermute | solution.py:441
  57.7 4.6 %collective-permute-start.8 = (f32[8,128]{1,0:T(8,128)S(1)}, f32[8,128]{1,0:T(8,128)S(1)}, u32[]{:S(2)}, u32[]{:S(2)}) collective-permute-start(f32[8,128]{1,0:T(8,128)S(1)} %energy_part.1), channel_id=1, source_target_pairs={{0,96},{32,64},{64,32},{96,0},{128,224},{160,192},{192,160},{224,1... | collective-permute-start | bytes 12296 | tf_op jit(solution)/shard_map/ppermute | solution.py:441
  62.3 4.3 %collective-permute-start.9 = (f32[8,128]{1,0:T(8,128)S(1)}, f32[8,128]{1,0:T(8,128)S(1)}, u32[]{:S(2)}, u32[]{:S(2)}) collective-permute-start(f32[8,128]{1,0:T(8,128)S(1)} %add_add_fusion), channel_id=1, source_target_pairs={{0,128},{32,160},{64,192},{96,224},{128,0},{160,32},{192,64},{224,... | collective-permute-start | bytes 12296 | tf_op jit(solution)/shard_map/ppermute | solution.py:441

commit v5 on v4

--- a/solution.py
+++ b/solution.py
@@ -195,6 +195,30 @@
     )
 
 
+LEVELS = 10
+BASE = 2 * LEVELS + 1
+
+
+def remainder(value):
+    high = value.astype(bf16)
+    wide = high.astype(f32)
+    share = (value - wide) / jnp.where(wide == 0.0, 1.0, wide)
+    return high, jnp.floor(share * (256.0 * LEVELS) + 0.5)
+
+
+def coded(real, imag):
+    real, first = remainder(real)
+    imag, second = remainder(imag)
+    return jnp.concatenate((real, imag), axis=1), first * BASE + second
+
+
+def decoded(high, code):
+    first = jnp.floor(code * (1.0 / BASE) + 0.5)
+    second = code - first * BASE
+    step = 1.0 / (256.0 * LEVELS)
+    return high[..., :8, :] * (1.0 + first * step), high[..., 8:, :] * (1.0 + second * step)
+
+
 def exchange_kernel(scale, call, counts, received, *refs):
     left, right, twiddle, *rest = refs[SOURCES[call] :]
     group, y_at, k2, k, core = place()
@@ -208,7 +232,9 @@
         screen_of(received, refs[0], core, scale, screen)
         held = None
     else:
-        screen, held, total = rest
+        screen, held, total = rest[:3]
+        if call == 3:
+            leaving, energy, total = rest[2:]
     k2_at = lax.rem(group + 8 - k2 // 2, 8) * 2 + k2 % 2
     core_from = 1 - core if call % 2 else core
     bands = (
@@ -256,6 +282,7 @@
     backs = [values[2 * half : 2 * half + 2] for half in range(2)]
     for side in range(2):
         rows = slice(side * 16, side * 16 + 16)
+        codes = []
         for a in range(2):
             add_real, add_imag = 0.0, 0.0
             if held is not None:
@@ -270,34 +297,21 @@
                 add_imag += b_real * imag + b_imag * real
             total[rows, 2 * a] = add_real
             total[rows, 2 * a + 1] = add_imag
-
-
-def energy_kernel(counts, received, total, energy):
-    group, y_at, k2, k, core = place()
-    lane = lax.broadcasted_iota(jnp.int32, (1, 16), 1)
-    count = jnp.sum(
-        jnp.where(lane == group * 2 + k, counts[...].astype(f32), 0.0), axis=1, keepdims=True
-    )
-    energy_sum = jnp.zeros((8, 128), f32)
-    for a in range(2):
-        band = y_at * 4 + core * 2 + a
-        occupied = jnp.where(count > band.astype(f32), 1.0, 0.0)
-        own = received[:, OWN_ROWS[a]].astype(f32)
-        both = own[:, :8] * total[:, 2 * a] + own[:, 8:] * total[:, 2 * a + 1]
-        energy_sum += jnp.sum(both, axis=0) * occupied
-    energy[...] = jnp.full((8, 128), jnp.sum(energy_sum) * (1.0 / (32.0 * 32768.0)), f32)
-
-
-def energy_part(counts, received, total):
-    vmem = pl.BlockSpec(memory_space=pltpu.VMEM)
-    return pl.pallas_call(
-        energy_kernel,
-        out_shape=jax.ShapeDtypeStruct((8, 128), f32),
-        in_specs=[vmem] * 3,
-        out_specs=vmem,
-        compiler_params=pltpu.CompilerParams(vmem_limit_bytes=4 * MIB),
-        name="energy_part",
-    )(counts, received, total)
+            if call == 3:
+                leaving[rows, 16 * a : 16 * a + 16], code = coded(add_real, add_imag)
+                codes.append(code)
+        if call == 3:
+            leaving[rows, 32:48] = jnp.concatenate(codes, axis=1).astype(bf16)
+
+    if call == 3:
+        count = count_of(group * 2 + k)
+        energy_sum = jnp.zeros((8, 128), f32)
+        for a in range(2):
+            occupied = jnp.where(count > (y_at * 4 + core * 2 + a).astype(f32), 1.0, 0.0)
+            own = received[:, OWN_ROWS[a]].astype(f32)
+            both = own[:, :8] * total[:, 2 * a] + own[:, 8:] * total[:, 2 * a + 1]
+            energy_sum += jnp.sum(both, axis=0) * occupied
+        energy[...] = jnp.full((8, 128), jnp.sum(energy_sum) * (1.0 / (32.0 * 32768.0)), f32)
 
 
 SOURCES = (1, 1, 2, 2)
@@ -306,7 +320,10 @@
 def exchange(scale, call, counts, received, partners, tables, *carried):
     vmem = pl.BlockSpec(memory_space=pltpu.VMEM)
     operands = (counts, received, *partners, *tables, *carried)
-    shapes = [jax.ShapeDtypeStruct((32, 4, 8, 128), f32)]
+    shapes, scratch = [jax.ShapeDtypeStruct((32, 4, 8, 128), f32)], []
+    if call == 3:
+        shapes = [jax.ShapeDtypeStruct((32, 48, 128), bf16), jax.ShapeDtypeStruct((8, 128), f32)]
+        scratch = [pltpu.VMEM((32, 4, 8, 128), f32)]
     if call == 0:
         shapes.append(jax.ShapeDtypeStruct((2, 128, 128), f32))
     return pl.pallas_call(
@@ -314,6 +331,7 @@
         out_shape=tuple(shapes),
         in_specs=[vmem] * len(operands),
         out_specs=(vmem,) * len(shapes),
+        scratch_shapes=scratch,
         compiler_params=pltpu.CompilerParams(vmem_limit_bytes=24 * MIB),
         cost_estimate=pl.CostEstimate(
             flops=2 * 12 * 2 * 512 * 256 * 256, bytes_accessed=4 << 20, transcendentals=0
@@ -326,7 +344,17 @@
     fields = []
     for k in range(2):
         for y_at in range(2):
-            fields.append(sum(returned[y_at, k2, k] for k2 in range(4)))
+            for core in range(2):
+                sums = [0.0] * 4
+                for k2 in range(4):
+                    block = returned[y_at, k2, k, core].astype(f32)
+                    for a in range(2):
+                        parts = decoded(
+                            block[16 * a : 16 * a + 16], block[32 + 8 * a : 40 + 8 * a]
+                        )
+                        for part in range(2):
+                            sums[2 * a + part] += parts[part]
+                fields += [value.reshape(1, 8, 128) for value in sums]
     fields = jnp.concatenate(fields, axis=0)
     vectors[...] = fields
     lane = lax.broadcasted_iota(jnp.int32, (8, 128), 1)
@@ -434,15 +462,14 @@
     next_y, next_z, total = lax.optimization_barrier((next_y, next_z, total))
     far = (shown(next_y, 1), shown(next_z, 1))
     (total,) = exchange(scale, 2, counts, received, (next_y, next_z), tables, screen, total)
-    (total,) = exchange(scale, 3, counts, received, far, tables, screen, total)
-
-    returned = lax.all_to_all(total, "ga", 0, 0, tiled=True)
-    energy = energy_part(counts, received, total)
+    leaving, energy = exchange(scale, 3, counts, received, far, tables, screen, total)
+
+    returned = lax.all_to_all(leaving, "ga", 0, 0, tiled=True)
     shown_energy = lambda value, bit: lax.ppermute(value, "ka", [(i, i ^ bit) for i in range(groups)])
     near = [shown_energy(energy, bit) for bit in (1, 2, 3)]
     energy = (energy + near[0]) + (near[1] + near[2])
     energy = energy + shown_energy(energy, 4)
-    vectors, message = finish(returned.reshape(2, 4, 2, 8, 8, 128), orbitals, energy)
+    vectors, message = finish(returned.reshape(2, 4, 2, 2, 48, 128), orbitals, energy)
     matrix, energy = close(lax.all_to_all(message, "ga", 0, 0, tiled=True))
     return (vectors.reshape(2, 8, 2, 1, 1024), matrix, energy[0, 0])
 

time: 87.2 us -> 85.8 us (0.984)
  waiting for transfers between devices: 11.9 us -> 10.7 us
  Pallas kernels: 13.2 us -> 12.1 us
  blocking collectives: 41.9 us -> 42.8 us
    pallas_call x1 -> x0, Pallas kernels: 1.28 us -> none  [energy_part(): pl.pallas_call(energy_kernel, out_shape=jax.ShapeDtypeStruct((8, 128), f3...]
    all_to_all x1, waiting for transfers between devices: 5.89 us -> 4.67 us  [on_device(): returned = lax.all_to_all(leaving, 'ga', 0, 0, tiled=True)]
    all_to_all x1, blocking collectives: 12.8 us -> 13.7 us  [on_device(): matrix, energy = close(lax.all_to_all(message, 'ga', 0, 0, tiled=True))]
  transfers between devices with their start and end apart: 11 -> 11, of which waited for: 5 -> 5; matrix products, arithmetic and copies ran while one was open for 2% -> 2% of each run, Pallas kernels for 10% -> 8%
where the time goes in v5:
time: 85.8 us; the launch traced here: 85.4 us
  blocking collectives  42.8 us (50%)
  starting transfers between devices  16.9 us (20%)
  Pallas kernels  12.1 us (14%)
  waiting for transfers between devices  10.7 us (12%)
  local copies, waits for them, and re-layouts  2.11 us (2%)
    all_to_all x1, blocking collectives, on_device(): received = lax.all_to_all(packed, 'ga', 0, 0, tiled=True)  29.1 us
    all_to_all x1, blocking collectives, on_device(): matrix, energy = close(lax.all_to_all(message, 'ga', 0, 0, tiled=True))  13.7 us
    pallas_call x4, Pallas kernels, exchange(): pl.pallas_call(functools.partial(exchange_kernel, scale, call), out_shape...  9.73 us
    ppermute x4, starting transfers between devices, on_device(): lax.ppermute(value, 'ka', [(i, i ^ bit) for i in range(groups)])  6.56 us
    all_to_all x1, waiting for transfers between devices, on_device(): returned = lax.all_to_all(leaving, 'ga', 0, 0, tiled=True)  4.67 us
    ppermute x5, starting transfers between devices, shown(): return lax.ppermute(value, 'ga', [(i, i ^ bit) for i in range(32)])  4.48 us
    all_to_all x1, starting transfers between devices, on_device(): returned = lax.all_to_all(leaving, 'ga', 0, 0, tiled=True)  3.76 us
    ppermute x1, waiting for transfers between devices, on_device(): lax.ppermute(orbitals, 'ka', [(i, (i + 1) % groups) for i in range(groups)])  3.03 us
  transfers between devices with their start and end apart: 11, of which 5 were waited for; matrix products, arithmetic and copies ran while one was open for 2% of the time, Pallas kernels for 8%

profile of v5, /device:TPU:1, one launch (start us, length us, event | category | flops | bytes accessed | tf_op | source)
XLA Modules:
  0.0 85.4 jit_solution(1314066040750981589)
XLA Ops:
  0.6 2.1 %collective-permute-start = (bf16[2,8,2,1,1024]{4,2,3,1,0:T(2,128)(2,1)}, bf16[2,8,2,1,1024]{4,2,3,1,0:T(2,128)(2,1)S(1)}, u32[]{:S(2)}, u32[]{:S(2)}) collective-permute-start(bf16[2,8,2,1,1024]{4,2,3,1,0:T(2,128)(2,1)} %param.7), channel_id=1, source_target_pairs={{0,32},{32,64},{64,96},{96,128},{128,160},{160,192},{192,224},{224... | collective-permute-start | bytes 196616 | tf_op jit(solution)/shard_map/ppermute | solution.py:447
  2.7 0.9 %reshape.25.orbitals = bf16[16,16,128]{2,1,0:T(8,128)(2,1)S(1)} reshape(bf16[2,8,2,1,1024]{4,2,3,1,0:T(2,128)(2,1)} %param.7) | data formatting | bytes 131072 | tf_op jit(solution)/shard_map/reshape | solution.py:450
  3.7 1.1 %reshape.27.kernel = f32[16,8,128]{2,1,0:T(8,128)S(1)} reshape(f32[16,32,32]{2,1,0:T(8,128)} %param.10) | data formatting | bytes 131072 | tf_op jit(solution)/shard_map/reshape | solution.py:448
  4.8 0.7 choose.1.chosen
  5.5 3.0 %collective-permute-done = bf16[2,8,2,1,1024]{4,2,3,1,0:T(2,128)(2,1)S(1)} collective-permute-done((bf16[2,8,2,1,1024]{4,2,3,1,0:T(2,128)(2,1)}, bf16[2,8,2,1,1024]{4,2,3,1,0:T(2,128)(2,1)S(1)}, u32[]{:S(2)}, u32[]{:S(2)}) %collective-permute-start) | collective-permute-done | bytes 65568 | tf_op jit(solution)/shard_map/ppermute | solution.py:447
  8.6 29.1 %all_to_all.15.received = bf16[32,72,128]{2,1,0:T(8,128)(2,1)S(1)} all-to-all(bf16[32,72,128]{2,1,0:T(8,128)(2,1)S(1)} %pack.1), channel_id=1, replica_groups=mesh['ka'=8,'ga'=32] {'ga'}, dimensions={0} | all-to-all | bytes 1179648 | tf_op jit(solution)/shard_map/all_to_all | solution.py:452
  37.8 2.1 %collective-permute-start.3 = (bf16[32,40,128]{2,1,0:T(8,128)(2,1)S(1)}, bf16[32,40,128]{2,1,0:T(8,128)(2,1)S(1)}, u32[]{:S(2)}, u32[]{:S(2)}) collective-permute-start(bf16[32,40,128]{2,1,0:T(8,128)(2,1)S(1)} %slice.14), channel_id=1, source_target_pairs={{0,1},{1,0},{2,3},{3,2},{4,5},{5,4},{6,7},{7,6},{8,9},{9,8},{10,11... | collective-permute-start | bytes 983048 | tf_op jit(solution)/shard_map/ppermute | solution.py:455
  40.0 0.5 collective-permute-start.1
  40.5 0.9 %collective-permute-start.2 = (bf16[32,16,128]{2,1,0:T(8,128)(2,1)S(1)}, bf16[32,16,128]{2,1,0:T(8,128)(2,1)S(1)}, u32[]{:S(2)}, u32[]{:S(2)}) collective-permute-start(bf16[32,16,128]{2,1,0:T(8,128)(2,1)S(1)} %get-tuple-element.28), channel_id=1, source_target_pairs={{0,2},{1,3},{2,0},{3,1},{4,6},{5,7},{6,4},{7,5},{8,10},{9,11},{10,... | collective-permute-start | bytes 393224 | tf_op jit(solution)/shard_map/ppermute | solution.py:455
  41.4 2.2 %exchange_0.1 = (f32[32,4,8,128]{3,2,1,0:T(8,128)S(1)}, f32[2,128,128]{2,1,0:T(8,128)S(1)}) custom-call(s32[1,16]{1,0:T(1,128)S(1)} %bitcast.9, bf16[32,72,128]{2,1,0:T(8,128)(2,1)S(1)} %all_to_all.15.received, bf16[32,40,128]{2,1,0:T(8,128)(2,1)S(1)} %collective-permute-done.3.refs_0_, bf16[4,256,512]{2,1,0:T(8,128)(2,1)S(1)} %copy-done.2, ...), custom_call_target="tpu_custom_call" | custom-call | flops 1610612736 | bytes 4194304 | tf_op jit(solution)/shard_map/exchange_0/pallas_call | solution.py:329
  43.6 2.2 %exchange_1.1.refs_6_ = f32[32,4,8,128]{3,2,1,0:T(8,128)S(1)} custom-call(s32[1,16]{1,0:T(1,128)S(1)} %bitcast.10, bf16[32,72,128]{2,1,0:T(8,128)(2,1)S(1)} %all_to_all.15.received, bf16[32,40,128]{2,1,0:T(8,128)(2,1)S(1)} %collective-permute-done.3.refs_0_, bf16[4,256,512]{2,1,0:T(8,128)(2,1)S(1)} %copy-done.2, bf16[2,512,256]{2,1,0:T(8,128)(2,1)S(1)} %copy-done.3, ...), custom_call_target="tpu_custom_call" | custom-call | flops 1610612736 | bytes 4194304 | tf_op jit(solution)/shard_map/exchange_1/pallas_call | solution.py:329
  45.8 0.7 collective-permute-start.4
  46.7 2.2 %exchange_2.1.refs_6_ = f32[32,4,8,128]{3,2,1,0:T(8,128)S(1)} custom-call(s32[1,16]{1,0:T(1,128)S(1)} %bitcast.11, bf16[32,72,128]{2,1,0:T(8,128)(2,1)S(1)} %all_to_all.15.received, bf16[32,16,128]{2,1,0:T(8,128)(2,1)S(1)} %collective-permute-done.1.refs_0_, bf16[32,16,128]{2,1,0:T(8,128)(2,1)S(1)} %collective-permute-done.2.refs_1_, ...), custom_call_target="tpu_custom_call" | custom-call | flops 1610612736 | bytes 4194304 | tf_op jit(solution)/shard_map/exchange_2/pallas_call | solution.py:329
  48.9 3.2 %exchange_3.1 = (bf16[32,48,128]{2,1,0:T(8,128)(2,1)}, f32[8,128]{1,0:T(8,128)S(1)}) custom-call(s32[1,16]{1,0:T(1,128)S(1)} %bitcast.12, bf16[32,72,128]{2,1,0:T(8,128)(2,1)S(1)} %all_to_all.15.received, bf16[32,16,128]{2,1,0:T(8,128)(2,1)S(1)} %collective-permute-done.4.refs_0_, bf16[32,16,128]{2,1,0:T(8,128)(2,1)S(1)} %collective-permute-done.5.refs_1_, ...), custom_call_target="tpu_custom_call" | custom-call | flops 1610612736 | bytes 4194304 | tf_op jit(solution)/shard_map/exchange_3/pallas_call | solution.py:329
  52.1 3.8 %all-to-all-start.1 = ((bf16[32,48,128]{2,1,0:T(8,128)(2,1)}), bf16[32,48,128]{2,1,0:T(8,128)(2,1)S(1)}, u32[]{:S(2)}, u32[]{:S(2)}) async-start(bf16[32,48,128]{2,1,0:T(8,128)(2,1)} %get-tuple-element.19), calls=%async_computation.1 | async-start | bytes 786432 | tf_op jit(solution)/shard_map/all_to_all | solution.py:467
  56.0 0.5 collective-permute-start.7
  56.5 3.3 %collective-permute-start.8 = (f32[8,128]{1,0:T(8,128)S(1)}, f32[8,128]{1,0:T(8,128)S(1)}, u32[]{:S(2)}, u32[]{:S(2)}) collective-permute-start(f32[8,128]{1,0:T(8,128)S(1)} %get-tuple-element.20), channel_id=1, source_target_pairs={{0,96},{32,64},{64,32},{96,0},{128,224},{160,192},{192,160},{224,1... | collective-permute-start | bytes 12296 | tf_op jit(solution)/shard_map/ppermute | solution.py:468
  60.0 1.1 %collective-permute-done.8 = f32[8,128]{1,0:T(8,128)S(1)} collective-permute-done((f32[8,128]{1,0:T(8,128)S(1)}, f32[8,128]{1,0:T(8,128)S(1)}, u32[]{:S(2)}, u32[]{:S(2)}) %collective-permute-start.8) | collective-permute-done | bytes 4128 | tf_op jit(solution)/shard_map/ppermute | solution.py:468
  61.2 2.6 %collective-permute-start.9 = (f32[8,128]{1,0:T(8,128)S(1)}, f32[8,128]{1,0:T(8,128)S(1)}, u32[]{:S(2)}, u32[]{:S(2)}) collective-permute-start(f32[8,128]{1,0:T(8,128)S(1)} %add_add_fusion), channel_id=1, source_target_pairs={{0,128},{32,160},{64,192},{96,224},{128,0},{160,32},{192,64},{224,... | collective-permute-start | bytes 12296 | tf_op jit(solution)/shard_map/ppermute | solution.py:468
  63.8 1.6 %collective-permute-done.9 = f32[8,128]{1,0:T(8,128)S(1)} collective-permute-done((f32[8,128]{1,0:T(8,128)S(1)}, f32[8,128]{1,0:T(8,128)S(1)}, u32[]{:S(2)}, u32[]{:S(2)}) %collective-permute-start.9) | collective-permute-done | bytes 4128 | tf_op jit(solution)/shard_map/ppermute | solution.py:468
  65.4 4.7 %all-to-all-done.1 = bf16[32,48,128]{2,1,0:T(8,128)(2,1)S(1)} async-done(((bf16[32,48,128]{2,1,0:T(8,128)(2,1)}), bf16[32,48,128]{2,1,0:T(8,128)(2,1)S(1)}, u32[]{:S(2)}, u32[]{:S(2)}) %all-to-all-start.1) | async-done | bytes 393248 | tf_op jit(solution)/shard_map/all_to_all | solution.py:467
  70.1 0.8 finish.1
  70.9 13.7 %all_to_all.16.messages = f32[32,4,128]{2,1,0:T(4,128)S(1)} all-to-all(f32[32,4,128]{2,1,0:T(4,128)S(1)} %get-tuple-element.22), channel_id=1, replica_groups=mesh['ka'=8,'ga'=32] {'ga'}, dimensions={0} | all-to-all | bytes 131072 | tf_op jit(solution)/shard_map/all_to_all | solution.py:473
  84.6 0.8 close.1
  (25 shorter events, 0.8 us)
Async XLA Ops:
  0.6 7.9 %collective-permute-start = (bf16[2,8,2,1,1024]{4,2,3,1,0:T(2,128)(2,1)}, bf16[2,8,2,1,1024]{4,2,3,1,0:T(2,128)(2,1)S(1)}, u32[]{:S(2)}, u32[]{:S(2)}) collective-permute-start(bf16[2,8,2,1,1024]{4,2,3,1,0:T(2,128)(2,1)} %param.7), channel_id=1, source_target_pairs={{0,32},{32,64},{64,96},{96,128},{128,160},{160,192},{192,224},{224... | collective-permute-start | bytes 196616 | tf_op jit(solution)/shard_map/ppermute | solution.py:447
  3.7 1.1 %copy-start = (s32[16,16]{1,0:T(8,128)S(1)}, s32[16,16]{1,0:T(8,128)}, u32[]{:S(2)}) copy-start(s32[16,16]{1,0:T(8,128)} %pair_slot.1) | copy-start | bytes 3076
  8.6 32.7 %copy-start.2 = (bf16[4,256,512]{2,1,0:T(8,128)(2,1)S(1)}, bf16[4,256,512]{2,1,0:T(8,128)(2,1)}, u32[]{:S(2)}) copy-start(bf16[4,256,512]{2,1,0:T(8,128)(2,1)} %constant.6.clone.refs_1_.refs_2_) | copy-start | bytes 3145732
  37.7 3.6 %copy-start.3 = (bf16[2,512,256]{2,1,0:T(8,128)(2,1)S(1)}, bf16[2,512,256]{2,1,0:T(8,128)(2,1)}, u32[]{:S(2)}) copy-start(bf16[2,512,256]{2,1,0:T(8,128)(2,1)} %constant.7.clone.refs_2_.refs_3_) | copy-start | bytes 1572868
  37.8 3.6 %copy-start.4 = (f32[2,128,128]{2,1,0:T(8,128)S(1)}, f32[2,128,128]{2,1,0:T(8,128)}, u32[]{:S(2)}) copy-start(f32[2,128,128]{2,1,0:T(8,128)} %constant.8.clone.refs_3_.refs_4_) | copy-start | bytes 393220
  37.8 3.6 %collective-permute-start.3 = (bf16[32,40,128]{2,1,0:T(8,128)(2,1)S(1)}, bf16[32,40,128]{2,1,0:T(8,128)(2,1)S(1)}, u32[]{:S(2)}, u32[]{:S(2)}) collective-permute-start(bf16[32,40,128]{2,1,0:T(8,128)(2,1)S(1)} %slice.14), channel_id=1, source_target_pairs={{0,1},{1,0},{2,3},{3,2},{4,5},{5,4},{6,7},{7,6},{8,9},{9,8},{10,11... | collective-permute-start | bytes 983048 | tf_op jit(solution)/shard_map/ppermute | solution.py:455
  40.0 5.8 %collective-permute-start.1 = (bf16[32,16,128]{2,1,0:T(8,128)(2,1)S(1)}, bf16[32,16,128]{2,1,0:T(8,128)(2,1)S(1)}, u32[]{:S(2)}, u32[]{:S(2)}) collective-permute-start(bf16[32,16,128]{2,1,0:T(8,128)(2,1)S(1)} %get-tuple-element.29), channel_id=1, source_target_pairs={{0,16},{1,17},{2,18},{3,19},{4,20},{5,21},{6,22},{7,23},{8,24},{9,... | collective-permute-start | bytes 393224 | tf_op jit(solution)/shard_map/ppermute | solution.py:455
  40.5 0.9 %copy-start.1 = (s32[16]{0:T(128)S(1)}, s32[16]{0:T(128)}, u32[]{:S(2)}) copy-start(s32[16]{0:T(128)} %param.8) | copy-start | bytes 196
  40.5 5.3 %collective-permute-start.2 = (bf16[32,16,128]{2,1,0:T(8,128)(2,1)S(1)}, bf16[32,16,128]{2,1,0:T(8,128)(2,1)S(1)}, u32[]{:S(2)}, u32[]{:S(2)}) collective-permute-start(bf16[32,16,128]{2,1,0:T(8,128)(2,1)S(1)} %get-tuple-element.28), channel_id=1, source_target_pairs={{0,2},{1,3},{2,0},{3,1},{4,6},{5,7},{6,4},{7,5},{8,10},{9,11},{10,... | collective-permute-start | bytes 393224 | tf_op jit(solution)/shard_map/ppermute | solution.py:455
  45.8 3.1 %collective-permute-start.4 = (bf16[32,16,128]{2,1,0:T(8,128)(2,1)S(1)}, bf16[32,16,128]{2,1,0:T(8,128)(2,1)S(1)}, u32[]{:S(2)}, u32[]{:S(2)}) collective-permute-start(bf16[32,16,128]{2,1,0:T(8,128)(2,1)S(1)} %collective-permute-done.1.refs_0_), channel_id=1, source_target_pairs={{0,1},{1,0},{2,3},{3,2},{4,5},{5,4},{6,7},{7,6},{8,9},{9,8},{10,11... | collective-permute-start | bytes 393224 | tf_op jit(solution)/shard_map/ppermute | solution.py:455
  46.5 2.5 %collective-permute-start.5 = (bf16[32,16,128]{2,1,0:T(8,128)(2,1)S(1)}, bf16[32,16,128]{2,1,0:T(8,128)(2,1)S(1)}, u32[]{:S(2)}, u32[]{:S(2)}) collective-permute-start(bf16[32,16,128]{2,1,0:T(8,128)(2,1)S(1)} %collective-permute-done.2.refs_1_), channel_id=1, source_target_pairs={{0,1},{1,0},{2,3},{3,2},{4,5},{5,4},{6,7},{7,6},{8,9},{9,8},{10,11... | collective-permute-start | bytes 393224 | tf_op jit(solution)/shard_map/ppermute | solution.py:455
  52.1 18.0 %all-to-all-start.1 = ((bf16[32,48,128]{2,1,0:T(8,128)(2,1)}), bf16[32,48,128]{2,1,0:T(8,128)(2,1)S(1)}, u32[]{:S(2)}, u32[]{:S(2)}) async-start(bf16[32,48,128]{2,1,0:T(8,128)(2,1)} %get-tuple-element.19), calls=%async_computation.1 | async-start | bytes 786432 | tf_op jit(solution)/shard_map/all_to_all | solution.py:467
  55.9 3.9 %collective-permute-start.6 = (f32[8,128]{1,0:T(8,128)S(1)}, f32[8,128]{1,0:T(8,128)S(1)}, u32[]{:S(2)}, u32[]{:S(2)}) collective-permute-start(f32[8,128]{1,0:T(8,128)S(1)} %get-tuple-element.20), channel_id=1, source_target_pairs={{0,32},{32,0},{64,96},{96,64},{128,160},{160,128},{192,224},{224,1... | collective-permute-start | bytes 12296 | tf_op jit(solution)/shard_map/ppermute | solution.py:468
  56.0 4.0 %collective-permute-start.7 = (f32[8,128]{1,0:T(8,128)S(1)}, f32[8,128]{1,0:T(8,128)S(1)}, u32[]{:S(2)}, u32[]{:S(2)}) collective-permute-start(f32[8,128]{1,0:T(8,128)S(1)} %get-tuple-element.20), channel_id=1, source_target_pairs={{0,64},{32,96},{64,0},{96,32},{128,192},{160,224},{192,128},{224,1... | collective-permute-start | bytes 12296 | tf_op jit(solution)/shard_map/ppermute | solution.py:468
  56.5 4.6 %collective-permute-start.8 = (f32[8,128]{1,0:T(8,128)S(1)}, f32[8,128]{1,0:T(8,128)S(1)}, u32[]{:S(2)}, u32[]{:S(2)}) collective-permute-start(f32[8,128]{1,0:T(8,128)S(1)} %get-tuple-element.20), channel_id=1, source_target_pairs={{0,96},{32,64},{64,32},{96,0},{128,224},{160,192},{192,160},{224,1... | collective-permute-start | bytes 12296 | tf_op jit(solution)/shard_map/ppermute | solution.py:468
  61.2 4.3 %collective-permute-start.9 = (f32[8,128]{1,0:T(8,128)S(1)}, f32[8,128]{1,0:T(8,128)S(1)}, u32[]{:S(2)}, u32[]{:S(2)}) collective-permute-start(f32[8,128]{1,0:T(8,128)S(1)} %add_add_fusion), channel_id=1, source_target_pairs={{0,128},{32,160},{64,192},{96,224},{128,0},{160,32},{192,64},{224,... | collective-permute-start | bytes 12296 | tf_op jit(solution)/shard_map/ppermute | solution.py:468

commit v6 on v5

--- a/solution.py
+++ b/solution.py
@@ -7,6 +7,7 @@
 from jax.experimental import pallas as pl
 from jax.experimental.pallas import tpu as pltpu
 from jax.sharding import PartitionSpec as P
+
 
 highest = lax.Precision.HIGHEST
 f32 = jnp.float32
@@ -336,7 +337,6 @@
         cost_estimate=pl.CostEstimate(
             flops=2 * 12 * 2 * 512 * 256 * 256, bytes_accessed=4 << 20, transcendentals=0
         ),
-        name=("exchange_0", "exchange_1", "exchange_2", "exchange_3")[call],
     )(*operands)
 
 
@@ -464,10 +464,13 @@
     (total,) = exchange(scale, 2, counts, received, (next_y, next_z), tables, screen, total)
     leaving, energy = exchange(scale, 3, counts, received, far, tables, screen, total)
 
+    def shown_energy(value, bit):
+        return lax.ppermute(value, "ka", [(i, i ^ bit) for i in range(groups)])
+
+    first = shown_energy(energy, 1)
     returned = lax.all_to_all(leaving, "ga", 0, 0, tiled=True)
-    shown_energy = lambda value, bit: lax.ppermute(value, "ka", [(i, i ^ bit) for i in range(groups)])
-    near = [shown_energy(energy, bit) for bit in (1, 2, 3)]
-    energy = (energy + near[0]) + (near[1] + near[2])
+    energy = energy + first
+    energy = energy + shown_energy(energy, 2)
     energy = energy + shown_energy(energy, 4)
     vectors, message = finish(returned.reshape(2, 4, 2, 2, 48, 128), orbitals, energy)
     matrix, energy = close(lax.all_to_all(message, "ga", 0, 0, tiled=True))

time: 85.8 us -> 88 us (1.026)
  waiting for transfers between devices: 10.7 us -> 14.5 us
  starting transfers between devices: 16.9 us -> 13.1 us
  blocking collectives: 42.8 us -> 45.1 us
    ppermute x4 -> x3, waiting for transfers between devices: 2.93 us -> 8.65 us  [shown_energy(): return lax.ppermute(value, 'ka', [(i, i ^ bit) for i in range(groups)])]
    ppermute x4 -> x3, starting transfers between devices: 6.56 us -> 2.72 us  [shown_energy(): return lax.ppermute(value, 'ka', [(i, i ^ bit) for i in range(groups)])]
    all_to_all x1, blocking collectives: 13.7 us -> 16 us  [on_device(): matrix, energy = close(lax.all_to_all(message, 'ga', 0, 0, tiled=True))]
    all_to_all x1, waiting for transfers between devices: 4.67 us -> 2.8 us  [on_device(): returned = lax.all_to_all(leaving, 'ga', 0, 0, tiled=True)]
  transfers between devices with their start and end apart: 11 -> 10, of which waited for: 5 -> 5; matrix products, arithmetic and copies ran while one was open for 2% -> 2% of each run, Pallas kernels for 8% -> 8%
where the time goes in v6:
time: 88 us; the launch traced here: 87.7 us
  blocking collectives  45.1 us (51%)
  waiting for transfers between devices  14.5 us (16%)
  starting transfers between devices  13.1 us (15%)
  Pallas kernels  12.1 us (14%)
  local copies, waits for them, and re-layouts  2.11 us (2%)
    all_to_all x1, blocking collectives, on_device(): received = lax.all_to_all(packed, 'ga', 0, 0, tiled=True)  29.1 us
    all_to_all x1, blocking collectives, on_device(): matrix, energy = close(lax.all_to_all(message, 'ga', 0, 0, tiled=True))  16 us
    pallas_call x4, Pallas kernels, exchange(): pl.pallas_call(functools.partial(exchange_kernel, scale, call), out_shape...  9.74 us
    ppermute x3, waiting for transfers between devices, shown_energy(): return lax.ppermute(value, 'ka', [(i, i ^ bit) for i in range(groups)])  8.65 us
    ppermute x5, starting transfers between devices, shown(): return lax.ppermute(value, 'ga', [(i, i ^ bit) for i in range(32)])  4.48 us
    all_to_all x1, starting transfers between devices, on_device(): returned = lax.all_to_all(leaving, 'ga', 0, 0, tiled=True)  3.76 us
    ppermute x1, waiting for transfers between devices, on_device(): lax.ppermute(orbitals, 'ka', [(i, (i + 1) % groups) for i in range(groups)])  3.03 us
    all_to_all x1, waiting for transfers between devices, on_device(): returned = lax.all_to_all(leaving, 'ga', 0, 0, tiled=True)  2.8 us
  transfers between devices with their start and end apart: 10, of which 5 were waited for; matrix products, arithmetic and copies ran while one was open for 2% of the time, Pallas kernels for 8%

profile of v6, /device:TPU:1, one launch (start us, length us, event | category | flops | bytes accessed | tf_op | source)
XLA Modules:
  0.0 87.7 jit_solution(3463025051693290000)
XLA Ops:
  0.6 2.1 %collective-permute-start = (bf16[2,8,2,1,1024]{4,2,3,1,0:T(2,128)(2,1)}, bf16[2,8,2,1,1024]{4,2,3,1,0:T(2,128)(2,1)S(1)}, u32[]{:S(2)}, u32[]{:S(2)}) collective-permute-start(bf16[2,8,2,1,1024]{4,2,3,1,0:T(2,128)(2,1)} %param.7), channel_id=1, source_target_pairs={{0,32},{32,64},{64,96},{96,128},{128,160},{160,192},{192,224},{224... | collective-permute-start | bytes 196616 | tf_op jit(solution)/shard_map/ppermute | solution.py:447
  2.7 0.9 %reshape.25.orbitals = bf16[16,16,128]{2,1,0:T(8,128)(2,1)S(1)} reshape(bf16[2,8,2,1,1024]{4,2,3,1,0:T(2,128)(2,1)} %param.7) | data formatting | bytes 131072 | tf_op jit(solution)/shard_map/reshape | solution.py:450
  3.7 1.1 %reshape.27.kernel = f32[16,8,128]{2,1,0:T(8,128)S(1)} reshape(f32[16,32,32]{2,1,0:T(8,128)} %param.10) | data formatting | bytes 131072 | tf_op jit(solution)/shard_map/reshape | solution.py:448
  4.8 0.7 choose.1.chosen
  5.5 3.0 %collective-permute-done = bf16[2,8,2,1,1024]{4,2,3,1,0:T(2,128)(2,1)S(1)} collective-permute-done((bf16[2,8,2,1,1024]{4,2,3,1,0:T(2,128)(2,1)}, bf16[2,8,2,1,1024]{4,2,3,1,0:T(2,128)(2,1)S(1)}, u32[]{:S(2)}, u32[]{:S(2)}) %collective-permute-start) | collective-permute-done | bytes 65568 | tf_op jit(solution)/shard_map/ppermute | solution.py:447
  8.6 29.1 %all_to_all.15.received = bf16[32,72,128]{2,1,0:T(8,128)(2,1)S(1)} all-to-all(bf16[32,72,128]{2,1,0:T(8,128)(2,1)S(1)} %pack.1), channel_id=1, replica_groups=mesh['ka'=8,'ga'=32] {'ga'}, dimensions={0} | all-to-all | bytes 1179648 | tf_op jit(solution)/shard_map/all_to_all | solution.py:452
  37.8 2.1 %collective-permute-start.3 = (bf16[32,40,128]{2,1,0:T(8,128)(2,1)S(1)}, bf16[32,40,128]{2,1,0:T(8,128)(2,1)S(1)}, u32[]{:S(2)}, u32[]{:S(2)}) collective-permute-start(bf16[32,40,128]{2,1,0:T(8,128)(2,1)S(1)} %slice.14), channel_id=1, source_target_pairs={{0,1},{1,0},{2,3},{3,2},{4,5},{5,4},{6,7},{7,6},{8,9},{9,8},{10,11... | collective-permute-start | bytes 983048 | tf_op jit(solution)/shard_map/ppermute | solution.py:455
  40.0 0.5 collective-permute-start.1
  40.5 0.9 %collective-permute-start.2 = (bf16[32,16,128]{2,1,0:T(8,128)(2,1)S(1)}, bf16[32,16,128]{2,1,0:T(8,128)(2,1)S(1)}, u32[]{:S(2)}, u32[]{:S(2)}) collective-permute-start(bf16[32,16,128]{2,1,0:T(8,128)(2,1)S(1)} %get-tuple-element.28), channel_id=1, source_target_pairs={{0,2},{1,3},{2,0},{3,1},{4,6},{5,7},{6,4},{7,5},{8,10},{9,11},{10,... | collective-permute-start | bytes 393224 | tf_op jit(solution)/shard_map/ppermute | solution.py:455
  41.4 2.2 %shard_map.94 = (f32[32,4,8,128]{3,2,1,0:T(8,128)S(1)}, f32[2,128,128]{2,1,0:T(8,128)S(1)}) custom-call(s32[1,16]{1,0:T(1,128)S(1)} %bitcast.9, bf16[32,72,128]{2,1,0:T(8,128)(2,1)S(1)} %all_to_all.15.received, bf16[32,40,128]{2,1,0:T(8,128)(2,1)S(1)} %collective-permute-done.3.refs_0_, bf16[4,256,512]{2,1,0:T(8,128)(2,1)S(1)} %copy-done.2, ...), custom_call_target="tpu_custom_call" | custom-call | flops 1610612736 | bytes 4194304 | tf_op jit(solution)/shard_map/pallas_call | solution.py:330
  43.6 2.2 %shard_map.95.refs_6_ = f32[32,4,8,128]{3,2,1,0:T(8,128)S(1)} custom-call(s32[1,16]{1,0:T(1,128)S(1)} %bitcast.10, bf16[32,72,128]{2,1,0:T(8,128)(2,1)S(1)} %all_to_all.15.received, bf16[32,40,128]{2,1,0:T(8,128)(2,1)S(1)} %collective-permute-done.3.refs_0_, bf16[4,256,512]{2,1,0:T(8,128)(2,1)S(1)} %copy-done.2, bf16[2,512,256]{2,1,0:T(8,128)(2,1)S(1)} %copy-done.3, ...), custom_call_target="tpu_custom_call" | custom-call | flops 1610612736 | bytes 4194304 | tf_op jit(solution)/shard_map/pallas_call | solution.py:330
  45.8 0.7 collective-permute-start.4
  46.5 0.3 collective-permute-start.5
  46.7 2.2 %shard_map.96.refs_6_ = f32[32,4,8,128]{3,2,1,0:T(8,128)S(1)} custom-call(s32[1,16]{1,0:T(1,128)S(1)} %bitcast.11, bf16[32,72,128]{2,1,0:T(8,128)(2,1)S(1)} %all_to_all.15.received, bf16[32,16,128]{2,1,0:T(8,128)(2,1)S(1)} %collective-permute-done.1.refs_0_, bf16[32,16,128]{2,1,0:T(8,128)(2,1)S(1)} %collective-permute-done.2.refs_1_, ...), custom_call_target="tpu_custom_call" | custom-call | flops 1610612736 | bytes 4194304 | tf_op jit(solution)/shard_map/pallas_call | solution.py:330
  48.9 3.2 %shard_map.97 = (bf16[32,48,128]{2,1,0:T(8,128)(2,1)}, f32[8,128]{1,0:T(8,128)S(1)}) custom-call(s32[1,16]{1,0:T(1,128)S(1)} %bitcast.12, bf16[32,72,128]{2,1,0:T(8,128)(2,1)S(1)} %all_to_all.15.received, bf16[32,16,128]{2,1,0:T(8,128)(2,1)S(1)} %collective-permute-done.4.refs_0_, bf16[32,16,128]{2,1,0:T(8,128)(2,1)S(1)} %collective-permute-done.5.refs_1_, ...), custom_call_target="tpu_custom_call" | custom-call | flops 1610612736 | bytes 4194304 | tf_op jit(solution)/shard_map/pallas_call | solution.py:330
  52.1 3.8 %all-to-all-start.1 = ((bf16[32,48,128]{2,1,0:T(8,128)(2,1)}), bf16[32,48,128]{2,1,0:T(8,128)(2,1)S(1)}, u32[]{:S(2)}, u32[]{:S(2)}) async-start(bf16[32,48,128]{2,1,0:T(8,128)(2,1)} %get-tuple-element.19), calls=%async_computation.1 | async-start | bytes 786432 | tf_op jit(solution)/shard_map/all_to_all | solution.py:471
  56.0 2.7 %collective-permute-done.6 = f32[8,128]{1,0:T(8,128)S(1)} collective-permute-done((f32[8,128]{1,0:T(8,128)S(1)}, f32[8,128]{1,0:T(8,128)S(1)}, u32[]{:S(2)}, u32[]{:S(2)}) %collective-permute-start.6) | collective-permute-done | bytes 4128 | tf_op jit(solution)/shard_map/ppermute | solution.py:468
  58.7 4.3 %collective-permute-done.7 = f32[8,128]{1,0:T(8,128)S(1)} collective-permute-done((f32[8,128]{1,0:T(8,128)S(1)}, f32[8,128]{1,0:T(8,128)S(1)}, u32[]{:S(2)}, u32[]{:S(2)}) %collective-permute-start.7) | collective-permute-done | bytes 4128 | tf_op jit(solution)/shard_map/ppermute | solution.py:468
  63.0 2.6 %collective-permute-start.8 = (f32[8,128]{1,0:T(8,128)S(1)}, f32[8,128]{1,0:T(8,128)S(1)}, u32[]{:S(2)}, u32[]{:S(2)}) collective-permute-start(f32[8,128]{1,0:T(8,128)S(1)} %add.10), channel_id=1, source_target_pairs={{0,128},{32,160},{64,192},{96,224},{128,0},{160,32},{192,64},{224,... | collective-permute-start | bytes 12296 | tf_op jit(solution)/shard_map/ppermute | solution.py:468
  65.6 1.7 %collective-permute-done.8 = f32[8,128]{1,0:T(8,128)S(1)} collective-permute-done((f32[8,128]{1,0:T(8,128)S(1)}, f32[8,128]{1,0:T(8,128)S(1)}, u32[]{:S(2)}, u32[]{:S(2)}) %collective-permute-start.8) | collective-permute-done | bytes 4128 | tf_op jit(solution)/shard_map/ppermute | solution.py:468
  67.3 2.8 %all-to-all-done.1 = bf16[32,48,128]{2,1,0:T(8,128)(2,1)S(1)} async-done(((bf16[32,48,128]{2,1,0:T(8,128)(2,1)}), bf16[32,48,128]{2,1,0:T(8,128)(2,1)S(1)}, u32[]{:S(2)}, u32[]{:S(2)}) %all-to-all-start.1) | async-done | bytes 393248 | tf_op jit(solution)/shard_map/all_to_all | solution.py:471
  70.1 0.8 finish.1
  70.9 16.0 %all_to_all.16.messages = f32[32,4,128]{2,1,0:T(4,128)S(1)} all-to-all(f32[32,4,128]{2,1,0:T(4,128)S(1)} %get-tuple-element.22), channel_id=1, replica_groups=mesh['ka'=8,'ga'=32] {'ga'}, dimensions={0} | all-to-all | bytes 131072 | tf_op jit(solution)/shard_map/all_to_all | solution.py:476
  86.9 0.8 close.1
  (24 shorter events, 0.3 us)
Async XLA Ops:
  0.6 7.9 %collective-permute-start = (bf16[2,8,2,1,1024]{4,2,3,1,0:T(2,128)(2,1)}, bf16[2,8,2,1,1024]{4,2,3,1,0:T(2,128)(2,1)S(1)}, u32[]{:S(2)}, u32[]{:S(2)}) collective-permute-start(bf16[2,8,2,1,1024]{4,2,3,1,0:T(2,128)(2,1)} %param.7), channel_id=1, source_target_pairs={{0,32},{32,64},{64,96},{96,128},{128,160},{160,192},{192,224},{224... | collective-permute-start | bytes 196616 | tf_op jit(solution)/shard_map/ppermute | solution.py:447
  3.7 1.1 %copy-start = (s32[16,16]{1,0:T(8,128)S(1)}, s32[16,16]{1,0:T(8,128)}, u32[]{:S(2)}) copy-start(s32[16,16]{1,0:T(8,128)} %pair_slot.1) | copy-start | bytes 3076
  8.6 32.7 %copy-start.2 = (bf16[4,256,512]{2,1,0:T(8,128)(2,1)S(1)}, bf16[4,256,512]{2,1,0:T(8,128)(2,1)}, u32[]{:S(2)}) copy-start(bf16[4,256,512]{2,1,0:T(8,128)(2,1)} %constant.6.clone.refs_1_.refs_2_) | copy-start | bytes 3145732
  37.7 3.6 %copy-start.3 = (bf16[2,512,256]{2,1,0:T(8,128)(2,1)S(1)}, bf16[2,512,256]{2,1,0:T(8,128)(2,1)}, u32[]{:S(2)}) copy-start(bf16[2,512,256]{2,1,0:T(8,128)(2,1)} %constant.7.clone.refs_2_.refs_3_) | copy-start | bytes 1572868
  37.8 3.6 %copy-start.4 = (f32[2,128,128]{2,1,0:T(8,128)S(1)}, f32[2,128,128]{2,1,0:T(8,128)}, u32[]{:S(2)}) copy-start(f32[2,128,128]{2,1,0:T(8,128)} %constant.8.clone.refs_3_.refs_4_) | copy-start | bytes 393220
  37.8 3.6 %collective-permute-start.3 = (bf16[32,40,128]{2,1,0:T(8,128)(2,1)S(1)}, bf16[32,40,128]{2,1,0:T(8,128)(2,1)S(1)}, u32[]{:S(2)}, u32[]{:S(2)}) collective-permute-start(bf16[32,40,128]{2,1,0:T(8,128)(2,1)S(1)} %slice.14), channel_id=1, source_target_pairs={{0,1},{1,0},{2,3},{3,2},{4,5},{5,4},{6,7},{7,6},{8,9},{9,8},{10,11... | collective-permute-start | bytes 983048 | tf_op jit(solution)/shard_map/ppermute | solution.py:455
  40.0 5.8 %collective-permute-start.1 = (bf16[32,16,128]{2,1,0:T(8,128)(2,1)S(1)}, bf16[32,16,128]{2,1,0:T(8,128)(2,1)S(1)}, u32[]{:S(2)}, u32[]{:S(2)}) collective-permute-start(bf16[32,16,128]{2,1,0:T(8,128)(2,1)S(1)} %get-tuple-element.29), channel_id=1, source_target_pairs={{0,16},{1,17},{2,18},{3,19},{4,20},{5,21},{6,22},{7,23},{8,24},{9,... | collective-permute-start | bytes 393224 | tf_op jit(solution)/shard_map/ppermute | solution.py:455
  40.5 0.9 %copy-start.1 = (s32[16]{0:T(128)S(1)}, s32[16]{0:T(128)}, u32[]{:S(2)}) copy-start(s32[16]{0:T(128)} %param.8) | copy-start | bytes 196
  40.5 5.3 %collective-permute-start.2 = (bf16[32,16,128]{2,1,0:T(8,128)(2,1)S(1)}, bf16[32,16,128]{2,1,0:T(8,128)(2,1)S(1)}, u32[]{:S(2)}, u32[]{:S(2)}) collective-permute-start(bf16[32,16,128]{2,1,0:T(8,128)(2,1)S(1)} %get-tuple-element.28), channel_id=1, source_target_pairs={{0,2},{1,3},{2,0},{3,1},{4,6},{5,7},{6,4},{7,5},{8,10},{9,11},{10,... | collective-permute-start | bytes 393224 | tf_op jit(solution)/shard_map/ppermute | solution.py:455
  45.8 3.1 %collective-permute-start.4 = (bf16[32,16,128]{2,1,0:T(8,128)(2,1)S(1)}, bf16[32,16,128]{2,1,0:T(8,128)(2,1)S(1)}, u32[]{:S(2)}, u32[]{:S(2)}) collective-permute-start(bf16[32,16,128]{2,1,0:T(8,128)(2,1)S(1)} %collective-permute-done.1.refs_0_), channel_id=1, source_target_pairs={{0,1},{1,0},{2,3},{3,2},{4,5},{5,4},{6,7},{7,6},{8,9},{9,8},{10,11... | collective-permute-start | bytes 393224 | tf_op jit(solution)/shard_map/ppermute | solution.py:455
  46.5 2.5 %collective-permute-start.5 = (bf16[32,16,128]{2,1,0:T(8,128)(2,1)S(1)}, bf16[32,16,128]{2,1,0:T(8,128)(2,1)S(1)}, u32[]{:S(2)}, u32[]{:S(2)}) collective-permute-start(bf16[32,16,128]{2,1,0:T(8,128)(2,1)S(1)} %collective-permute-done.2.refs_1_), channel_id=1, source_target_pairs={{0,1},{1,0},{2,3},{3,2},{4,5},{5,4},{6,7},{7,6},{8,9},{9,8},{10,11... | collective-permute-start | bytes 393224 | tf_op jit(solution)/shard_map/ppermute | solution.py:455
  52.1 18.0 %all-to-all-start.1 = ((bf16[32,48,128]{2,1,0:T(8,128)(2,1)}), bf16[32,48,128]{2,1,0:T(8,128)(2,1)S(1)}, u32[]{:S(2)}, u32[]{:S(2)}) async-start(bf16[32,48,128]{2,1,0:T(8,128)(2,1)} %get-tuple-element.19), calls=%async_computation.1 | async-start | bytes 786432 | tf_op jit(solution)/shard_map/all_to_all | solution.py:471
  55.9 2.8 %collective-permute-start.6 = (f32[8,128]{1,0:T(8,128)S(1)}, f32[8,128]{1,0:T(8,128)S(1)}, u32[]{:S(2)}, u32[]{:S(2)}) collective-permute-start(f32[8,128]{1,0:T(8,128)S(1)} %get-tuple-element.20), channel_id=1, source_target_pairs={{0,32},{32,0},{64,96},{96,64},{128,160},{160,128},{192,224},{224,1... | collective-permute-start | bytes 12296 | tf_op jit(solution)/shard_map/ppermute | solution.py:468
  58.7 4.3 %collective-permute-start.7 = (f32[8,128]{1,0:T(8,128)S(1)}, f32[8,128]{1,0:T(8,128)S(1)}, u32[]{:S(2)}, u32[]{:S(2)}) collective-permute-start(f32[8,128]{1,0:T(8,128)S(1)} %add.9), channel_id=1, source_target_pairs={{0,64},{32,96},{64,0},{96,32},{128,192},{160,224},{192,128},{224,1... | collective-permute-start | bytes 12296 | tf_op jit(solution)/shard_map/ppermute | solution.py:468
  63.0 4.3 %collective-permute-start.8 = (f32[8,128]{1,0:T(8,128)S(1)}, f32[8,128]{1,0:T(8,128)S(1)}, u32[]{:S(2)}, u32[]{:S(2)}) collective-permute-start(f32[8,128]{1,0:T(8,128)S(1)} %add.10), channel_id=1, source_target_pairs={{0,128},{32,160},{64,192},{96,224},{128,0},{160,32},{192,64},{224,... | collective-permute-start | bytes 12296 | tf_op jit(solution)/shard_map/ppermute | solution.py:468

commit v7 on v6

--- a/solution.py
+++ b/solution.py
@@ -235,7 +235,7 @@
     else:
         screen, held, total = rest[:3]
         if call == 3:
-            leaving, energy, total = rest[2:]
+            left_memory, energy, total, leaving, sent = rest[2:]
     k2_at = lax.rem(group + 8 - k2 // 2, 8) * 2 + k2 % 2
     core_from = 1 - core if call % 2 else core
     bands = (
@@ -305,6 +305,8 @@
             leaving[rows, 32:48] = jnp.concatenate(codes, axis=1).astype(bf16)
 
     if call == 3:
+        copy = pltpu.make_async_copy(leaving, left_memory, sent)
+        copy.start()
         count = count_of(group * 2 + k)
         energy_sum = jnp.zeros((8, 128), f32)
         for a in range(2):
@@ -313,6 +315,7 @@
             both = own[:, :8] * total[:, 2 * a] + own[:, 8:] * total[:, 2 * a + 1]
             energy_sum += jnp.sum(both, axis=0) * occupied
         energy[...] = jnp.full((8, 128), jnp.sum(energy_sum) * (1.0 / (32.0 * 32768.0)), f32)
+        copy.wait()
 
 
 SOURCES = (1, 1, 2, 2)
@@ -324,14 +327,18 @@
     shapes, scratch = [jax.ShapeDtypeStruct((32, 4, 8, 128), f32)], []
     if call == 3:
         shapes = [jax.ShapeDtypeStruct((32, 48, 128), bf16), jax.ShapeDtypeStruct((8, 128), f32)]
-        scratch = [pltpu.VMEM((32, 4, 8, 128), f32)]
+        scratch = [
+            pltpu.VMEM((32, 4, 8, 128), f32),
+            pltpu.VMEM((32, 48, 128), bf16),
+            pltpu.SemaphoreType.DMA(()),
+        ]
     if call == 0:
         shapes.append(jax.ShapeDtypeStruct((2, 128, 128), f32))
     return pl.pallas_call(
         functools.partial(exchange_kernel, scale, call),
         out_shape=tuple(shapes),
         in_specs=[vmem] * len(operands),
-        out_specs=(vmem,) * len(shapes),
+        out_specs=(pl.BlockSpec(memory_space=pl.ANY) if call == 3 else vmem, *(vmem,) * (len(shapes) - 1)),
         scratch_shapes=scratch,
         compiler_params=pltpu.CompilerParams(vmem_limit_bytes=24 * MIB),
         cost_estimate=pl.CostEstimate(

time: 88 us -> 88 us (level)
  no operation moved by 1% of the time
where the time goes in v7:
time: 88 us; the launch traced here: 87.7 us
  blocking collectives  45.1 us (51%)
  waiting for transfers between devices  14.5 us (16%)
  starting transfers between devices  13.1 us (15%)
  Pallas kernels  12.1 us (14%)
  local copies, waits for them, and re-layouts  2.11 us (2%)
    all_to_all x1, blocking collectives, on_device(): received = lax.all_to_all(packed, 'ga', 0, 0, tiled=True)  29.1 us
    all_to_all x1, blocking collectives, on_device(): matrix, energy = close(lax.all_to_all(message, 'ga', 0, 0, tiled=True))  16 us
    pallas_call x4, Pallas kernels, exchange(): pl.pallas_call(functools.partial(exchange_kernel, scale, call), out_shape...  9.72 us
    ppermute x3, waiting for transfers between devices, shown_energy(): return lax.ppermute(value, 'ka', [(i, i ^ bit) for i in range(groups)])  8.65 us
    ppermute x5, starting transfers between devices, shown(): return lax.ppermute(value, 'ga', [(i, i ^ bit) for i in range(32)])  4.48 us
    all_to_all x1, starting transfers between devices, on_device(): returned = lax.all_to_all(leaving, 'ga', 0, 0, tiled=True)  3.77 us
    ppermute x1, waiting for transfers between devices, on_device(): lax.ppermute(orbitals, 'ka', [(i, (i + 1) % groups) for i in range(groups)])  3.03 us
    all_to_all x1, waiting for transfers between devices, on_device(): returned = lax.all_to_all(leaving, 'ga', 0, 0, tiled=True)  2.8 us
  transfers between devices with their start and end apart: 10, of which 5 were waited for; matrix products, arithmetic and copies ran while one was open for 2% of the time, Pallas kernels for 8%

profile of v7, /device:TPU:1, one launch (start us, length us, event | category | flops | bytes accessed | tf_op | source)
XLA Modules:
  0.0 87.7 jit_solution(3892100121070115034)
XLA Ops:
  0.6 2.1 %collective-permute-start = (bf16[2,8,2,1,1024]{4,2,3,1,0:T(2,128)(2,1)}, bf16[2,8,2,1,1024]{4,2,3,1,0:T(2,128)(2,1)S(1)}, u32[]{:S(2)}, u32[]{:S(2)}) collective-permute-start(bf16[2,8,2,1,1024]{4,2,3,1,0:T(2,128)(2,1)} %param.7), channel_id=1, source_target_pairs={{0,32},{32,64},{64,96},{96,128},{128,160},{160,192},{192,224},{224... | collective-permute-start | bytes 196616 | tf_op jit(solution)/shard_map/ppermute | solution.py:454
  2.7 0.9 %reshape.25.orbitals = bf16[16,16,128]{2,1,0:T(8,128)(2,1)S(1)} reshape(bf16[2,8,2,1,1024]{4,2,3,1,0:T(2,128)(2,1)} %param.7) | data formatting | bytes 131072 | tf_op jit(solution)/shard_map/reshape | solution.py:457
  3.7 1.1 %reshape.27.kernel = f32[16,8,128]{2,1,0:T(8,128)S(1)} reshape(f32[16,32,32]{2,1,0:T(8,128)} %param.10) | data formatting | bytes 131072 | tf_op jit(solution)/shard_map/reshape | solution.py:455
  4.8 0.7 choose.1.chosen
  5.5 3.0 %collective-permute-done = bf16[2,8,2,1,1024]{4,2,3,1,0:T(2,128)(2,1)S(1)} collective-permute-done((bf16[2,8,2,1,1024]{4,2,3,1,0:T(2,128)(2,1)}, bf16[2,8,2,1,1024]{4,2,3,1,0:T(2,128)(2,1)S(1)}, u32[]{:S(2)}, u32[]{:S(2)}) %collective-permute-start) | collective-permute-done | bytes 65568 | tf_op jit(solution)/shard_map/ppermute | solution.py:454
  8.6 29.1 %all_to_all.15.received = bf16[32,72,128]{2,1,0:T(8,128)(2,1)S(1)} all-to-all(bf16[32,72,128]{2,1,0:T(8,128)(2,1)S(1)} %pack.1), channel_id=1, replica_groups=mesh['ka'=8,'ga'=32] {'ga'}, dimensions={0} | all-to-all | bytes 1179648 | tf_op jit(solution)/shard_map/all_to_all | solution.py:459
  37.8 2.1 %collective-permute-start.3 = (bf16[32,40,128]{2,1,0:T(8,128)(2,1)S(1)}, bf16[32,40,128]{2,1,0:T(8,128)(2,1)S(1)}, u32[]{:S(2)}, u32[]{:S(2)}) collective-permute-start(bf16[32,40,128]{2,1,0:T(8,128)(2,1)S(1)} %slice.14), channel_id=1, source_target_pairs={{0,1},{1,0},{2,3},{3,2},{4,5},{5,4},{6,7},{7,6},{8,9},{9,8},{10,11... | collective-permute-start | bytes 983048 | tf_op jit(solution)/shard_map/ppermute | solution.py:462
  40.0 0.5 collective-permute-start.1
  40.5 0.9 %collective-permute-start.2 = (bf16[32,16,128]{2,1,0:T(8,128)(2,1)S(1)}, bf16[32,16,128]{2,1,0:T(8,128)(2,1)S(1)}, u32[]{:S(2)}, u32[]{:S(2)}) collective-permute-start(bf16[32,16,128]{2,1,0:T(8,128)(2,1)S(1)} %get-tuple-element.28), channel_id=1, source_target_pairs={{0,2},{1,3},{2,0},{3,1},{4,6},{5,7},{6,4},{7,5},{8,10},{9,11},{10,... | collective-permute-start | bytes 393224 | tf_op jit(solution)/shard_map/ppermute | solution.py:462
  41.4 2.2 %shard_map.94 = (f32[32,4,8,128]{3,2,1,0:T(8,128)S(1)}, f32[2,128,128]{2,1,0:T(8,128)S(1)}) custom-call(s32[1,16]{1,0:T(1,128)S(1)} %bitcast.9, bf16[32,72,128]{2,1,0:T(8,128)(2,1)S(1)} %all_to_all.15.received, bf16[32,40,128]{2,1,0:T(8,128)(2,1)S(1)} %collective-permute-done.3.refs_0_, bf16[4,256,512]{2,1,0:T(8,128)(2,1)S(1)} %copy-done.2, ...), custom_call_target="tpu_custom_call" | custom-call | flops 1610612736 | bytes 4194304 | tf_op jit(solution)/shard_map/pallas_call | solution.py:337
  43.6 2.2 %shard_map.95.refs_6_ = f32[32,4,8,128]{3,2,1,0:T(8,128)S(1)} custom-call(s32[1,16]{1,0:T(1,128)S(1)} %bitcast.10, bf16[32,72,128]{2,1,0:T(8,128)(2,1)S(1)} %all_to_all.15.received, bf16[32,40,128]{2,1,0:T(8,128)(2,1)S(1)} %collective-permute-done.3.refs_0_, bf16[4,256,512]{2,1,0:T(8,128)(2,1)S(1)} %copy-done.2, bf16[2,512,256]{2,1,0:T(8,128)(2,1)S(1)} %copy-done.3, ...), custom_call_target="tpu_custom_call" | custom-call | flops 1610612736 | bytes 4194304 | tf_op jit(solution)/shard_map/pallas_call | solution.py:337
  45.8 0.7 collective-permute-start.4
  46.5 0.3 collective-permute-start.5
  46.7 2.2 %shard_map.96.refs_6_ = f32[32,4,8,128]{3,2,1,0:T(8,128)S(1)} custom-call(s32[1,16]{1,0:T(1,128)S(1)} %bitcast.11, bf16[32,72,128]{2,1,0:T(8,128)(2,1)S(1)} %all_to_all.15.received, bf16[32,16,128]{2,1,0:T(8,128)(2,1)S(1)} %collective-permute-done.1.refs_0_, bf16[32,16,128]{2,1,0:T(8,128)(2,1)S(1)} %collective-permute-done.2.refs_1_, ...), custom_call_target="tpu_custom_call" | custom-call | flops 1610612736 | bytes 4194304 | tf_op jit(solution)/shard_map/pallas_call | solution.py:337
  48.9 3.2 %shard_map.97 = (bf16[32,48,128]{2,1,0:T(8,128)(2,1)}, f32[8,128]{1,0:T(8,128)S(1)}) custom-call(s32[1,16]{1,0:T(1,128)S(1)} %bitcast.12, bf16[32,72,128]{2,1,0:T(8,128)(2,1)S(1)} %all_to_all.15.received, bf16[32,16,128]{2,1,0:T(8,128)(2,1)S(1)} %collective-permute-done.4.refs_0_, bf16[32,16,128]{2,1,0:T(8,128)(2,1)S(1)} %collective-permute-done.5.refs_1_, ...), custom_call_target="tpu_custom_call" | custom-call | flops 1610612736 | bytes 4194304 | tf_op jit(solution)/shard_map/pallas_call | solution.py:337
  52.1 3.8 %all-to-all-start.1 = ((bf16[32,48,128]{2,1,0:T(8,128)(2,1)}), bf16[32,48,128]{2,1,0:T(8,128)(2,1)S(1)}, u32[]{:S(2)}, u32[]{:S(2)}) async-start(bf16[32,48,128]{2,1,0:T(8,128)(2,1)} %get-tuple-element.19), calls=%async_computation.1 | async-start | bytes 786432 | tf_op jit(solution)/shard_map/all_to_all | solution.py:478
  56.0 2.7 %collective-permute-done.6 = f32[8,128]{1,0:T(8,128)S(1)} collective-permute-done((f32[8,128]{1,0:T(8,128)S(1)}, f32[8,128]{1,0:T(8,128)S(1)}, u32[]{:S(2)}, u32[]{:S(2)}) %collective-permute-start.6) | collective-permute-done | bytes 4128 | tf_op jit(solution)/shard_map/ppermute | solution.py:475
  58.8 4.3 %collective-permute-done.7 = f32[8,128]{1,0:T(8,128)S(1)} collective-permute-done((f32[8,128]{1,0:T(8,128)S(1)}, f32[8,128]{1,0:T(8,128)S(1)}, u32[]{:S(2)}, u32[]{:S(2)}) %collective-permute-start.7) | collective-permute-done | bytes 4128 | tf_op jit(solution)/shard_map/ppermute | solution.py:475
  63.0 2.6 %collective-permute-start.8 = (f32[8,128]{1,0:T(8,128)S(1)}, f32[8,128]{1,0:T(8,128)S(1)}, u32[]{:S(2)}, u32[]{:S(2)}) collective-permute-start(f32[8,128]{1,0:T(8,128)S(1)} %add.10), channel_id=1, source_target_pairs={{0,128},{32,160},{64,192},{96,224},{128,0},{160,32},{192,64},{224,... | collective-permute-start | bytes 12296 | tf_op jit(solution)/shard_map/ppermute | solution.py:475
  65.6 1.7 %collective-permute-done.8 = f32[8,128]{1,0:T(8,128)S(1)} collective-permute-done((f32[8,128]{1,0:T(8,128)S(1)}, f32[8,128]{1,0:T(8,128)S(1)}, u32[]{:S(2)}, u32[]{:S(2)}) %collective-permute-start.8) | collective-permute-done | bytes 4128 | tf_op jit(solution)/shard_map/ppermute | solution.py:475
  67.3 2.8 %all-to-all-done.1 = bf16[32,48,128]{2,1,0:T(8,128)(2,1)S(1)} async-done(((bf16[32,48,128]{2,1,0:T(8,128)(2,1)}), bf16[32,48,128]{2,1,0:T(8,128)(2,1)S(1)}, u32[]{:S(2)}, u32[]{:S(2)}) %all-to-all-start.1) | async-done | bytes 393248 | tf_op jit(solution)/shard_map/all_to_all | solution.py:478
  70.1 0.8 finish.1
  70.9 16.0 %all_to_all.16.messages = f32[32,4,128]{2,1,0:T(4,128)S(1)} all-to-all(f32[32,4,128]{2,1,0:T(4,128)S(1)} %get-tuple-element.22), channel_id=1, replica_groups=mesh['ka'=8,'ga'=32] {'ga'}, dimensions={0} | all-to-all | bytes 131072 | tf_op jit(solution)/shard_map/all_to_all | solution.py:483
  86.9 0.8 close.1
  (24 shorter events, 0.3 us)
Async XLA Ops:
  0.6 7.9 %collective-permute-start = (bf16[2,8,2,1,1024]{4,2,3,1,0:T(2,128)(2,1)}, bf16[2,8,2,1,1024]{4,2,3,1,0:T(2,128)(2,1)S(1)}, u32[]{:S(2)}, u32[]{:S(2)}) collective-permute-start(bf16[2,8,2,1,1024]{4,2,3,1,0:T(2,128)(2,1)} %param.7), channel_id=1, source_target_pairs={{0,32},{32,64},{64,96},{96,128},{128,160},{160,192},{192,224},{224... | collective-permute-start | bytes 196616 | tf_op jit(solution)/shard_map/ppermute | solution.py:454
  3.7 1.1 %copy-start = (s32[16,16]{1,0:T(8,128)S(1)}, s32[16,16]{1,0:T(8,128)}, u32[]{:S(2)}) copy-start(s32[16,16]{1,0:T(8,128)} %pair_slot.1) | copy-start | bytes 3076
  8.6 32.7 %copy-start.2 = (bf16[4,256,512]{2,1,0:T(8,128)(2,1)S(1)}, bf16[4,256,512]{2,1,0:T(8,128)(2,1)}, u32[]{:S(2)}) copy-start(bf16[4,256,512]{2,1,0:T(8,128)(2,1)} %constant.6.clone.refs_1_.refs_2_) | copy-start | bytes 3145732
  37.7 3.6 %copy-start.3 = (bf16[2,512,256]{2,1,0:T(8,128)(2,1)S(1)}, bf16[2,512,256]{2,1,0:T(8,128)(2,1)}, u32[]{:S(2)}) copy-start(bf16[2,512,256]{2,1,0:T(8,128)(2,1)} %constant.7.clone.refs_2_.refs_3_) | copy-start | bytes 1572868
  37.8 3.6 %copy-start.4 = (f32[2,128,128]{2,1,0:T(8,128)S(1)}, f32[2,128,128]{2,1,0:T(8,128)}, u32[]{:S(2)}) copy-start(f32[2,128,128]{2,1,0:T(8,128)} %constant.8.clone.refs_3_.refs_4_) | copy-start | bytes 393220
  37.8 3.6 %collective-permute-start.3 = (bf16[32,40,128]{2,1,0:T(8,128)(2,1)S(1)}, bf16[32,40,128]{2,1,0:T(8,128)(2,1)S(1)}, u32[]{:S(2)}, u32[]{:S(2)}) collective-permute-start(bf16[32,40,128]{2,1,0:T(8,128)(2,1)S(1)} %slice.14), channel_id=1, source_target_pairs={{0,1},{1,0},{2,3},{3,2},{4,5},{5,4},{6,7},{7,6},{8,9},{9,8},{10,11... | collective-permute-start | bytes 983048 | tf_op jit(solution)/shard_map/ppermute | solution.py:462
  40.0 5.8 %collective-permute-start.1 = (bf16[32,16,128]{2,1,0:T(8,128)(2,1)S(1)}, bf16[32,16,128]{2,1,0:T(8,128)(2,1)S(1)}, u32[]{:S(2)}, u32[]{:S(2)}) collective-permute-start(bf16[32,16,128]{2,1,0:T(8,128)(2,1)S(1)} %get-tuple-element.29), channel_id=1, source_target_pairs={{0,16},{1,17},{2,18},{3,19},{4,20},{5,21},{6,22},{7,23},{8,24},{9,... | collective-permute-start | bytes 393224 | tf_op jit(solution)/shard_map/ppermute | solution.py:462
  40.5 0.9 %copy-start.1 = (s32[16]{0:T(128)S(1)}, s32[16]{0:T(128)}, u32[]{:S(2)}) copy-start(s32[16]{0:T(128)} %param.8) | copy-start | bytes 196
  40.5 5.3 %collective-permute-start.2 = (bf16[32,16,128]{2,1,0:T(8,128)(2,1)S(1)}, bf16[32,16,128]{2,1,0:T(8,128)(2,1)S(1)}, u32[]{:S(2)}, u32[]{:S(2)}) collective-permute-start(bf16[32,16,128]{2,1,0:T(8,128)(2,1)S(1)} %get-tuple-element.28), channel_id=1, source_target_pairs={{0,2},{1,3},{2,0},{3,1},{4,6},{5,7},{6,4},{7,5},{8,10},{9,11},{10,... | collective-permute-start | bytes 393224 | tf_op jit(solution)/shard_map/ppermute | solution.py:462
  45.8 3.1 %collective-permute-start.4 = (bf16[32,16,128]{2,1,0:T(8,128)(2,1)S(1)}, bf16[32,16,128]{2,1,0:T(8,128)(2,1)S(1)}, u32[]{:S(2)}, u32[]{:S(2)}) collective-permute-start(bf16[32,16,128]{2,1,0:T(8,128)(2,1)S(1)} %collective-permute-done.1.refs_0_), channel_id=1, source_target_pairs={{0,1},{1,0},{2,3},{3,2},{4,5},{5,4},{6,7},{7,6},{8,9},{9,8},{10,11... | collective-permute-start | bytes 393224 | tf_op jit(solution)/shard_map/ppermute | solution.py:462
  46.5 2.5 %collective-permute-start.5 = (bf16[32,16,128]{2,1,0:T(8,128)(2,1)S(1)}, bf16[32,16,128]{2,1,0:T(8,128)(2,1)S(1)}, u32[]{:S(2)}, u32[]{:S(2)}) collective-permute-start(bf16[32,16,128]{2,1,0:T(8,128)(2,1)S(1)} %collective-permute-done.2.refs_1_), channel_id=1, source_target_pairs={{0,1},{1,0},{2,3},{3,2},{4,5},{5,4},{6,7},{7,6},{8,9},{9,8},{10,11... | collective-permute-start | bytes 393224 | tf_op jit(solution)/shard_map/ppermute | solution.py:462
  52.1 18.0 %all-to-all-start.1 = ((bf16[32,48,128]{2,1,0:T(8,128)(2,1)}), bf16[32,48,128]{2,1,0:T(8,128)(2,1)S(1)}, u32[]{:S(2)}, u32[]{:S(2)}) async-start(bf16[32,48,128]{2,1,0:T(8,128)(2,1)} %get-tuple-element.19), calls=%async_computation.1 | async-start | bytes 786432 | tf_op jit(solution)/shard_map/all_to_all | solution.py:478
  55.9 2.8 %collective-permute-start.6 = (f32[8,128]{1,0:T(8,128)S(1)}, f32[8,128]{1,0:T(8,128)S(1)}, u32[]{:S(2)}, u32[]{:S(2)}) collective-permute-start(f32[8,128]{1,0:T(8,128)S(1)} %get-tuple-element.20), channel_id=1, source_target_pairs={{0,32},{32,0},{64,96},{96,64},{128,160},{160,128},{192,224},{224,1... | collective-permute-start | bytes 12296 | tf_op jit(solution)/shard_map/ppermute | solution.py:475
  58.8 4.3 %collective-permute-start.7 = (f32[8,128]{1,0:T(8,128)S(1)}, f32[8,128]{1,0:T(8,128)S(1)}, u32[]{:S(2)}, u32[]{:S(2)}) collective-permute-start(f32[8,128]{1,0:T(8,128)S(1)} %add.9), channel_id=1, source_target_pairs={{0,64},{32,96},{64,0},{96,32},{128,192},{160,224},{192,128},{224,1... | collective-permute-start | bytes 12296 | tf_op jit(solution)/shard_map/ppermute | solution.py:475
  63.0 4.3 %collective-permute-start.8 = (f32[8,128]{1,0:T(8,128)S(1)}, f32[8,128]{1,0:T(8,128)S(1)}, u32[]{:S(2)}, u32[]{:S(2)}) collective-permute-start(f32[8,128]{1,0:T(8,128)S(1)} %add.10), channel_id=1, source_target_pairs={{0,128},{32,160},{64,192},{96,224},{128,0},{160,32},{192,64},{224,... | collective-permute-start | bytes 12296 | tf_op jit(solution)/shard_map/ppermute | solution.py:475
